TPU v7x, 32 devices: a whole 2x2x4 slice. The times are simulated.
32 devices in a mesh: leaf: 8 (over z, x), sub: 4 (over y, core).
Axes of the slice: x: 2, y: 2, z: 4, core: 2. Of those that a mesh axis runs over, the one named last changes fastest.
Arguments:
- probe_rhs: float32 [32, 32768], P(None, ('leaf', 'sub')), may hold values from -22.5 to 22.5
- coords: float32 [3, 32768], P(None, ('leaf', 'sub')), may hold values from -52.7 to 52.7
- near_list: int32 [128, 5], P(('leaf', 'sub')), may hold values from -1 to 127, as said below
- far_leaf_list: int32 [128, 8], P(('leaf', 'sub')), may hold values from -1 to 127, as said below
- far_group_list: int32 [8, 14], P('leaf'), may hold values from -1 to 7, as said below
- leaf_basis: float32 [128, 64, 256], P(('leaf', 'sub')), may hold values from -0.375 to 0.375
- leaf_skeleton: float32 [3, 8192], P(None, ('leaf', 'sub')), may hold values from -52.7 to 52.7
- leaf_transfer: float32 [128, 64, 64], P(('leaf', 'sub')), may hold values from -0.375 to 0.375
- device_transfer: float32 [32, 64, 64], P(('leaf', 'sub')), may hold values from -0.375 to 0.375
- group_skeleton: float32 [3, 512], P(None, 'leaf'), may hold values from -1.5 to 4.5
Outputs:
- solution: float32 [32, 32768], P(None, ('leaf', 'sub'))
- residual: float32 [32, 32768], P(None, ('leaf', 'sub'))
Inputs may be any that keep to these rules, and one draw needn't show every extreme that they name: `near_list`: row i names distinct leaves within 2 of i, always i itself, -1 in unused slots, in any order; j is named in row i exactly when i is named in row j. `far_leaf_list`: row i names distinct leaves of the same group of 16 consecutive leaves, each more than 2 away from i, -1 in unused slots, in any order; the relation is symmetric. `far_group_list`: row g names distinct groups other than g, -1 in unused slots, in any order; the relation is symmetric.
All inputs are finite; a program needn't handle non-finite values.
Results may differ from a plain program's by a relative error of at most 0.0003.
Values sent between devices are 32-bit elements; how exact they have to be, the bound alone decides.
No kernel may reach another device: no remote copies, remote signals or barrier semaphores. Data moves between devices by JAX's collectives and lax.ppermute only.
A program may use at most 64 MiB of HBM per device.

v0:
```python
import jax
import jax.numpy as jnp
from jax import lax
from jax.sharding import PartitionSpec as P

LEAF = 256
RANK = 64
PROBES = 32
REACH = 2
ITERS = 2


NOISE = 1.0
ROOT_FIVE = 5.0**0.5
HIGHEST = lax.Precision.HIGHEST


def with_halo(block, sides, width):
    for axis, dim in sides:
        count = lax.axis_size(axis)
        forward = [(i, i + 1) for i in range(count - 1)]
        backward = [(target, source) for source, target in forward]
        low = lax.ppermute(
            lax.slice_in_dim(block, block.shape[dim] - width, None, axis=dim), axis, forward
        )
        high = lax.ppermute(lax.slice_in_dim(block, 0, width, axis=dim), axis, backward)
        block = jnp.concatenate([low, block, high], axis=dim)
    return block


def matern(left_points, right_points):
    spread = left_points[..., :, :, None] - right_points[..., :, None, :]
    scaled = ROOT_FIVE * jnp.sqrt(jnp.sum(spread * spread, axis=-3))
    return (1.0 + scaled + scaled * scaled / 3.0) * jnp.exp(-scaled)


def near_field(padded_vec, padded_pts, weights):
    local_leaves = weights.shape[0]
    window = weights.shape[1]
    padded_count = local_leaves + window - 1
    vec_blocks = padded_vec.reshape(PROBES, padded_count, LEAF)
    pts_blocks = padded_pts.reshape(3, padded_count, LEAF)
    padded_weights = jnp.pad(weights, ((REACH, REACH), (0, 0)))

    def one_position(position):
        own_points = lax.dynamic_index_in_dim(pts_blocks, position, 1, keepdims=False)
        own_values = lax.dynamic_index_in_dim(vec_blocks, position, 1, keepdims=False)
        own_weights = lax.dynamic_index_in_dim(padded_weights, position, 0, keepdims=False)
        forward = jnp.zeros((PROBES, LEAF), jnp.float32)
        backward = []
        for offset in range(REACH + 1):
            other_points = lax.dynamic_index_in_dim(
                pts_blocks, position + offset, 1, keepdims=False
            )
            kernel_tile = matern(own_points, other_points)
            other_values = lax.dynamic_index_in_dim(
                vec_blocks, position + offset, 1, keepdims=False
            )
            forward = forward + own_weights[REACH + offset] * jnp.dot(
                other_values, kernel_tile.T, precision=HIGHEST
            )
            if offset > 0:
                other_weights = lax.dynamic_index_in_dim(
                    padded_weights, position + offset, 0, keepdims=False
                )
                backward.append(
                    other_weights[REACH - offset]
                    * jnp.dot(own_values, kernel_tile, precision=HIGHEST)
                )
        return (forward, jnp.stack(backward, axis=0))

    forward_all, backward_all = lax.map(
        one_position, jnp.arange(local_leaves + REACH, dtype=jnp.int32)
    )
    totals = forward_all[REACH : REACH + local_leaves]
    for offset in range(1, REACH + 1):
        totals = totals + backward_all[REACH - offset : REACH - offset + local_leaves, offset - 1]
    return totals


def squares(residual):
    return lax.psum(jnp.sum(residual * residual, axis=1), ("leaf", "sub"))


def shards(
    probe_rhs,
    coords,
    near_list,
    far_leaf_list,
    far_group_list,
    leaf_basis,
    leaf_skeleton,
    leaf_transfer,
    device_transfer,
    group_skeleton,
):
    local_leaves = near_list.shape[0]
    window = 2 * REACH + 1
    first_leaf = lax.axis_index(("leaf", "sub")) * local_leaves
    group_first = lax.axis_index("leaf") * local_leaves * lax.axis_size("sub")
    targets = (
        first_leaf
        + jnp.arange(local_leaves, dtype=jnp.int32)[:, None, None]
        + jnp.arange(window, dtype=jnp.int32)[None, None, :]
        - REACH
    )
    near_weights = jnp.sum((near_list[:, :, None] == targets).astype(jnp.float32), axis=1)
    padded_pts = with_halo(coords, ((("leaf", "sub"), 1),), REACH * LEAF)
    group_skel = lax.all_gather(leaf_skeleton, "sub", axis=1, tiled=True).reshape(3, -1, RANK)
    own_skel = jnp.transpose(leaf_skeleton.reshape(3, local_leaves, RANK), (1, 0, 2))
    partner_local = far_leaf_list - group_first
    partner_skel = jnp.take(group_skel, jnp.maximum(partner_local, 0), axis=1)
    partner_skel = jnp.transpose(partner_skel, (1, 2, 0, 3))
    leaf_tiles = (
        matern(own_skel[:, None], partner_skel)
        * (far_leaf_list >= 0).astype(jnp.float32)[:, :, None, None]
    )
    every_group = lax.all_gather(group_skeleton, "leaf", axis=1, tiled=True).reshape(3, -1, RANK)
    group_list = far_group_list[0]
    partner_groups = jnp.transpose(
        jnp.take(every_group, jnp.maximum(group_list, 0), axis=1), (1, 0, 2)
    )
    group_tiles = (
        matern(group_skeleton[None], partner_groups)
        * (group_list >= 0).astype(jnp.float32)[:, None, None]
    )
    slots_group = group_list.shape[0]
    solution = jnp.zeros_like(probe_rhs)
    residual = probe_rhs
    direction = probe_rhs
    norm_now = squares(residual)
    for iteration in range(ITERS):
        padded_vec = with_halo(direction, ((("leaf", "sub"), 1),), REACH * LEAF)
        near_part = near_field(padded_vec, padded_pts, near_weights)
        by_leaf = direction.reshape(PROBES, local_leaves, LEAF)
        coefficients = jnp.einsum("pla,lra->lrp", by_leaf, leaf_basis, precision=HIGHEST)
        add_piece = lax.all_gather(
            coefficients.reshape(local_leaves, RANK * PROBES), "sub", axis=0, tiled=True
        )
        add_count = add_piece.shape[0]
        add_chosen = (
            partner_local[:, :, None] == jnp.arange(add_count, dtype=jnp.int32)[None, None, :]
        ).astype(jnp.float32)
        picked = jnp.einsum("lkm,mx->lkx", add_chosen, add_piece, precision=HIGHEST).reshape(
            local_leaves, -1, RANK, PROBES
        )
        leaf_far = jnp.zeros((local_leaves, RANK, PROBES), jnp.float32) + jnp.einsum(
            "lkrs,lksp->lrp", leaf_tiles, picked, precision=HIGHEST
        )
        device_coef = jnp.einsum("lrs,lrp->sp", leaf_transfer, coefficients, precision=HIGHEST)
        group_term = jnp.dot(device_transfer[0].T, device_coef, precision=HIGHEST).T
        summed = lax.psum(group_term.reshape(1, PROBES * RANK), "sub")
        piece = lax.all_gather(summed, "leaf", axis=0, tiled=True)
        count = piece.shape[0]
        chosen = (group_list[:, None] == jnp.arange(count, dtype=jnp.int32)[None, :]).astype(
            jnp.float32
        )
        apply_picked = jnp.zeros((slots_group, PROBES * RANK), jnp.float32) + jnp.dot(
            chosen, piece, precision=HIGHEST
        )
        group_far = jnp.einsum(
            "krs,kps->rp",
            group_tiles,
            apply_picked.reshape(slots_group, PROBES, RANK),
            precision=HIGHEST,
        )
        device_far = jnp.dot(device_transfer[0], group_far, precision=HIGHEST)
        leaf_total = leaf_far + jnp.einsum(
            "lrs,sp->lrp", leaf_transfer, device_far, precision=HIGHEST
        )
        far_part = jnp.einsum("lra,lrp->pla", leaf_basis, leaf_total, precision=HIGHEST)
        near_flat = jnp.transpose(near_part, (1, 0, 2)).reshape(PROBES, -1)
        image_vec = NOISE * direction + near_flat + far_part.reshape(PROBES, -1)
        curvature = lax.psum(jnp.sum(direction * image_vec, axis=1), ("leaf", "sub"))
        step_length = norm_now / curvature
        solution = solution + step_length[:, None] * direction
        residual = residual - step_length[:, None] * image_vec
        if iteration + 1 < ITERS:
            norm_next = squares(residual)
            direction = residual + (norm_next / norm_now)[:, None] * direction
            norm_now = norm_next
    return (solution, residual)


def solution(mesh):
    return jax.shard_map(
        shards,
        mesh=mesh,
        in_specs=(
            P(None, ("leaf", "sub")),
            P(None, ("leaf", "sub")),
            P(("leaf", "sub"), None),
            P(("leaf", "sub"), None),
            P("leaf", None),
            P(("leaf", "sub"), None, None),
            P(None, ("leaf", "sub")),
            P(("leaf", "sub"), None, None),
            P(("leaf", "sub"), None, None),
            P(None, "leaf"),
        ),
        out_specs=(P(None, ("leaf", "sub")), P(None, ("leaf", "sub"))),
        check_vma=False,
    )
```

profile of v0, /device:TPU:0, one launch (start us, length us, event | category | flops | bytes accessed | tf_op | source)
XLA Modules:
  0.0 420.2 jit_solution(17418005044914235301)
XLA Ops:
  1.4 2.4 collective-permute-start.2
  3.8 1.3 collective-permute-start.3
  6.0 5.2 %collective-permute-start = (f32[32,512]{1,0:T(8,128)S(1)}, f32[32,512]{1,0:T(8,128)S(1)}, u32[]{:S(2)}, u32[]{:S(2)}) collective-permute-start(f32[32,512]{1,0:T(8,128)S(1)} %get-tuple-element.258), channel_id=1, source_target_pairs={{0,1},{1,2},{2,3},{3,4},{4,5},{5,6},{6,7},{7,8},{8,9},{9,10},{10,1... | collective-permute-start | bytes 196616 | tf_op jit(solution)/shard_map/ppermute | solution.py:23
  11.2 1.3 collective-permute-start.1
  14.6 8.0 %all_gather.18 = f32[3,1024]{1,0:T(4,128)S(1)} all-gather(f32[3,256]{1,0:T(4,128)} %param.20), channel_id=1, replica_groups=mesh['leaf'=8,'sub'=4] {'sub'}, dimensions={1}, use_global_device_ids=true | all-gather | bytes 15360 | tf_op jit(solution)/shard_map/all_gather | solution.py:109
  24.2 30.0 %all-gather.1 = f32[8,64,3]{1,2,0:T(4,128)S(1)} all-gather(f32[1,64,3]{1,2,0:T(4,128)} %bitcast.297), channel_id=1, replica_groups=mesh['leaf'=8,'sub'=4] {'leaf'}, dimensions={0}, use_global_device_ids=true | all-gather | bytes 6912 | tf_op jit(solution)/shard_map/all_gather | solution.py:118
  54.5 1.3 fusion.92
  56.4 5.9 %psum.43 = f32[1,2048]{1,0:T(1,128)S(1)} all-reduce(f32[1,2048]{1,0:T(1,128)S(1)} %reshape.167), channel_id=1, replica_groups=mesh['leaf'=8,'sub'=4] {'sub'}, use_global_device_ids=true, to_apply=%region_10.11 | all-reduce | flops 2048 | bytes 16384 | tf_op jit(solution)/shard_map/psum | solution.py:152
  62.2 30.5 %all-gather.2 = f32[8,1,2048]{2,1,0:T(1,128)S(1)} all-gather(f32[1,1,2048]{2,1,0:T(1,128)S(1)} %bitcast.291), channel_id=1, replica_groups=mesh['leaf'=8,'sub'=4] {'leaf'}, dimensions={0}, use_global_device_ids=true | all-gather | bytes 73728 | tf_op jit(solution)/shard_map/all_gather | solution.py:153
  92.9 5.4 %all-gather = f32[4,4,2048]{2,1,0:T(4,128)S(1)} all-gather(f32[1,4,2048]{2,1,0:T(4,128)S(1)} %reshape.197), channel_id=1, replica_groups=mesh['leaf'=8,'sub'=4] {'sub'}, dimensions={0}, use_global_device_ids=true | all-gather | bytes 163840 | tf_op jit(solution)/shard_map/all_gather | solution.py:137
  102.5 2.2 convolution_bitcast_fusion.5
  105.9 71.2 %while.28 = (s32[]{:T(128)}, f32[6,32,256]{2,1,0:T(8,128)S(1)}, f32[6,2,32,256]{3,2,1,0:T(8,128)S(1)}, s32[6]{0:T(128)S(1)}, f32[8,5]{1,0:T(8,128)S(1)}, /*index...) while((s32[]{:T(128)}, f32[6,32,256]{2,1,0:T(8,128)S(1)}, ...), condition=%wide.region_7.8_spmd, body=%wide.region_3.0_spmd.sunk | while | flops 129769488 | bytes 2846183 | solution.py:72
  116.6 1.1 fusion.194
  128.4 1.1 fusion.194
  140.3 1.1 fusion.194
  152.1 1.1 fusion.194
  164.0 1.1 fusion.194
  175.9 1.1 fusion.194
  177.2 36.8 %all-reduce.1 = (f32[32]{0:T(128)S(1)}, f32[32]{0:T(128)S(1)}) all-reduce(f32[32]{0:T(128)S(1)} %get-tuple-element.195, f32[32]{0:T(128)S(1)} %get-tuple-element.194), channel_id=1, replica_groups=mesh['leaf'=8,'sub'=4] {'leaf','sub'}, use_global_device_ids=true, to_apply=%region_1.2 | all-reduce | flops 64 | bytes 512 | tf_op jit(solution)/shard_map/psum | solution.py:82
  214.3 41.2 %psum.45 = f32[32]{0:T(128)S(1)} all-reduce(f32[32]{0:T(128)S(1)} %get-tuple-element.226), channel_id=1, replica_groups=mesh['leaf'=8,'sub'=4] {'leaf','sub'}, use_global_device_ids=true, to_apply=%region_14.15 | all-reduce | flops 32 | bytes 256 | tf_op jit(solution)/shard_map/psum | solution.py:82
  257.1 6.9 %psum.46 = f32[1,2048]{1,0:T(1,128)S(1)} all-reduce(f32[1,2048]{1,0:T(1,128)S(1)} %reshape.175), channel_id=1, replica_groups=mesh['leaf'=8,'sub'=4] {'sub'}, use_global_device_ids=true, to_apply=%region_20.21 | all-reduce | flops 2048 | bytes 16384 | tf_op jit(solution)/shard_map/psum | solution.py:152
  264.0 30.6 %all-gather.4 = f32[8,1,2048]{2,1,0:T(1,128)S(1)} all-gather(f32[1,1,2048]{2,1,0:T(1,128)S(1)} %bitcast.292), channel_id=1, replica_groups=mesh['leaf'=8,'sub'=4] {'leaf'}, dimensions={0}, use_global_device_ids=true | all-gather | bytes 73728 | tf_op jit(solution)/shard_map/all_gather | solution.py:153
  294.9 5.6 %all-gather.3 = f32[4,4,2048]{2,1,0:T(4,128)S(1)} all-gather(f32[1,4,2048]{2,1,0:T(4,128)S(1)} %reshape.203), channel_id=1, replica_groups=mesh['leaf'=8,'sub'=4] {'sub'}, dimensions={0}, use_global_device_ids=true | all-gather | bytes 163840 | tf_op jit(solution)/shard_map/all_gather | solution.py:137
  301.9 2.9 collective-permute-start.4
  304.8 1.3 collective-permute-start.5
  306.4 2.2 convolution_bitcast_fusion.3
  310.5 69.0 %while.29 = (s32[]{:T(128)}, f32[6,32,256]{2,1,0:T(8,128)S(1)}, f32[6,2,32,256]{3,2,1,0:T(8,128)S(1)}, s32[6]{0:T(128)S(1)}, f32[8,5]{1,0:T(8,128)S(1)}, /*index...) while((s32[]{:T(128)}, f32[6,32,256]{2,1,0:T(8,128)S(1)}, ...), condition=%wide.region_19.20_spmd, body=%wide.region_15.19_spmd.sunk | while | flops 129769488 | bytes 2846183 | solution.py:72
  320.8 1.1 fusion.206
  332.4 1.1 fusion.206
  343.9 1.1 fusion.206
  366.9 1.1 fusion.206
  379.7 39.7 %psum.47 = f32[32]{0:T(128)S(1)} all-reduce(f32[32]{0:T(128)S(1)} %multiply_reduce_fusion.8), channel_id=1, replica_groups=mesh['leaf'=8,'sub'=4] {'leaf','sub'}, use_global_device_ids=true, to_apply=%region_22.23 | all-reduce | flops 32 | bytes 256 | tf_op jit(solution)/shard_map/psum | solution.py:174
  (253 shorter events, 90.8 us)
Async XLA Ops:
  0.6 53.9 %copy-start = (f32[4,64,256]{2,1,0:T(8,128)S(1)}, f32[4,64,256]{2,1,0:T(8,128)}, u32[]{:S(2)}) copy-start(f32[4,64,256]{2,1,0:T(8,128)} %param.19) | copy-start | bytes 786436
  0.6 55.2 %copy-start.2 = (f32[4,64,64]{2,1,0:T(8,128)S(1)}, f32[4,64,64]{2,1,0:T(8,128)}, u32[]{:S(2)}) copy-start(f32[4,64,64]{2,1,0:T(8,128)} %param.21) | copy-start | bytes 196612
  0.7 55.5 %copy-start.3 = (f32[1,64,64]{2,1,0:T(8,128)S(1)}, f32[1,64,64]{2,1,0:T(8,128)}, u32[]{:S(2)}) copy-start(f32[1,64,64]{2,1,0:T(8,128)} %param.22) | copy-start | bytes 49156
  1.4 104.2 %collective-permute-start.2 = (f32[3,512]{1,0:T(4,128)S(1)}, f32[3,512]{1,0:T(4,128)S(1)}, u32[]{:S(2)}, u32[]{:S(2)}) collective-permute-start(f32[3,512]{1,0:T(4,128)S(1)} %get-tuple-element.260), channel_id=1, source_target_pairs={{0,1},{1,2},{2,3},{3,4},{4,5},{5,6},{6,7},{7,8},{8,9},{9,10},{10,1... | collective-permute-start | bytes 18440 | tf_op jit(solution)/shard_map/ppermute | solution.py:23
  3.8 101.8 %collective-permute-start.3 = (f32[3,512]{1,0:T(4,128)S(1)}, f32[3,512]{1,0:T(4,128)S(1)}, u32[]{:S(2)}, u32[]{:S(2)}) collective-permute-start(f32[3,512]{1,0:T(4,128)S(1)} %get-tuple-element.261), channel_id=1, source_target_pairs={{1,0},{2,1},{3,2},{4,3},{5,4},{6,5},{7,6},{8,7},{9,8},{10,9},{11,1... | collective-permute-start | bytes 18440 | tf_op jit(solution)/shard_map/ppermute | solution.py:26
  6.0 92.3 %copy-start.8 = (s32[1,14]{1,0:T(1,128)S(1)}, s32[1,14]{1,0:T(1,128)}, u32[]{:S(2)}) copy-start(s32[1,14]{1,0:T(1,128)} %param.18) | copy-start | bytes 172
  6.0 99.6 %collective-permute-start = (f32[32,512]{1,0:T(8,128)S(1)}, f32[32,512]{1,0:T(8,128)S(1)}, u32[]{:S(2)}, u32[]{:S(2)}) collective-permute-start(f32[32,512]{1,0:T(8,128)S(1)} %get-tuple-element.258), channel_id=1, source_target_pairs={{0,1},{1,2},{2,3},{3,4},{4,5},{5,6},{6,7},{7,8},{8,9},{9,10},{10,1... | collective-permute-start | bytes 196616 | tf_op jit(solution)/shard_map/ppermute | solution.py:23
  11.2 94.5 %collective-permute-start.1 = (f32[32,512]{1,0:T(8,128)S(1)}, f32[32,512]{1,0:T(8,128)S(1)}, u32[]{:S(2)}, u32[]{:S(2)}) collective-permute-start(f32[32,512]{1,0:T(8,128)S(1)} %get-tuple-element.259), channel_id=1, source_target_pairs={{1,0},{2,1},{3,2},{4,3},{5,4},{6,5},{7,6},{8,7},{9,8},{10,9},{11,1... | collective-permute-start | bytes 196616 | tf_op jit(solution)/shard_map/ppermute | solution.py:26
  55.9 43.8 %copy-start.7 = (f32[3,64]{1,0:T(4,128)S(1)}, f32[3,64]{1,0:T(4,128)}, u32[]{:S(2)}) copy-start(f32[3,64]{1,0:T(4,128)} %param.23) | copy-start | bytes 2308
  100.0 0.8 copy-start.4
  102.5 3.1 copy-start.6
  104.7 0.9 copy-start.1
  255.9 44.8 %copy-start.5 = (f32[14,64,64]{2,1,0:T(8,128)S(1)}, f32[14,64,64]{2,1,0:T(8,128)}, u32[]{:S(2)}) copy-start(f32[14,64,64]{2,1,0:T(8,128)} %copy-done.4) | copy-start | bytes 688132
  301.9 7.5 %collective-permute-start.4 = (f32[32,512]{1,0:T(8,128)}, f32[32,512]{1,0:T(8,128)}, u32[]{:S(2)}, u32[]{:S(2)}) collective-permute-start(f32[32,512]{1,0:T(8,128)} %get-tuple-element.256), channel_id=1, source_target_pairs={{0,1},{1,2},{2,3},{3,4},{4,5},{5,6},{6,7},{7,8},{8,9},{9,10},{10,1... | collective-permute-start | bytes 196616 | tf_op jit(solution)/shard_map/ppermute | solution.py:23
  304.8 4.6 %collective-permute-start.5 = (f32[32,512]{1,0:T(8,128)S(1)}, f32[32,512]{1,0:T(8,128)}, u32[]{:S(2)}, u32[]{:S(2)}) collective-permute-start(f32[32,512]{1,0:T(8,128)S(1)} %get-tuple-element.257), channel_id=1, source_target_pairs={{1,0},{2,1},{3,2},{4,3},{5,4},{6,5},{7,6},{8,7},{9,8},{10,9},{11,1... | collective-permute-start | bytes 196616 | tf_op jit(solution)/shard_map/ppermute | solution.py:26
where the time goes:
time: 423 us; the launch traced here: 420 us
  blocking collectives  240 us (57%)
  matrix products  67.4 us (16%)
  loops' own time  56.5 us (13%)
  local copies, waits for them, and re-layouts  31.3 us (7%)
  starting transfers between devices  14.3 us (3%)
  other arithmetic  8.95 us (2%)
    psum x2, blocking collectives, squares(): return lax.psum(jnp.sum(residual * residual, axis=1), ('leaf', 'sub'))  78 us
    all_gather x2, blocking collectives, shards(): piece = lax.all_gather(summed, 'leaf', axis=0, tiled=True)  61.1 us
    another operation x2, loops' own time, near_field(): lax.map(one_position, jnp.arange(local_leaves + REACH, dtype=jnp.int32))  56.5 us
    psum x1, blocking collectives, shards(): lax.psum(jnp.sum(direction * image_vec, axis=1), ('leaf', 'sub'))  39.7 us
    dot_general x36, matrix products, one_position(): jnp.dot(other_values, kernel_tile.T, precision=HIGHEST)  38.7 us
    all_gather x1, blocking collectives, shards(): lax.all_gather(group_skeleton, 'leaf', axis=1, tiled=True)  30 us
    dot_general x24, matrix products, one_position(): jnp.dot(own_values, kernel_tile, precision=HIGHEST)  17.5 us
    psum x2, blocking collectives, shards(): summed = lax.psum(group_term.reshape(1, PROBES * RANK), 'sub')  12.7 us
  transfers between devices with their start and end apart: 6, of which 0 were waited for; matrix products, arithmetic and copies ran while one was open for 4% of the time, Pallas kernels for 0%

commit v1 on v0

v1 whole, which is shorter than its diff:
```python
import jax
import jax.numpy as jnp
from jax import lax
from jax.experimental import pallas as pl
from jax.experimental.pallas import tpu as pltpu
from jax.sharding import PartitionSpec as P

REACH = 2
NOISE = 1.0
ROOT_FIVE = 5.0**0.5
LOG2_E = 1.4426950408889634
HIGHEST = lax.Precision.HIGHEST
F32 = jnp.float32
BF16 = jnp.bfloat16
DOWN = 2.0**-40
UP = 2.0**20
LANE = 128
EXTRA = 8


def dot(a, b, ca=1, cb=0):
    return lax.dot_general(
        a, b, (((ca,), (cb,)), ((), ())), precision=HIGHEST, preferred_element_type=F32
    )


def dot16(a, b):
    return lax.dot_general(a, b, (((1,), (0,)), ((), ())), preferred_element_type=F32)


def split(x):
    high = x.astype(BF16)
    return high, (x - high.astype(F32)).astype(BF16)


def matern(rows, cols):
    total = None
    for axis in range(3):
        spread = rows[:, axis : axis + 1] - cols[axis : axis + 1, :]
        total = spread * spread if total is None else total + spread * spread
    distance = total * lax.rsqrt(jnp.maximum(total, 1e-35))
    poly = (1.0 + ROOT_FIVE * distance) + (5.0 / 3.0) * total
    return poly * jnp.exp2((-ROOT_FIVE * LOG2_E) * distance)


def named(list_ref, row, index):
    hit = list_ref[row, 0] == index
    for column in range(1, list_ref.shape[1]):
        hit = jnp.logical_or(hit, list_ref[row, column] == index)
    return jnp.where(hit, 1.0, 0.0).astype(F32)


def leaf_coefficients(vec, basis_ref):
    leaves, rank, leaf = basis_ref.shape
    pieces = [
        dot(vec[:, i * leaf : (i + 1) * leaf], basis_ref[i], 1, 1) for i in range(leaves)
    ]
    return jnp.concatenate(pieces, axis=1)


def write_messages(vec, coefs, term, outs, width, rows):
    m1, m2, m3, m4 = outs
    half = REACH * width
    count = vec.shape[1]
    even = lax.axis_index("sub") % 2 == 0
    low = vec[:, :half]
    high = vec[:, count - half :]
    part_a = jnp.where(even, high, low)
    part_b = jnp.where(even, low, high)
    span = coefs.shape[1]
    base = m2.shape[1]
    for ref in (m1, m2, m3):
        ref[rows, 0:span] = coefs
        ref[rows, span:base] = term
    m1[rows, base : base + half] = part_a
    m3[rows, base : base + half] = part_b
    m4[rows, :] = part_b


def padded_lanes(x, lanes):
    return jnp.concatenate(
        [x, jnp.zeros((x.shape[0], lanes - x.shape[1]), x.dtype)], axis=1
    )


def padded_rows(x, rows):
    return jnp.concatenate(
        [x, jnp.zeros((rows - x.shape[0], x.shape[1]), x.dtype)], axis=0
    )


def first_kernel(vec_ref, coords_ref, skel_ref, gskel_ref, basis_ref, transfer_ref, device_ref, *outs):
    leaf = basis_ref.shape[2]
    probes = vec_ref.shape[0]
    vec = vec_ref[...]
    coefs = leaf_coefficients(vec, basis_ref)
    term = dot(dot(coefs, transfer_ref[...]), device_ref[...])
    term = padded_lanes(term, outs[1].shape[1] - coefs.shape[1])
    write_messages(vec, coefs, term, outs, leaf, slice(0, probes))
    coords = padded_rows(coords_ref[...], EXTRA)
    skel = padded_rows(skel_ref[...], EXTRA)
    gskel = padded_rows(padded_lanes(gskel_ref[...], term.shape[1]), EXTRA)
    write_messages(coords, skel, gskel, outs, leaf, slice(probes, probes + EXTRA))


def halos(r1, r3, r4, rows, base):
    sub = lax.axis_index("sub")
    count = lax.axis_size("sub")
    inner = jnp.logical_and(sub > 0, sub < count - 1)
    from_a = r1[rows, base:]
    from_b = jnp.where(inner, r3[rows, base:], r4[rows, :])
    odd = sub % 2 == 1
    return jnp.where(odd, from_a, from_b), jnp.where(odd, from_b, from_a)


def near_product(vec, low, high, stack_ref, th_ref, tl_ref, leaf, leaves, out_ref):
    probes = vec.shape[0]
    half = REACH * leaf
    count = vec.shape[1]
    for start, block in ((0, low), (half, vec), (half + count, high)):
        top, rest = split(block)
        stack_ref[0:probes, start : start + block.shape[1]] = top
        stack_ref[probes:, start : start + block.shape[1]] = rest
    window = (2 * REACH + 1) * leaf
    for i in range(leaves):
        both = dot16(stack_ref[:, i * leaf : i * leaf + window], th_ref[i])
        more = dot16(stack_ref[0:probes, i * leaf : i * leaf + window], tl_ref[i])
        out_ref[:, i * leaf : (i + 1) * leaf] = (
            NOISE * vec[:, i * leaf : (i + 1) * leaf]
            + (both[0:probes] + both[probes:])
            + more
        )


def far_product(blocks, klh_ref, kll_ref):
    everything = jnp.concatenate(blocks, axis=1)
    high, low = split(everything)
    both = dot16(jnp.concatenate([high, low], axis=0), klh_ref[...])
    probes = everything.shape[0]
    return both[0:probes] + both[probes:] + dot16(high, kll_ref[...])


def tiles_kernel(
    near_ref, far_ref, vec_ref, coords_ref, own, r1, r2, r3, r4,
    th_ref, tl_ref, klh_ref, kll_ref, part_ref, lf_ref,
    points_ref, columns_ref, stack_ref,
):
    leaves = near_ref.shape[0]
    probes, count = vec_ref.shape
    leaf = count // leaves
    half = REACH * leaf
    base = own.shape[1]
    span = klh_ref.shape[1]
    rank = span // leaves
    sub = lax.axis_index("sub")
    subs = lax.axis_size("sub")
    group_first = lax.axis_index("leaf") * subs * leaves
    first = group_first + sub * leaves
    extra = slice(probes, probes + EXTRA)
    low, high = halos(r1, r3, r4, extra, base)
    points_ref[:, 0:half] = low
    points_ref[:, half : half + count] = padded_rows(coords_ref[...], EXTRA)
    points_ref[:, half + count :] = high
    columns_ref[...] = points_ref[...].T
    chunk = 64
    parts = leaf // chunk
    for i in range(leaves):
        cols = points_ref[:, half + i * leaf : half + (i + 1) * leaf]
        for k in range(2 * REACH + 1):
            weight = named(near_ref, i, first + i + k - REACH)

            def body(step, _, i=i, k=k, weight=weight, cols=cols):
                row = pl.multiple_of(k * leaf + step * chunk, chunk)
                source = pl.multiple_of((i + k) * leaf + step * chunk, chunk)
                tile = weight * matern(columns_ref[pl.ds(source, chunk), :], cols)
                top, rest = split(tile)
                th_ref[i, pl.ds(row, chunk), :] = top
                tl_ref[i, pl.ds(row, chunk), :] = rest
                return 0

            lax.fori_loop(0, parts, body, 0)
    messages = (own, r1, r2, r3)
    own_skel = own[extra, 0:span]
    lane_leaf = lax.broadcasted_iota(jnp.int32, (1, span), 1) // rank
    for m, message in enumerate(messages):
        skel = message[extra, 0:span].T
        for j in range(leaves):
            index = group_first + (sub ^ m) * leaves + j
            mask = jnp.zeros((1, span), F32)
            for i in range(leaves):
                mask = jnp.where(lane_leaf == i, named(far_ref, i, index), mask)
            tile = mask * matern(skel[j * rank : (j + 1) * rank], own_skel)
            top, rest = split(tile)
            row = m * span + j * rank
            klh_ref[row : row + rank, :] = top
            kll_ref[row : row + rank, :] = rest
    rows = slice(0, probes)
    vec = vec_ref[...]
    low, high = halos(r1, r3, r4, rows, base)
    near_product(vec, low, high, stack_ref, th_ref, tl_ref, leaf, leaves, part_ref)
    lf_ref[...] = far_product([r[rows, 0:span] for r in messages], klh_ref, kll_ref)


def local_kernel(
    vec_ref, own, r1, r2, r3, r4, th_ref, tl_ref, klh_ref, kll_ref,
    part_ref, lf_ref, stack_ref,
):
    leaves = th_ref.shape[0]
    probes, count = vec_ref.shape
    leaf = count // leaves
    base = own.shape[1]
    span = klh_ref.shape[1]
    rows = slice(0, probes)
    vec = vec_ref[...]
    low, high = halos(r1, r3, r4, rows, base)
    near_product(vec, low, high, stack_ref, th_ref, tl_ref, leaf, leaves, part_ref)
    lf_ref[...] = far_product([r[rows, 0:span] for r in (own, r1, r2, r3)], klh_ref, kll_ref)


def finish_image(part_ref, lf_ref, group_ref, kg_ref, basis_ref, transfer_ref, device_ref):
    leaves, rank, leaf = basis_ref.shape
    groups = group_ref.shape[0]
    probes = part_ref.shape[0]

    def one(m, total):
        return total + dot(group_ref[m, 0:probes, 0:rank], kg_ref[m], 1, 1)

    group_far = lax.fori_loop(
        0, groups, one, jnp.zeros((probes, rank), F32), unroll=groups <= 16
    )
    device_far = dot(group_far, device_ref[...], 1, 1)
    total = lf_ref[...] + dot(device_far, transfer_ref[...], 1, 1)
    pieces = [
        part_ref[:, i * leaf : (i + 1) * leaf]
        + dot(total[:, i * rank : (i + 1) * rank], basis_ref[i])
        for i in range(leaves)
    ]
    return jnp.concatenate(pieces, axis=1)


def middle_kernel(
    list_ref, part_ref, lf_ref, group_ref, gskel_ref, basis_ref, transfer_ref, device_ref,
    image_ref, kg_ref, *outs,
):
    leaves, rank, leaf = basis_ref.shape
    groups = group_ref.shape[0]
    probes = part_ref.shape[0]
    mine = lax.axis_index("leaf")
    own = padded_rows(padded_lanes(gskel_ref[...], LANE), EXTRA).T[0:rank]

    def one(m, _):
        weight = named(list_ref, 0, mine ^ m)
        other = group_ref[m, probes : probes + EXTRA, 0:rank]
        kg_ref[m] = weight * matern(own, other)
        return 0

    lax.fori_loop(0, groups, one, 0, unroll=groups <= 16)
    image = finish_image(part_ref, lf_ref, group_ref, kg_ref, basis_ref, transfer_ref, device_ref)
    image_ref[...] = image
    coefs = leaf_coefficients(image, basis_ref)
    term = dot(dot(coefs, transfer_ref[...]), device_ref[...])
    term = padded_lanes(term, outs[1].shape[1] - coefs.shape[1])
    write_messages(image, coefs, term, outs, leaf, slice(0, probes))


def last_kernel(
    vec_ref, first_ref, part_ref, lf_ref, group_ref, kg_ref, basis_ref, transfer_ref, device_ref,
    second_ref, sums_ref,
):
    probes, count = vec_ref.shape
    second = finish_image(part_ref, lf_ref, group_ref, kg_ref, basis_ref, transfer_ref, device_ref)
    second_ref[...] = second
    vec = vec_ref[...]
    first = first_ref[...]
    ones = jnp.ones((8, count), F32)
    row = lax.broadcasted_iota(jnp.int32, (8, probes), 0)
    products = (vec * vec, vec * first, first * first, (DOWN * first) * second)
    sums = jnp.zeros((8, probes), F32)
    for k, product in enumerate(products):
        sums = jnp.where(row == k, dot(ones, product, 1, 1), sums)
    for k in range(sums_ref.shape[0] // 8):
        sums_ref[8 * k : 8 * k + 8, :] = sums


def update_kernel(sums_ref, vec_ref, first_ref, second_ref, solution_ref, residual_ref):
    gathered = sums_ref[...]
    rows = gathered.shape[0]
    pick = (
        lax.broadcasted_iota(jnp.int32, (rows, LANE), 0) % 8
        == lax.broadcasted_iota(jnp.int32, (rows, LANE), 1)
    ).astype(F32)
    scalars = dot(gathered, pick, 0, 0)
    bb = scalars[:, 0:1]
    bw = scalars[:, 1:2]
    ww = scalars[:, 2:3]
    wv = scalars[:, 3:4]
    step = bb / bw
    rise = (step * ww) * step
    norm = rise - bb
    grow = rise / bb
    scaled = step * UP
    curvature = (grow * grow) * bw - (2.0 * grow) * (step * ww) + (scaled * wv) * scaled
    again = norm / curvature
    vec = vec_ref[...]
    first = first_ref[...]
    second = second_ref[...]
    direction = grow * vec - step * first
    solution_ref[...] = step * vec + again * direction
    residual_ref[...] = (vec - step * first) - again * (grow * first - step * second)


def vmem(count):
    return [pl.BlockSpec(memory_space=pltpu.VMEM)] * count


def smem(count):
    return [pl.BlockSpec(memory_space=pltpu.SMEM)] * count


def shape(*dims, dtype=F32):
    return jax.ShapeDtypeStruct(dims, dtype)


def call(kernel, outs, args, scalars=0, scratch=(), name=None, flops=0):
    return pl.pallas_call(
        kernel,
        out_shape=tuple(outs),
        in_specs=smem(scalars) + vmem(len(args) - scalars),
        out_specs=tuple(vmem(len(outs))),
        scratch_shapes=list(scratch),
        name=name,
        cost_estimate=pl.CostEstimate(flops=flops, transcendentals=0, bytes_accessed=1000000),
    )(*args)


def message_shapes(rows, base, half):
    return [
        shape(rows, base + half),
        shape(rows, base),
        shape(rows, base + half),
        shape(rows, half),
    ]


def exchange(m1, m2, m3, m4):
    subs = lax.axis_size("sub")
    nodes = subs * lax.axis_size("leaf")

    def swap(x, m):
        return lax.ppermute(x, "sub", [(i, i ^ m) for i in range(subs)])

    across = [(q, q + 1) for q in range(subs - 1, nodes - 1, subs)]
    across = across + [(target, source) for source, target in across]
    return swap(m1, 1), swap(m2, 2), swap(m3, 3), lax.ppermute(m4, ("leaf", "sub"), across)


def group_gather(own, r1, r2, r3, span, base):
    groups = lax.axis_size("leaf")
    held = sum(x[:, span:base] for x in (r1, r2, r3)) + own[:, span:base]
    return spread_groups(held[None], groups)


def spread_groups(held, groups):
    bit = 1
    while bit < groups:
        came = lax.ppermute(held, "leaf", [(i, i ^ bit) for i in range(groups)])
        held = jnp.concatenate([held, came], axis=0)
        bit = 2 * bit
    return held


def shards(
    probe_rhs,
    coords,
    near_list,
    far_leaf_list,
    far_group_list,
    leaf_basis,
    leaf_skeleton,
    leaf_transfer,
    device_transfer,
    group_skeleton,
):
    leaves, rank, leaf = leaf_basis.shape
    probes, count = probe_rhs.shape
    groups = lax.axis_size("leaf")
    nodes = groups * lax.axis_size("sub")
    half = REACH * leaf
    span = leaves * rank
    base = span + LANE
    window = (2 * REACH + 1) * leaf
    transfer = leaf_transfer.reshape(span, rank)
    device = device_transfer[0]
    sent = call(
        first_kernel,
        message_shapes(probes + EXTRA, base, half),
        (probe_rhs, coords, leaf_skeleton, group_skeleton, leaf_basis, transfer, device),
        name="coefficients",
    )
    came = exchange(*sent)
    own = sent[1]
    term = own[:probes, span:base] + sum(x[:probes, span:base] for x in came[:3])
    held = jnp.concatenate([term, own[probes:, span:base]], axis=0)
    gathered = spread_groups(held[None], groups)
    th, tl, klh, kll, part, lf = call(
        tiles_kernel,
        [
            shape(leaves, window, leaf, dtype=BF16),
            shape(leaves, window, leaf, dtype=BF16),
            shape(lax.axis_size("sub") * span, span, dtype=BF16),
            shape(lax.axis_size("sub") * span, span, dtype=BF16),
            shape(probes, count),
            shape(probes, span),
        ],
        (near_list, far_leaf_list, probe_rhs, coords, own, *came),
        scalars=2,
        scratch=[
            pltpu.VMEM((EXTRA, count + 2 * half), F32),
            pltpu.VMEM((count + 2 * half, EXTRA), F32),
            pltpu.VMEM((2 * probes, count + 2 * half), BF16),
        ],
        name="tiles",
    )
    image, kg, *sent = call(
        middle_kernel,
        [shape(probes, count), shape(groups, rank, rank)]
        + message_shapes(probes, base, half),
        (far_group_list, part, lf, gathered, group_skeleton, leaf_basis, transfer, device),
        scalars=1,
        name="middle",
    )
    came = exchange(*sent)
    own = sent[1]
    gathered = group_gather(own, came[0], came[1], came[2], span, base)
    part, lf = call(
        local_kernel,
        [shape(probes, count), shape(probes, span)],
        (image, own, *came, th, tl, klh, kll),
        scratch=[pltpu.VMEM((2 * probes, count + 2 * half), BF16)],
        name="local",
    )
    second, sums = call(
        last_kernel,
        [shape(probes, count), shape(8 * nodes, probes)],
        (probe_rhs, image, part, lf, gathered, kg, leaf_basis, transfer, device),
        name="last",
    )
    sums = lax.all_to_all(sums, ("leaf", "sub"), 0, 0, tiled=True)
    return call(
        update_kernel,
        [shape(probes, count), shape(probes, count)],
        (sums, probe_rhs, image, second),
        name="update",
    )


def solution(mesh):
    return jax.shard_map(
        shards,
        mesh=mesh,
        in_specs=(
            P(None, ("leaf", "sub")),
            P(None, ("leaf", "sub")),
            P(("leaf", "sub"), None),
            P(("leaf", "sub"), None),
            P("leaf", None),
            P(("leaf", "sub"), None, None),
            P(None, ("leaf", "sub")),
            P(("leaf", "sub"), None, None),
            P(("leaf", "sub"), None, None),
            P(None, "leaf"),
        ),
        out_specs=(P(None, ("leaf", "sub")), P(None, ("leaf", "sub"))),
        check_vma=False,
    )
```

time: 423 us -> 95.4 us (0.23)
  blocking collectives: 240 us -> 13 us
  matrix products: 67.4 us -> 0 us
  loops' own time: 56.5 us -> 0 us
  Pallas kernels: 0 us -> 34.8 us
  local copies, waits for them, and re-layouts: 31.3 us -> 4.24 us
  waiting for transfers between devices: 0.02 us -> 16.8 us
  starting transfers between devices: 14.3 us -> 21.8 us
  other arithmetic: 8.95 us -> 3.62 us
    psum x5 -> x0, blocking collectives: 130 us -> none  [the longest x2 78 us: squares(): return lax.psum(jnp.sum(residual * residual, axis=1), ('leaf', 'sub'))]
    all_gather x6 -> x0, blocking collectives: 110 us -> none  [the longest x2 61.1 us: shards(): piece = lax.all_gather(summed, 'leaf', axis=0, tiled=True)]
    dot_general x80 -> x0, matrix products: 67.4 us -> none  [the longest x36 38.7 us: one_position(): jnp.dot(other_values, kernel_tile.T, precision=HIGHEST)]
    another operation x2 -> x0, loops' own time: 56.5 us -> none  [near_field(): lax.map(one_position, jnp.arange(local_leaves + REACH, dtype=jnp.int32))]
    pallas_call x0 -> x6, Pallas kernels: none -> 34.8 us  [call(): pl.pallas_call(kernel, out_shape=tuple(outs), in_specs=smem(scalars) + vm...]
    slice x27 -> x1, local copies, waits for them, and re-layouts: 17.8 us -> 0.72 us  [shards(): held = jnp.concatenate([term, own[probes:, span:base]], axis=0)]
    ppermute x6 -> x14, waiting for transfers between devices: 0.02 us -> 16.8 us  [the longest x6 9.76 us: swap(): return lax.ppermute(x, 'sub', [(i, i ^ m) for i in range(subs)])]
    all_to_all x0 -> x1, blocking collectives: none -> 13 us  [shards(): sums = lax.all_to_all(sums, ('leaf', 'sub'), 0, 0, tiled=True)]
  transfers between devices with their start and end apart: 6 -> 14, of which waited for: 0 -> 6; matrix products, arithmetic and copies ran while one was open for 4% -> 1% of each run, Pallas kernels for 0% -> 22%
where the time goes in v1:
time: 95.4 us; the launch traced here: 94.9 us
  Pallas kernels  34.8 us (36%)
  starting transfers between devices  21.8 us (23%)
  waiting for transfers between devices  16.8 us (18%)
  blocking collectives  13 us (14%)
  local copies, waits for them, and re-layouts  4.24 us (4%)
  other arithmetic  3.62 us (4%)
    pallas_call x6, Pallas kernels, call(): pl.pallas_call(kernel, out_shape=tuple(outs), in_specs=smem(scalars) + vm...  34.8 us
    ppermute x6, starting transfers between devices, spread_groups(): came = lax.ppermute(held, 'leaf', [(i, i ^ bit) for i in range(groups)])  15.2 us
    all_to_all x1, blocking collectives, shards(): sums = lax.all_to_all(sums, ('leaf', 'sub'), 0, 0, tiled=True)  13 us
    ppermute x6, waiting for transfers between devices, swap(): return lax.ppermute(x, 'sub', [(i, i ^ m) for i in range(subs)])  9.76 us
    ppermute x6, waiting for transfers between devices, spread_groups(): came = lax.ppermute(held, 'leaf', [(i, i ^ bit) for i in range(groups)])  6.99 us
    ppermute x6, starting transfers between devices, swap(): return lax.ppermute(x, 'sub', [(i, i ^ m) for i in range(subs)])  5.26 us
    unnamed x18, local copies, waits for them, and re-layouts  3.02 us
  transfers between devices with their start and end apart: 14, of which 6 were waited for; matrix products, arithmetic and copies ran while one was open for 1% of the time, Pallas kernels for 22%

profile of v1, /device:TPU:0, one launch (start us, length us, event | category | flops | bytes accessed | tf_op | source)
XLA Modules:
  0.0 94.9 jit_solution(7591467688109029704)
XLA Ops:
  0.6 2.6 %coefficients.1 = (f32[40,896]{1,0:T(8,128)}, f32[40,384]{1,0:T(8,128)}, f32[40,896]{1,0:T(8,128)}, f32[40,512]{1,0:T(8,128)}) custom-call(f32[32,1024]{1,0:T(8,128)} %vec_ref.7, f32[3,1024]{1,0:T(4,128)} %coords_ref.3, f32[3,256]{1,0:T(4,128)} %skel_ref.1, f32[3,64]{1,0:T(4,128)} %gskel_ref.3, f32[4,64,256]{2,1,0:T(8,128)} %basis_ref.5, f32[256,64]{1,0:T(8,128)} %bitcast.8, ...), custom_call_target="tpu_custom_call" | custom-call | bytes 1000000 | tf_op jit(solution)/shard_map/coefficients/pallas_call | solution.py:325
  3.7 2.6 %collective-permute-start.2 = (f32[40,896]{1,0:T(8,128)}, f32[40,896]{1,0:T(8,128)S(1)}, u32[]{:S(2)}, u32[]{:S(2)}) collective-permute-start(f32[40,896]{1,0:T(8,128)} %get-tuple-element.24), channel_id=1, source_target_pairs={{0,3},{1,2},{2,1},{3,0},{4,7},{5,6},{6,5},{7,4},{8,11},{9,10},{10,... | collective-permute-start | bytes 430088 | tf_op jit(solution)/shard_map/ppermute | solution.py:350
  6.3 0.7 slice.31
  7.0 5.1 %collective-permute-done.1.r2 = f32[40,384]{1,0:T(8,128)S(1)} collective-permute-done((f32[40,384]{1,0:T(8,128)}, f32[40,384]{1,0:T(8,128)S(1)}, u32[]{:S(2)}, u32[]{:S(2)}) %collective-permute-start.1) | collective-permute-done | bytes 61472 | tf_op jit(solution)/shard_map/ppermute | solution.py:350
  12.2 0.8 fusion.2
  13.0 1.7 %collective-permute-start.4 = (f32[1,40,128]{2,1,0:T(8,128)S(1)}, f32[1,40,128]{2,1,0:T(8,128)S(1)}, u32[]{:S(2)}, u32[]{:S(2)}) collective-permute-start(f32[1,40,128]{2,1,0:T(8,128)S(1)} %maximum_bitcast_fusion), channel_id=1, source_target_pairs={{0,4},{4,0},{8,12},{12,8},{16,20},{20,16},{24,28},{28,24},{1,5},{5... | collective-permute-start | bytes 61448 | tf_op jit(solution)/shard_map/ppermute | solution.py:366
  14.7 2.1 %collective-permute-done.4 = f32[1,40,128]{2,1,0:T(8,128)S(1)} collective-permute-done((f32[1,40,128]{2,1,0:T(8,128)S(1)}, f32[1,40,128]{2,1,0:T(8,128)S(1)}, u32[]{:S(2)}, u32[]{:S(2)}) %collective-permute-start.4) | collective-permute-done | bytes 20512 | tf_op jit(solution)/shard_map/ppermute | solution.py:366
  16.8 1.7 %collective-permute-start.5 = (f32[2,40,128]{2,1,0:T(8,128)S(1)}, f32[2,40,128]{2,1,0:T(8,128)S(1)}, u32[]{:S(2)}, u32[]{:S(2)}) collective-permute-start(f32[2,40,128]{2,1,0:T(8,128)S(1)} %pad_maximum_fusion.4), channel_id=1, source_target_pairs={{0,8},{4,12},{8,0},{12,4},{16,24},{20,28},{24,16},{28,20},{1,9},{5... | collective-permute-start | bytes 122888 | tf_op jit(solution)/shard_map/ppermute | solution.py:366
  18.5 0.7 collective-permute-start.3
  19.2 1.6 %collective-permute-done.5 = f32[2,40,128]{2,1,0:T(8,128)S(1)} collective-permute-done((f32[2,40,128]{2,1,0:T(8,128)S(1)}, f32[2,40,128]{2,1,0:T(8,128)S(1)}, u32[]{:S(2)}, u32[]{:S(2)}) %collective-permute-start.5) | collective-permute-done | bytes 40992 | tf_op jit(solution)/shard_map/ppermute | solution.py:366
  20.8 3.1 %collective-permute-start.6 = (f32[4,40,128]{2,1,0:T(8,128)S(1)}, f32[4,40,128]{2,1,0:T(8,128)S(1)}, u32[]{:S(2)}, u32[]{:S(2)}) collective-permute-start(f32[4,40,128]{2,1,0:T(8,128)S(1)} %pad_maximum_fusion.2), channel_id=1, source_target_pairs={{0,16},{4,20},{8,24},{12,28},{16,0},{20,4},{24,8},{28,12},{1,17},{... | collective-permute-start | bytes 245768 | tf_op jit(solution)/shard_map/ppermute | solution.py:366
  23.9 0.6 copy-done.6
  24.6 16.3 %tiles.1 = (bf16[4,1280,256]{2,1,0:T(8,128)(2,1)}, bf16[4,1280,256]{2,1,0:T(8,128)(2,1)}, bf16[1024,256]{1,0:T(8,128)(2,1)}, bf16[1024,256]{1,0:T(8,128)(2,1)}, f32[32,1024]{1,0:T(8,128)}, /*index=5*/f32[32,256]{1,0:T(8,128)}) custom-call(s32[4,5]{1,0:T(4,128)} %near_ref.1, s32[4,8]{1,0:T(4,128)} %far_ref.1, f32[32,1024]{1,0:T(8,128)} %vec_ref.7, ...), custom_call_target="tpu_custom_call" | custom-call | bytes 1000000 | tf_op jit(solution)/shard_map/tiles/pallas_call | solution.py:325
  40.9 0.7 pad_maximum_fusion.group_ref
  41.6 4.6 %middle.1 = (f32[32,1024]{1,0:T(8,128)}, f32[8,64,64]{2,1,0:T(8,128)}, f32[32,896]{1,0:T(8,128)}, f32[32,384]{1,0:T(8,128)}, f32[32,896]{1,0:T(8,128)}, /*index=5*/f32[32,512]{1,0:T(8,128)}) custom-call(s32[1,14]{1,0:T(1,128)} %list_ref.1, f32[32,1024]{1,0:T(8,128)} %get-tuple-element.26.part_ref, f32[32,256]{1,0:T(8,128)} %get-tuple-element.27.lf_ref, ...), custom_call_target="tpu_custom_call" | custom-call | bytes 1000000 | tf_op jit(solution)/shard_map/middle/pallas_call | solution.py:325
  46.2 1.7 %collective-permute-start.9 = (f32[32,896]{1,0:T(8,128)}, f32[32,896]{1,0:T(8,128)S(1)}, u32[]{:S(2)}, u32[]{:S(2)}) collective-permute-start(f32[32,896]{1,0:T(8,128)} %get-tuple-element.31), channel_id=1, source_target_pairs={{0,3},{1,2},{2,1},{3,0},{4,7},{5,6},{6,5},{7,4},{8,11},{9,10},{10,... | collective-permute-start | bytes 344072 | tf_op jit(solution)/shard_map/ppermute | solution.py:350
  48.3 4.6 %collective-permute-done.8.r2 = f32[32,384]{1,0:T(8,128)S(1)} collective-permute-done((f32[32,384]{1,0:T(8,128)}, f32[32,384]{1,0:T(8,128)S(1)}, u32[]{:S(2)}, u32[]{:S(2)}) %collective-permute-start.8) | collective-permute-done | bytes 49184 | tf_op jit(solution)/shard_map/ppermute | solution.py:350
  53.0 0.8 fusion.1
  53.7 3.0 %collective-permute-start.11 = (f32[1,32,128]{2,1,0:T(8,128)S(1)}, f32[1,32,128]{2,1,0:T(8,128)S(1)}, u32[]{:S(2)}, u32[]{:S(2)}) collective-permute-start(f32[1,32,128]{2,1,0:T(8,128)S(1)} %fusion.1), channel_id=1, source_target_pairs={{0,4},{4,0},{8,12},{12,8},{16,20},{20,16},{24,28},{28,24},{1,5},{5... | collective-permute-start | bytes 49160 | tf_op jit(solution)/shard_map/ppermute | solution.py:366
  56.7 1.7 %collective-permute-done.11 = f32[1,32,128]{2,1,0:T(8,128)S(1)} collective-permute-done((f32[1,32,128]{2,1,0:T(8,128)S(1)}, f32[1,32,128]{2,1,0:T(8,128)S(1)}, u32[]{:S(2)}, u32[]{:S(2)}) %collective-permute-start.11) | collective-permute-done | bytes 16416 | tf_op jit(solution)/shard_map/ppermute | solution.py:366
  58.4 1.7 %collective-permute-start.12 = (f32[2,32,128]{2,1,0:T(8,128)S(1)}, f32[2,32,128]{2,1,0:T(8,128)S(1)}, u32[]{:S(2)}, u32[]{:S(2)}) collective-permute-start(f32[2,32,128]{2,1,0:T(8,128)S(1)} %pad_maximum_fusion.5), channel_id=1, source_target_pairs={{0,8},{4,12},{8,0},{12,4},{16,24},{20,28},{24,16},{28,20},{1,9},{5... | collective-permute-start | bytes 98312 | tf_op jit(solution)/shard_map/ppermute | solution.py:366
  60.2 0.7 collective-permute-start.10
  60.8 1.5 %collective-permute-done.12 = f32[2,32,128]{2,1,0:T(8,128)S(1)} collective-permute-done((f32[2,32,128]{2,1,0:T(8,128)S(1)}, f32[2,32,128]{2,1,0:T(8,128)S(1)}, u32[]{:S(2)}, u32[]{:S(2)}) %collective-permute-start.12) | collective-permute-done | bytes 32800 | tf_op jit(solution)/shard_map/ppermute | solution.py:366
  62.4 4.0 %collective-permute-start.13 = (f32[4,32,128]{2,1,0:T(8,128)S(1)}, f32[4,32,128]{2,1,0:T(8,128)S(1)}, u32[]{:S(2)}, u32[]{:S(2)}) collective-permute-start(f32[4,32,128]{2,1,0:T(8,128)S(1)} %pad_maximum_fusion.3), channel_id=1, source_target_pairs={{0,16},{4,20},{8,24},{12,28},{16,0},{20,4},{24,8},{28,12},{1,17},{... | collective-permute-start | bytes 196616 | tf_op jit(solution)/shard_map/ppermute | solution.py:366
  67.0 4.8 %local.1 = (f32[32,1024]{1,0:T(8,128)}, f32[32,256]{1,0:T(8,128)}) custom-call(f32[32,1024]{1,0:T(8,128)} %get-tuple-element.28.vec_ref.first_ref, f32[32,384]{1,0:T(8,128)} %get-tuple-element.29.own, f32[32,896]{1,0:T(8,128)} %copy-done.2, f32[32,384]{1,0:T(8,128)} %copy-done.5, f32[32,896]{1,0:T(8,128)} %copy-done.3, f32[32,512]{1,0:T(8,128)} %copy-done.7, ...), custom_call_target="tpu_custom_call" | custom-call | bytes 1000000 | tf_op jit(solution)/shard_map/local/pallas_call | solution.py:325
  71.8 0.7 pad_maximum_fusion.1.group_ref
  72.5 4.3 %last.1 = (f32[32,1024]{1,0:T(8,128)}, f32[256,32]{1,0:T(8,128)}) custom-call(f32[32,1024]{1,0:T(8,128)} %vec_ref.7, f32[32,1024]{1,0:T(8,128)} %get-tuple-element.28.vec_ref.first_ref, f32[32,1024]{1,0:T(8,128)} %get-tuple-element.37.part_ref, f32[32,256]{1,0:T(8,128)} %get-tuple-element.38.lf_ref, f32[8,32,128]{2,1,0:T(8,128)} %pad_maximum_fusion.1.group_ref, ...), custom_call_target="tpu_custom_call" | custom-call | bytes 1000000 | tf_op jit(solution)/shard_map/last/pallas_call | solution.py:325
  76.7 1.0 %reshape.10 = f32[32,1,256]{2,1,0:T(1,128)S(1)} reshape(f32[32,8,32]{2,1,0:T(8,128)} %bitcast.15) | data formatting | bytes 65536
  77.7 13.0 %all_to_all.11 = f32[32,1,256]{2,1,0:T(1,128)S(1)} all-to-all(f32[32,1,256]{2,1,0:T(1,128)S(1)} %reshape.10), channel_id=1, replica_groups=mesh['leaf'=8,'sub'=4] {'leaf','sub'}, dimensions={0} | all-to-all | bytes 65536 | tf_op jit(solution)/shard_map/all_to_all | solution.py:448
  91.3 0.7 reduce
  92.0 0.7 reshape.11
  92.7 2.2 %update.1 = (f32[32,1024]{1,0:T(8,128)}, f32[32,1024]{1,0:T(8,128)}) custom-call(f32[256,32]{1,0:T(8,128)} %bitcast.11, f32[32,1024]{1,0:T(8,128)} %vec_ref.7, f32[32,1024]{1,0:T(8,128)} %get-tuple-element.28.vec_ref.first_ref, f32[32,1024]{1,0:T(8,128)} %get-tuple-element.41.second_ref), custom_call_target="tpu_custom_call" | custom-call | bytes 1000000 | tf_op jit(solution)/shard_map/update/pallas_call | solution.py:325
  (33 shorter events, 2.2 us)
Async XLA Ops:
  3.2 9.0 %collective-permute-start = (f32[40,896]{1,0:T(8,128)}, f32[40,896]{1,0:T(8,128)S(1)}, u32[]{:S(2)}, u32[]{:S(2)}) collective-permute-start(f32[40,896]{1,0:T(8,128)} %get-tuple-element.23), channel_id=1, source_target_pairs={{0,1},{1,0},{2,3},{3,2},{4,5},{5,4},{6,7},{7,6},{8,9},{9,8},{10,11... | collective-permute-start | bytes 430088 | tf_op jit(solution)/shard_map/ppermute | solution.py:350
  3.7 8.5 %collective-permute-start.2 = (f32[40,896]{1,0:T(8,128)}, f32[40,896]{1,0:T(8,128)S(1)}, u32[]{:S(2)}, u32[]{:S(2)}) collective-permute-start(f32[40,896]{1,0:T(8,128)} %get-tuple-element.24), channel_id=1, source_target_pairs={{0,3},{1,2},{2,1},{3,0},{4,7},{5,6},{6,5},{7,4},{8,11},{9,10},{10,... | collective-permute-start | bytes 430088 | tf_op jit(solution)/shard_map/ppermute | solution.py:350
  6.3 5.8 %collective-permute-start.1 = (f32[40,384]{1,0:T(8,128)}, f32[40,384]{1,0:T(8,128)S(1)}, u32[]{:S(2)}, u32[]{:S(2)}) collective-permute-start(f32[40,384]{1,0:T(8,128)} %get-tuple-element.22.own), channel_id=1, source_target_pairs={{0,2},{1,3},{2,0},{3,1},{4,6},{5,7},{6,4},{7,5},{8,10},{9,11},{10,... | collective-permute-start | bytes 184328 | tf_op jit(solution)/shard_map/ppermute | solution.py:350
  12.2 11.8 %copy-start.4 = (f32[40,384]{1,0:T(8,128)}, f32[40,384]{1,0:T(8,128)S(1)}, u32[]{:S(2)}) copy-start(f32[40,384]{1,0:T(8,128)S(1)} %collective-permute-done.1.r2) | copy-start | bytes 184324
  12.2 11.7 %copy-start = (f32[40,896]{1,0:T(8,128)}, f32[40,896]{1,0:T(8,128)S(1)}, u32[]{:S(2)}) copy-start(f32[40,896]{1,0:T(8,128)S(1)} %collective-permute-done.r1) | copy-start | bytes 430084
  12.2 11.7 %copy-start.1 = (f32[40,896]{1,0:T(8,128)}, f32[40,896]{1,0:T(8,128)S(1)}, u32[]{:S(2)}) copy-start(f32[40,896]{1,0:T(8,128)S(1)} %collective-permute-done.2.r3) | copy-start | bytes 430084
  13.0 3.8 %collective-permute-start.4 = (f32[1,40,128]{2,1,0:T(8,128)S(1)}, f32[1,40,128]{2,1,0:T(8,128)S(1)}, u32[]{:S(2)}, u32[]{:S(2)}) collective-permute-start(f32[1,40,128]{2,1,0:T(8,128)S(1)} %maximum_bitcast_fusion), channel_id=1, source_target_pairs={{0,4},{4,0},{8,12},{12,8},{16,20},{20,16},{24,28},{28,24},{1,5},{5... | collective-permute-start | bytes 61448 | tf_op jit(solution)/shard_map/ppermute | solution.py:366
  16.8 4.0 %collective-permute-start.5 = (f32[2,40,128]{2,1,0:T(8,128)S(1)}, f32[2,40,128]{2,1,0:T(8,128)S(1)}, u32[]{:S(2)}, u32[]{:S(2)}) collective-permute-start(f32[2,40,128]{2,1,0:T(8,128)S(1)} %pad_maximum_fusion.4), channel_id=1, source_target_pairs={{0,8},{4,12},{8,0},{12,4},{16,24},{20,28},{24,16},{28,20},{1,9},{5... | collective-permute-start | bytes 122888 | tf_op jit(solution)/shard_map/ppermute | solution.py:366
  18.5 5.4 %collective-permute-start.3 = (f32[40,512]{1,0:T(8,128)}, f32[40,512]{1,0:T(8,128)S(1)}, u32[]{:S(2)}, u32[]{:S(2)}) collective-permute-start(f32[40,512]{1,0:T(8,128)} %get-tuple-element.25), channel_id=1, source_target_pairs={{3,4},{7,8},{11,12},{15,16},{19,20},{23,24},{27,28},{4,3},{8,7},{1... | collective-permute-start | bytes 245768 | tf_op jit(solution)/shard_map/ppermute | solution.py:354
  20.8 20.1 %collective-permute-start.6 = (f32[4,40,128]{2,1,0:T(8,128)S(1)}, f32[4,40,128]{2,1,0:T(8,128)S(1)}, u32[]{:S(2)}, u32[]{:S(2)}) collective-permute-start(f32[4,40,128]{2,1,0:T(8,128)S(1)} %pad_maximum_fusion.2), channel_id=1, source_target_pairs={{0,16},{4,20},{8,24},{12,28},{16,0},{20,4},{24,8},{28,12},{1,17},{... | collective-permute-start | bytes 245768 | tf_op jit(solution)/shard_map/ppermute | solution.py:366
  23.9 0.6 copy-start.6
  46.2 6.8 %collective-permute-start.7 = (f32[32,896]{1,0:T(8,128)}, f32[32,896]{1,0:T(8,128)S(1)}, u32[]{:S(2)}, u32[]{:S(2)}) collective-permute-start(f32[32,896]{1,0:T(8,128)} %get-tuple-element.30), channel_id=1, source_target_pairs={{0,1},{1,0},{2,3},{3,2},{4,5},{5,4},{6,7},{7,6},{8,9},{9,8},{10,11... | collective-permute-start | bytes 344072 | tf_op jit(solution)/shard_map/ppermute | solution.py:350
  46.2 6.8 %collective-permute-start.9 = (f32[32,896]{1,0:T(8,128)}, f32[32,896]{1,0:T(8,128)S(1)}, u32[]{:S(2)}, u32[]{:S(2)}) collective-permute-start(f32[32,896]{1,0:T(8,128)} %get-tuple-element.31), channel_id=1, source_target_pairs={{0,3},{1,2},{2,1},{3,0},{4,7},{5,6},{6,5},{7,4},{8,11},{9,10},{10,... | collective-permute-start | bytes 344072 | tf_op jit(solution)/shard_map/ppermute | solution.py:350
  47.9 5.1 %collective-permute-start.8 = (f32[32,384]{1,0:T(8,128)}, f32[32,384]{1,0:T(8,128)S(1)}, u32[]{:S(2)}, u32[]{:S(2)}) collective-permute-start(f32[32,384]{1,0:T(8,128)} %get-tuple-element.29.own), channel_id=1, source_target_pairs={{0,2},{1,3},{2,0},{3,1},{4,6},{5,7},{6,4},{7,5},{8,10},{9,11},{10,... | collective-permute-start | bytes 147464 | tf_op jit(solution)/shard_map/ppermute | solution.py:350
  52.9 13.4 %copy-start.5 = (f32[32,384]{1,0:T(8,128)}, f32[32,384]{1,0:T(8,128)S(1)}, u32[]{:S(2)}) copy-start(f32[32,384]{1,0:T(8,128)S(1)} %collective-permute-done.8.r2) | copy-start | bytes 147460
  53.0 13.4 %copy-start.2 = (f32[32,896]{1,0:T(8,128)}, f32[32,896]{1,0:T(8,128)S(1)}, u32[]{:S(2)}) copy-start(f32[32,896]{1,0:T(8,128)S(1)} %collective-permute-done.7.r1) | copy-start | bytes 344068
  53.0 13.4 %copy-start.3 = (f32[32,896]{1,0:T(8,128)}, f32[32,896]{1,0:T(8,128)S(1)}, u32[]{:S(2)}) copy-start(f32[32,896]{1,0:T(8,128)S(1)} %collective-permute-done.9.r3) | copy-start | bytes 344068
  53.7 4.7 %collective-permute-start.11 = (f32[1,32,128]{2,1,0:T(8,128)S(1)}, f32[1,32,128]{2,1,0:T(8,128)S(1)}, u32[]{:S(2)}, u32[]{:S(2)}) collective-permute-start(f32[1,32,128]{2,1,0:T(8,128)S(1)} %fusion.1), channel_id=1, source_target_pairs={{0,4},{4,0},{8,12},{12,8},{16,20},{20,16},{24,28},{28,24},{1,5},{5... | collective-permute-start | bytes 49160 | tf_op jit(solution)/shard_map/ppermute | solution.py:366
  58.4 3.9 %collective-permute-start.12 = (f32[2,32,128]{2,1,0:T(8,128)S(1)}, f32[2,32,128]{2,1,0:T(8,128)S(1)}, u32[]{:S(2)}, u32[]{:S(2)}) collective-permute-start(f32[2,32,128]{2,1,0:T(8,128)S(1)} %pad_maximum_fusion.5), channel_id=1, source_target_pairs={{0,8},{4,12},{8,0},{12,4},{16,24},{20,28},{24,16},{28,20},{1,9},{5... | collective-permute-start | bytes 98312 | tf_op jit(solution)/shard_map/ppermute | solution.py:366
  60.2 6.2 %collective-permute-start.10 = (f32[32,512]{1,0:T(8,128)}, f32[32,512]{1,0:T(8,128)S(1)}, u32[]{:S(2)}, u32[]{:S(2)}) collective-permute-start(f32[32,512]{1,0:T(8,128)} %get-tuple-element.32), channel_id=1, source_target_pairs={{3,4},{7,8},{11,12},{15,16},{19,20},{23,24},{27,28},{4,3},{8,7},{1... | collective-permute-start | bytes 196616 | tf_op jit(solution)/shard_map/ppermute | solution.py:354
  62.4 9.4 %collective-permute-start.13 = (f32[4,32,128]{2,1,0:T(8,128)S(1)}, f32[4,32,128]{2,1,0:T(8,128)S(1)}, u32[]{:S(2)}, u32[]{:S(2)}) collective-permute-start(f32[4,32,128]{2,1,0:T(8,128)S(1)} %pad_maximum_fusion.3), channel_id=1, source_target_pairs={{0,16},{4,20},{8,24},{12,28},{16,0},{20,4},{24,8},{28,12},{1,17},{... | collective-permute-start | bytes 196616 | tf_op jit(solution)/shard_map/ppermute | solution.py:366
  66.4 0.6 copy-start.7

commit v2 on v1

v2 whole, which is shorter than its diff:
```python
from functools import partial
import jax
import jax.numpy as jnp
from jax import lax
from jax.experimental import pallas as pl
from jax.experimental.pallas import tpu as pltpu
from jax.sharding import PartitionSpec as P

REACH = 2
NOISE = 1.0
ROOT_FIVE = 5.0**0.5
LOG2_E = 1.4426950408889634
HIGHEST = lax.Precision.HIGHEST
F32 = jnp.float32
BF16 = jnp.bfloat16
DOWN = 2.0**-40
UP = 2.0**20
LANE = 128
EXTRA = 8
CHUNK = 32
GRANT = 16 * 2**20
DENSE = 1024


def dot(a, b, ca=1, cb=0):
    return lax.dot_general(
        a, b, (((ca,), (cb,)), ((), ())), precision=HIGHEST, preferred_element_type=F32
    )


def split(x):
    high = x.astype(BF16)
    return high, (x - high.astype(F32)).astype(BF16)


def stacked(x):
    return jnp.concatenate(split(x), axis=0)


def product(stack, high, low, transposed=False):
    rows = stack.shape[0] // 2
    dims = (((1,), (1 if transposed else 0,)), ((), ()))
    both = lax.dot_general(stack, high, dims, preferred_element_type=F32)
    more = lax.dot_general(stack[:rows], low, dims, preferred_element_type=F32)
    return (both[:rows] + both[rows:]) + more


def matern(rows, cols, weight):
    total = None
    for row, col in zip(rows, cols):
        spread = row - col
        total = spread * spread if total is None else total + spread * spread
    distance = total * lax.rsqrt(jnp.maximum(total, 1e-35))
    poly = (weight + (ROOT_FIVE * weight) * distance) + ((5.0 / 3.0) * weight) * total
    return poly * jnp.exp2((-ROOT_FIVE * LOG2_E) * distance)


def named(list_ref, row, index):
    hit = list_ref[row, 0] == index
    for column in range(1, list_ref.shape[1]):
        hit = jnp.logical_or(hit, list_ref[row, column] == index)
    return jnp.where(hit, 1.0, 0.0).astype(F32)


def padded_lanes(x, lanes):
    return jnp.concatenate(
        [x, jnp.zeros((x.shape[0], lanes - x.shape[1]), x.dtype)], axis=1
    )


def padded_rows(x, rows):
    return jnp.concatenate(
        [x, jnp.zeros((rows - x.shape[0], x.shape[1]), x.dtype)], axis=0
    )


def write_messages(vec, coefs, term, outs, half, rows):
    m1, own, m4 = outs
    count = vec.shape[1]
    even = lax.axis_index("sub") % 2 == 0
    low = vec[:, :half]
    high = vec[:, count - half :]
    span = coefs.shape[1]
    base = own.shape[1]
    for ref in (m1, own):
        ref[rows, 0:span] = coefs
        ref[rows, span:base] = term
    m1[rows, base : base + half] = jnp.where(even, high, low)
    m4[rows, :] = jnp.where(even, low, high)


def halos(r1, r4, rows, base):
    odd = lax.axis_index("sub") % 2 == 1
    from_a = r1[rows, base:]
    from_b = r4[rows, :]
    return jnp.where(odd, from_a, from_b), jnp.where(odd, from_b, from_a)


def first_kernel(
    list_ref, vec_ref, coords_ref, skel_ref, gskel_ref, basis_ref, transfer_ref, device_ref,
    *outs,
):
    leaves, rank, leaf = basis_ref.shape
    probes = vec_ref.shape[0]
    half = REACH * leaf
    vec = vec_ref[...]
    coefs = jnp.concatenate(
        [dot(vec[:, i * leaf : (i + 1) * leaf], basis_ref[i], 1, 1) for i in range(leaves)],
        axis=1,
    )
    term = padded_lanes(dot(dot(coefs, transfer_ref[...]), device_ref[...]), LANE)
    write_messages(vec, coefs, term, outs, half, slice(0, probes))
    relative = lax.axis_index("leaf") ^ lax.broadcasted_iota(jnp.int32, (1, LANE), 1)
    listed = jnp.zeros((1, LANE), F32)
    for column in range(list_ref.shape[1]):
        listed = jnp.where(relative == list_ref[0, column], 1.0, listed)
    group_rows = jnp.concatenate([padded_lanes(gskel_ref[...], LANE), listed], axis=0)
    write_messages(
        padded_rows(coords_ref[...], EXTRA),
        padded_rows(skel_ref[...], EXTRA),
        padded_rows(group_rows, EXTRA),
        outs,
        half,
        slice(probes, probes + EXTRA),
    )


def spread_columns(points, wide_ref):
    columns = points.T
    for axis in range(3):
        wide_ref[axis] = jnp.broadcast_to(
            columns[:, axis : axis + 1], (columns.shape[0], LANE)
        )


def fill_tile(wide_ref, source, points_ref, top_row, lane, width, weight, pair, row, size):
    high_ref, low_ref = pair

    def body(step, _):
        start = pl.multiple_of(source + step * CHUNK, CHUNK)
        target = pl.multiple_of(row + step * CHUNK, CHUNK)
        rows = [wide_ref[axis, pl.ds(start, CHUNK), :] for axis in range(3)]
        for at in range(0, width, LANE):
            cols = [
                points_ref[top_row + axis : top_row + axis + 1, lane + at : lane + at + LANE]
                for axis in range(3)
            ]
            factor = weight[:, at : at + LANE] if weight.ndim else weight
            top, rest = split(matern(rows, cols, factor))
            high_ref[pl.ds(target, CHUNK), at : at + LANE] = top
            low_ref[pl.ds(target, CHUNK), at : at + LANE] = rest
        return 0

    lax.fori_loop(0, size // CHUNK, body, 0, unroll=2)


def window_tiles(leaves):
    inside = []
    across = []
    for i in range(leaves):
        for j in range(i - REACH, i + REACH + 1):
            (inside if 0 <= j < leaves else across).append((i, j))
    return inside, across


def prepare_kernel(
    near_ref, vec_ref, coords_ref, basis_ref, transfer_ref, device_ref,
    th_ref, tl_ref, ubh_ref, ubl_ref, copy_ref, points_ref, wide_ref,
):
    leaves, rank, leaf = basis_ref.shape
    copy_ref[...] = vec_ref[...]
    first = (lax.axis_index("leaf") * lax.axis_size("sub") + lax.axis_index("sub")) * leaves
    points_ref[...] = padded_rows(coords_ref[...], EXTRA)
    spread_columns(points_ref[...], wide_ref)
    for at, (i, j) in enumerate(window_tiles(leaves)[0]):
        fill_tile(
            wide_ref, j * leaf, points_ref, 0, i * leaf, leaf, named(near_ref, i, first + j),
            (th_ref, tl_ref), at * leaf, leaf,
        )
    chain = dot(transfer_ref[...], device_ref[...])
    for i in range(leaves):
        basis = basis_ref[i]
        group_basis = dot(chain[i * rank : (i + 1) * rank], basis, 0, 0)
        top, rest = split(jnp.concatenate([basis, group_basis], axis=0))
        ubh_ref[i] = top
        ubl_ref[i] = rest


def term_kernel(own, r1, r2, r3, out_ref):
    rows = out_ref.shape[0] - EXTRA
    span = own.shape[1] - LANE
    out_ref[rows:, :] = own[rows:, span:]
    out_ref[0:rows, :] = (own[0:rows, span:] + r1[0:rows, span : span + LANE]) + (
        r2[0:rows, span:] + r3[0:rows, span:]
    )


def local_part(vec, low, high, blocks, tiles, bases, out_ref):
    th_ref, tl_ref, hh_ref, hl_ref, klh_ref, kll_ref = tiles
    ubh_ref, ubl_ref = bases
    leaves, double, leaf = ubh_ref.shape
    rank = double // 2
    inside, across = window_tiles(leaves)
    low, own, high = stacked(low), stacked(vec), stacked(high)

    def piece(j):
        if j < 0:
            return low[:, (j + REACH) * leaf : (j + REACH + 1) * leaf]
        if j >= leaves:
            return high[:, (j - leaves) * leaf : (j - leaves + 1) * leaf]
        return own[:, j * leaf : (j + 1) * leaf]

    far = product(stacked(jnp.concatenate(blocks, axis=1)), klh_ref[...], kll_ref[...])
    far_stack = stacked(far)
    near = []
    for i in range(leaves):
        total = NOISE * vec[:, i * leaf : (i + 1) * leaf]
        for pairs, high_ref, low_ref in ((inside, th_ref, tl_ref), (across, hh_ref, hl_ref)):
            at = [n for n, pair in enumerate(pairs) if pair[0] == i]
            if at:
                where = slice(at[0] * leaf, (at[-1] + 1) * leaf)
                wide = jnp.concatenate([piece(pairs[n][1]) for n in at], axis=1)
                total = total + product(wide, high_ref[where, :], low_ref[where, :])
        near.append(total)
        out_ref[:, i * leaf : (i + 1) * leaf] = total + product(
            far_stack[:, i * rank : (i + 1) * rank], ubh_ref[i, 0:rank, :], ubl_ref[i, 0:rank, :]
        )
    return jnp.concatenate(near, axis=1), far


def border_kernel(
    near_ref, far_ref, vec_ref, own, r1, r2, r3, r4, points_ref, th_ref, tl_ref, ubh_ref, ubl_ref,
    hh_ref, hl_ref, klh_ref, kll_ref, part_ref,
    ends_ref, wide_ref, skel_wide_ref,
):
    leaves = near_ref.shape[0]
    probes, count = vec_ref.shape
    leaf = count // leaves
    half = REACH * leaf
    base = own.shape[1]
    span = klh_ref.shape[1]
    rank = span // leaves
    sub = lax.axis_index("sub")
    group_first = lax.axis_index("leaf") * lax.axis_size("sub") * leaves
    first = group_first + sub * leaves
    extra = slice(probes, probes + EXTRA)
    rows = slice(0, probes)
    low, high = halos(r1, r4, extra, base)
    ends_ref[:, 0:half] = low
    ends_ref[:, half:] = high
    spread_columns(ends_ref[...], wide_ref)
    for at, (i, j) in enumerate(window_tiles(leaves)[1]):
        source = (j + REACH) * leaf if j < 0 else half + (j - leaves) * leaf
        fill_tile(
            wide_ref, source, points_ref, 0, i * leaf, leaf, named(near_ref, i, first + j),
            (hh_ref, hl_ref), at * leaf, leaf,
        )
    messages = (own, r1, r2, r3)
    lane_leaf = lax.broadcasted_iota(jnp.int32, (1, span), 1) // rank
    for m, message in enumerate(messages):
        spread_columns(message[extra, 0:span], skel_wide_ref.at[m])
    for m in range(len(messages)):
        for j in range(leaves):
            index = group_first + (sub ^ m) * leaves + j
            mask = jnp.zeros((1, span), F32)
            for i in range(leaves):
                mask = jnp.where(lane_leaf == i, named(far_ref, i, index), mask)
            fill_tile(
                skel_wide_ref.at[m], j * rank, own, probes, 0, span, mask,
                (klh_ref, kll_ref), m * span + j * rank, rank,
            )
    low, high = halos(r1, r4, rows, base)
    local_part(
        vec_ref[...], low, high, [r[rows, 0:span] for r in messages],
        (th_ref, tl_ref, hh_ref, hl_ref, klh_ref, kll_ref), (ubh_ref, ubl_ref), part_ref,
    )


def row_sum(x):
    return jnp.sum(x, axis=1, keepdims=True)


def local_kernel(
    rhs_ref, vec_ref, own, r1, r2, r3, r4, th_ref, tl_ref, hh_ref, hl_ref, klh_ref, kll_ref,
    ubh_ref, ubl_ref, part_ref, message_ref,
):
    base = own.shape[1]
    span = klh_ref.shape[1]
    rank = ubh_ref.shape[1] // 2
    rows = slice(0, vec_ref.shape[0])
    rhs = rhs_ref[...]
    vec = vec_ref[...]
    low, high = halos(r1, r4, rows, base)
    blocks = [r[rows, 0:span] for r in (own, r1, r2, r3)]
    near, far = local_part(
        vec, low, high, blocks,
        (th_ref, tl_ref, hh_ref, hl_ref, klh_ref, kll_ref), (ubh_ref, ubl_ref), part_ref,
    )
    shares = (
        row_sum(rhs * rhs),
        row_sum(rhs * vec),
        row_sum(vec * vec),
        row_sum((DOWN * vec) * near) + row_sum((DOWN * blocks[0]) * far),
    )
    term = (own[:, span:base] + r1[:, span:base]) + (r2[:, span:base] + r3[:, span:base])
    lane = lax.broadcasted_iota(jnp.int32, term.shape, 1)
    for at, share in enumerate(shares):
        term = jnp.where(lane == rank + at, share, term)
    message_ref[...] = term


def group_row(group_ref, rows, rank):
    groups = group_ref.shape[0]
    return jnp.concatenate([group_ref[m, rows, 0:rank] for m in range(groups)], axis=1)


def group_mask(group_ref, row, block, rank):
    groups = group_ref.shape[0]
    listed = group_ref[block, row : row + 1, :]
    lane_group = lax.broadcasted_iota(jnp.int32, (1, groups * rank), 1) // rank
    mask = jnp.zeros((1, groups * rank), F32)
    for m in range(groups):
        mask = jnp.where(lane_group == m, listed[:, block ^ m : (block ^ m) + 1], mask)
    return mask


def middle_kernel(
    part_ref, group_ref, ubh_ref, ubl_ref, image_ref, kgh_ref, kgl_ref, *rest,
):
    outs = rest[:3]
    points_ref, wide_ref = rest[3:]
    leaves, double, leaf = ubh_ref.shape
    rank = double // 2
    groups = group_ref.shape[0]
    probes = part_ref.shape[0]
    points_ref[...] = group_row(group_ref, slice(probes, probes + EXTRA), rank)
    spread_columns(group_ref[0, probes : probes + EXTRA, :], wide_ref)
    fill_tile(
        wide_ref, 0, points_ref, 0, 0, groups * rank,
        group_mask(group_ref, probes + 3, 0, rank), (kgh_ref, kgl_ref), 0, rank,
    )
    held = group_row(group_ref, slice(0, probes), rank)
    group_far = product(stacked(held), kgh_ref[...], kgl_ref[...], True)
    group_stack = stacked(group_far)
    image = []
    coefs = []
    term = None
    for i in range(leaves):
        piece = part_ref[:, i * leaf : (i + 1) * leaf] + product(
            group_stack, ubh_ref[i, rank:, :], ubl_ref[i, rank:, :]
        )
        image.append(piece)
        both = product(stacked(piece), ubh_ref[i], ubl_ref[i], True)
        coefs.append(both[:, :rank])
        term = both if term is None else term + both
    image = jnp.concatenate(image, axis=1)
    image_ref[...] = image
    write_messages(
        image, jnp.concatenate(coefs, axis=1), padded_lanes(term[:, rank:], LANE), outs,
        REACH * leaf, slice(0, probes),
    )


def groups_kernel(group_ref, kah_ref, kal_ref, points_ref, wide_ref):
    groups, rows, _ = group_ref.shape
    rank = kah_ref.shape[0] // groups
    probes = rows - EXTRA
    points_ref[...] = group_row(group_ref, slice(probes, rows), rank)
    spread_columns(points_ref[...], wide_ref)
    for m in range(groups):
        fill_tile(
            wide_ref, m * rank, points_ref, 0, 0, groups * rank,
            group_mask(group_ref, probes + 3, m, rank), (kah_ref, kal_ref), m * rank, rank,
        )


def last_kernel(part_ref, group_ref, kah_ref, kal_ref, ubh_ref, ubl_ref, second_ref, pair_ref):
    leaves, double, leaf = ubh_ref.shape
    rank = double // 2
    probes = part_ref.shape[0]
    held = group_row(group_ref, slice(0, probes), rank)
    far = product(stacked(held), kah_ref[...], kal_ref[...], True)
    group_stack = stacked(far[:, :rank])
    for i in range(leaves):
        second_ref[:, i * leaf : (i + 1) * leaf] = part_ref[:, i * leaf : (i + 1) * leaf] + product(
            group_stack, ubh_ref[i, rank:, :], ubl_ref[i, rank:, :]
        )
    share = row_sum((DOWN * held[:, : far.shape[1]]) * far)
    pair_ref[...] = jnp.broadcast_to(share, (probes, LANE))


def update_kernel(
    rank, own, s1, s2, s3, pair_ref, vec_ref, first_ref, second_ref, solution_ref, residual_ref,
):
    sums = (own[...] + s1[...]) + (s2[...] + s3[...])
    bb, bw, ww, wv = (sums[:, rank + k : rank + k + 1] for k in range(4))
    wv = wv + pair_ref[:, 0:1]
    step = bb / bw
    rise = (step * ww) * step
    norm = rise - bb
    grow = rise / bb
    scaled = step * UP
    curvature = (grow * grow) * bw - (2.0 * grow) * (step * ww) + (scaled * wv) * scaled
    again = norm / curvature
    vec = vec_ref[...]
    first = first_ref[...]
    second = second_ref[...]
    direction = grow * vec - step * first
    solution_ref[...] = step * vec + again * direction
    residual_ref[...] = (vec - step * first) - again * (grow * first - step * second)


def vmem(count):
    return [pl.BlockSpec(memory_space=pltpu.VMEM)] * count


def smem(count):
    return [pl.BlockSpec(memory_space=pltpu.SMEM)] * count


def shape(*dims, dtype=F32):
    return jax.ShapeDtypeStruct(dims, dtype)


def pair(*dims):
    return [shape(*dims, dtype=BF16)] * 2


def call(kernel, outs, args, scalars=0, scratch=(), name=None, flops=0):
    return pl.pallas_call(
        kernel,
        out_shape=tuple(outs),
        in_specs=smem(scalars) + vmem(len(args) - scalars),
        out_specs=tuple(vmem(len(outs))),
        scratch_shapes=[pltpu.VMEM(dims, F32) for dims in scratch],
        name=name,
        compiler_params=pltpu.CompilerParams(vmem_limit_bytes=GRANT),
        cost_estimate=pl.CostEstimate(
            flops=flops, transcendentals=0, bytes_accessed=1000000
        ),
    )(*args)


def swap(x, axis, m):
    return lax.ppermute(x, axis, [(i, i ^ m) for i in range(lax.axis_size(axis))])


def exchange(m1, own, m4):
    nodes = lax.axis_size("sub") * lax.axis_size("leaf")
    across = [(q, q + 1) for q in range(1, nodes - 1, 2)]
    across = across + [(target, source) for source, target in across]
    return (
        swap(m1, "sub", 1),
        swap(own, "sub", 2),
        swap(own, "sub", 3),
        lax.ppermute(m4, ("leaf", "sub"), across),
    )


def spread_groups(held):
    held = held[None]
    bit = 1
    while bit < lax.axis_size("leaf"):
        held = jnp.concatenate([held, swap(held, "leaf", bit)], axis=0)
        bit = 2 * bit
    return held


def far_memory(*args):
    return [pltpu.with_memory_space_constraint(x, pltpu.HBM) for x in args]


def shards(
    probe_rhs,
    coords,
    near_list,
    far_leaf_list,
    far_group_list,
    leaf_basis,
    leaf_skeleton,
    leaf_transfer,
    device_transfer,
    group_skeleton,
):
    leaves, rank, leaf = leaf_basis.shape
    probes, count = probe_rhs.shape
    groups = lax.axis_size("leaf")
    half = REACH * leaf
    span = leaves * rank
    base = span + LANE
    inside, across = window_tiles(leaves)
    transfer = leaf_transfer.reshape(span, rank)
    device = device_transfer[0]

    def messages(rows):
        return [shape(rows, base + half), shape(rows, base), shape(rows, half)]

    sent = call(
        first_kernel,
        messages(probes + EXTRA),
        far_memory(
            far_group_list, probe_rhs, coords, leaf_skeleton, group_skeleton, leaf_basis,
            transfer, device,
        ),
        scalars=1,
        name="coefficients",
    )
    own = sent[1]
    r1, r2, r3, r4 = exchange(*sent)
    th, tl, ubh, ubl, rhs, points = call(
        prepare_kernel,
        pair(len(inside) * leaf, leaf)
        + pair(leaves, 2 * rank, leaf)
        + [shape(probes, count), shape(EXTRA, count)],
        far_memory(near_list, probe_rhs, coords, leaf_basis, transfer, device),
        scalars=1,
        scratch=[(3, count, LANE)],
        name="prepare",
        flops=4 * 10**9,
    )
    (term,) = call(
        term_kernel, [shape(probes + EXTRA, LANE)], (own, r1, r2, r3), name="term"
    )
    gathered = spread_groups(term)
    hh, hl, klh, kll, part = call(
        border_kernel,
        pair(len(across) * leaf, leaf)
        + pair(lax.axis_size("sub") * span, span)
        + [shape(probes, count)],
        (near_list, far_leaf_list, rhs, own, r1, r2, r3, r4, points, th, tl, ubh, ubl),
        scalars=2,
        scratch=[
            (EXTRA, 2 * half),
            (3, 2 * half, LANE),
            (lax.axis_size("sub"), 3, span, LANE),
        ],
        name="border",
        flops=4 * 10**9,
    )
    image, kgh, kgl, *sent = call(
        middle_kernel,
        [shape(probes, count)] + pair(rank, groups * rank) + messages(probes),
        (part, gathered, ubh, ubl),
        scratch=[(EXTRA, groups * rank), (3, LANE, LANE)],
        name="middle",
    )
    own = sent[1]
    r1, r2, r3, r4 = exchange(*sent)
    dense = groups * rank <= DENSE
    if dense:
        kgh, kgl = call(
            groups_kernel,
            pair(groups * rank, groups * rank),
            (gathered,),
            scratch=[(EXTRA, groups * rank), (3, groups * rank, LANE)],
            name="groups",
            flops=2 * 10**9,
        )
    part, message = call(
        local_kernel,
        [shape(probes, count), shape(probes, LANE)],
        (rhs, image, own, r1, r2, r3, r4, th, tl, hh, hl, klh, kll, ubh, ubl),
        name="local",
    )
    gathered = spread_groups(message)
    sums = jnp.sum(gathered, axis=0)
    shares = [swap(sums, "sub", m) for m in range(1, lax.axis_size("sub"))]
    second, group_pair = call(
        last_kernel,
        [shape(probes, count), shape(probes, LANE)],
        (part, gathered, kgh, kgl, ubh, ubl),
        name="last",
        flops=10**9,
    )
    if not dense:
        group_pair = lax.psum(group_pair, "leaf")
    return call(
        partial(update_kernel, rank),
        [shape(probes, count), shape(probes, count)],
        (sums, *shares, group_pair, rhs, image, second),
        name="update",
    )


def solution(mesh):
    return jax.shard_map(
        shards,
        mesh=mesh,
        in_specs=(
            P(None, ("leaf", "sub")),
            P(None, ("leaf", "sub")),
            P(("leaf", "sub"), None),
            P(("leaf", "sub"), None),
            P("leaf", None),
            P(("leaf", "sub"), None, None),
            P(None, ("leaf", "sub")),
            P(("leaf", "sub"), None, None),
            P(("leaf", "sub"), None, None),
            P(None, "leaf"),
        ),
        out_specs=(P(None, ("leaf", "sub")), P(None, ("leaf", "sub"))),
        check_vma=False,
    )
```

time: 95.4 us -> 59.9 us (0.63)
  Pallas kernels: 34.8 us -> 18 us
  blocking collectives: 13 us -> 0 us
  local copies, waits for them, and re-layouts: 4.24 us -> 0.01 us
  other arithmetic: 3.62 us -> 0.07 us
  starting transfers between devices: 21.8 us -> 23.2 us
    pallas_call x6 -> x9, Pallas kernels: 34.8 us -> 18 us  [call(): pl.pallas_call(kernel, out_shape=tuple(outs), in_specs=smem(scalars) + vm...]
    all_to_all x1 -> x0, blocking collectives: 13 us -> none  [shards(): sums = lax.all_to_all(sums, ('leaf', 'sub'), 0, 0, tiled=True)]
    unnamed x18 -> x4, local copies, waits for them, and re-layouts: 3.02 us -> 0.01 us
    ppermute x12 -> x15, starting transfers between devices: 20.5 us -> 21.9 us  [swap(): lax.ppermute(x, axis, [(i, i ^ m) for i in range(lax.axis_size(axis))])]
    concatenate x6, other arithmetic: 1.36 us -> 0.05 us  [spread_groups(): held = jnp.concatenate([held, swap(held, 'leaf', bit)], axis=0)]
    ppermute x12 -> x15, waiting for transfers between devices: 16.8 us -> 17.6 us  [swap(): lax.ppermute(x, axis, [(i, i ^ m) for i in range(lax.axis_size(axis))])]
  transfers between devices with their start and end apart: 14 -> 17, of which waited for: 6 -> 10; matrix products, arithmetic and copies ran while one was open for 1% -> 0% of each run, Pallas kernels for 22% -> 21%
where the time goes in v2:
time: 59.9 us; the launch traced here: 59.7 us
  starting transfers between devices  23.2 us (39%)
  Pallas kernels  18 us (30%)
  waiting for transfers between devices  17.7 us (30%)
  between operations  0.78 us (1%)
    ppermute x15, starting transfers between devices, swap(): lax.ppermute(x, axis, [(i, i ^ m) for i in range(lax.axis_size(axis))])  21.9 us
    pallas_call x9, Pallas kernels, call(): pl.pallas_call(kernel, out_shape=tuple(outs), in_specs=smem(scalars) + vm...  18 us
    ppermute x15, waiting for transfers between devices, swap(): lax.ppermute(x, axis, [(i, i ^ m) for i in range(lax.axis_size(axis))])  17.6 us
    ppermute x2, starting transfers between devices, exchange(): lax.ppermute(m4, ('leaf', 'sub'), across)  1.32 us
  transfers between devices with their start and end apart: 17, of which 10 were waited for; matrix products, arithmetic and copies ran while one was open for 0% of the time, Pallas kernels for 21%

profile of v2, /device:TPU:0, one launch (start us, length us, event | category | flops | bytes accessed | tf_op | source)
XLA Modules:
  0.0 59.7 jit_solution(3770016806460392668)
XLA Ops:
  0.6 1.8 %coefficients.1 = (f32[40,896]{1,0:T(8,128)S(1)}, f32[40,384]{1,0:T(8,128)S(1)}, f32[40,512]{1,0:T(8,128)S(1)}) custom-call(s32[1,14]{1,0:T(1,128)} %list_ref.1, f32[32,1024]{1,0:T(8,128)} %vec_ref.3, f32[3,1024]{1,0:T(4,128)} %coords_ref.3, f32[3,256]{1,0:T(4,128)} %skel_ref.1, f32[3,64]{1,0:T(4,128)} %gskel_ref.1, f32[4,64,256]{2,1,0:T(8,128)} %basis_ref.3, ...), custom_call_target="tpu_custom_call" | custom-call | bytes 1000000 | tf_op jit(solution)/shard_map/coefficients/pallas_call | solution.py:430
  2.5 0.6 collective-permute-start
  3.0 2.6 %collective-permute-start.1 = (f32[40,384]{1,0:T(8,128)S(1)}, f32[40,384]{1,0:T(8,128)S(1)}, u32[]{:S(2)}, u32[]{:S(2)}) collective-permute-start(f32[40,384]{1,0:T(8,128)S(1)} %get-tuple-element.27.own), channel_id=1, source_target_pairs={{0,2},{1,3},{2,0},{3,1},{4,6},{5,7},{6,4},{7,5},{8,10},{9,11},{10,... | collective-permute-start | bytes 184328 | tf_op jit(solution)/shard_map/ppermute | solution.py:445
  5.7 2.6 %collective-permute-done.1.r2 = f32[40,384]{1,0:T(8,128)S(1)} collective-permute-done((f32[40,384]{1,0:T(8,128)S(1)}, f32[40,384]{1,0:T(8,128)S(1)}, u32[]{:S(2)}, u32[]{:S(2)}) %collective-permute-start.1) | collective-permute-done | bytes 61472 | tf_op jit(solution)/shard_map/ppermute | solution.py:445
  8.2 1.4 %collective-permute-done.2.r3 = f32[40,384]{1,0:T(8,128)S(1)} collective-permute-done((f32[40,384]{1,0:T(8,128)S(1)}, f32[40,384]{1,0:T(8,128)S(1)}, u32[]{:S(2)}, u32[]{:S(2)}) %collective-permute-start.2) | collective-permute-done | bytes 61472 | tf_op jit(solution)/shard_map/ppermute | solution.py:445
  9.6 1.6 %collective-permute-start.4 = (f32[1,40,128]{2,1,0:T(8,128)S(1)}, f32[1,40,128]{2,1,0:T(8,128)S(1)}, u32[]{:S(2)}, u32[]{:S(2)}) collective-permute-start(f32[1,40,128]{2,1,0:T(8,128)S(1)} %bitcast.10), channel_id=1, source_target_pairs={{0,4},{4,0},{8,12},{12,8},{16,20},{20,16},{24,28},{28,24},{1,5},{5... | collective-permute-start | bytes 61448 | tf_op jit(solution)/shard_map/ppermute | solution.py:445
  11.2 0.7 %collective-permute-start.3 = (f32[40,512]{1,0:T(8,128)S(1)}, f32[40,512]{1,0:T(8,128)S(1)}, u32[]{:S(2)}, u32[]{:S(2)}) collective-permute-start(f32[40,512]{1,0:T(8,128)S(1)} %get-tuple-element.29), channel_id=1, source_target_pairs={{1,2},{3,4},{5,6},{7,8},{9,10},{11,12},{13,14},{15,16},{17,18},{19... | collective-permute-start | bytes 245768 | tf_op jit(solution)/shard_map/ppermute | solution.py:456
  11.8 1.6 %collective-permute-done.4 = f32[1,40,128]{2,1,0:T(8,128)S(1)} collective-permute-done((f32[1,40,128]{2,1,0:T(8,128)S(1)}, f32[1,40,128]{2,1,0:T(8,128)S(1)}, u32[]{:S(2)}, u32[]{:S(2)}) %collective-permute-start.4) | collective-permute-done | bytes 20512 | tf_op jit(solution)/shard_map/ppermute | solution.py:445
  13.5 2.0 %collective-permute-start.5 = (f32[2,40,128]{2,1,0:T(8,128)S(1)}, f32[2,40,128]{2,1,0:T(8,128)S(1)}, u32[]{:S(2)}, u32[]{:S(2)}) collective-permute-start(f32[2,40,128]{2,1,0:T(8,128)S(1)} %pad_maximum_fusion.4), channel_id=1, source_target_pairs={{0,8},{4,12},{8,0},{12,4},{16,24},{20,28},{24,16},{28,20},{1,9},{5... | collective-permute-start | bytes 122888 | tf_op jit(solution)/shard_map/ppermute | solution.py:445
  15.4 6.0 %prepare.1 = (bf16[3584,256]{1,0:T(8,128)(2,1)S(1)}, bf16[3584,256]{1,0:T(8,128)(2,1)S(1)}, bf16[4,128,256]{2,1,0:T(8,128)(2,1)S(1)}, bf16[4,128,256]{2,1,0:T(8,...) custom-call(s32[4,5]{1,0:T(4,128)} %near_ref.3, f32[32,1024]{1,0:T(8,128)} %vec_ref.3, ...), custom_call_target="tpu_custom_call" | custom-call | flops 4000000000 | bytes 1000000 | tf_op jit(solution)/shard_map/prepare/pallas_call | solution.py:430
  21.5 2.7 %collective-permute-start.6 = (f32[4,40,128]{2,1,0:T(8,128)S(1)}, f32[4,40,128]{2,1,0:T(8,128)S(1)}, u32[]{:S(2)}, u32[]{:S(2)}) collective-permute-start(f32[4,40,128]{2,1,0:T(8,128)S(1)} %pad_maximum_fusion.2), channel_id=1, source_target_pairs={{0,16},{4,20},{8,24},{12,28},{16,0},{20,4},{24,8},{28,12},{1,17},{... | collective-permute-start | bytes 245768 | tf_op jit(solution)/shard_map/ppermute | solution.py:445
  24.2 5.1 %border.1 = (bf16[1536,256]{1,0:T(8,128)(2,1)S(1)}, bf16[1536,256]{1,0:T(8,128)(2,1)S(1)}, bf16[1024,256]{1,0:T(8,128)(2,1)S(1)}, bf16[1024,256]{1,0:T(8,128)(2,1)S(1)}, f32[32,1024]{1,0:T(8,128)S(1)}) custom-call(s32[4,5]{1,0:T(4,128)S(1)} %copy-done, s32[4,8]{1,0:T(4,128)S(1)} %copy-done.1, f32[32,1024]{1,0:T(8,128)S(1)} %get-tuple-element.26.vec_ref.rhs_ref, ...), custom_call_target="tpu_custom_call" | custom-call | flops 4000000000 | bytes 1000000 | tf_op jit(solution)/shard_map/border/pallas_call | solution.py:430
  29.3 1.0 %middle.1 = (f32[32,1024]{1,0:T(8,128)S(1)}, bf16[64,512]{1,0:T(8,128)(2,1)}, bf16[64,512]{1,0:T(8,128)(2,1)}, f32[32,896]{1,0:T(8,128)S(1)}, f32[32,384]{1,0:T(8,128)S(1)}, /*index=5*/f32[32,512]{1,0:T(8,128)S(1)}) custom-call(f32[32,1024]{1,0:T(8,128)S(1)} %get-tuple-element.35.part_ref, f32[8,40,128]{2,1,0:T(8,128)S(1)} %pad_maximum_fusion.group_ref, ...), custom_call_target="tpu_custom_call" | custom-call | bytes 1000000 | tf_op jit(solution)/shard_map/middle/pallas_call | solution.py:430
  30.3 0.1 collective-permute-start.7
  30.4 0.7 %collective-permute-start.10 = (f32[32,512]{1,0:T(8,128)S(1)}, f32[32,512]{1,0:T(8,128)S(1)}, u32[]{:S(2)}, u32[]{:S(2)}) collective-permute-start(f32[32,512]{1,0:T(8,128)S(1)} %get-tuple-element.39), channel_id=1, source_target_pairs={{1,2},{3,4},{5,6},{7,8},{9,10},{11,12},{13,14},{15,16},{17,18},{19... | collective-permute-start | bytes 196616 | tf_op jit(solution)/shard_map/ppermute | solution.py:456
  31.1 3.4 %collective-permute-start.8 = (f32[32,384]{1,0:T(8,128)S(1)}, f32[32,384]{1,0:T(8,128)S(1)}, u32[]{:S(2)}, u32[]{:S(2)}) collective-permute-start(f32[32,384]{1,0:T(8,128)S(1)} %get-tuple-element.37.own), channel_id=1, source_target_pairs={{0,2},{1,3},{2,0},{3,1},{4,6},{5,7},{6,4},{7,5},{8,10},{9,11},{10,... | collective-permute-start | bytes 147464 | tf_op jit(solution)/shard_map/ppermute | solution.py:445
  34.5 0.7 %collective-permute-start.9 = (f32[32,384]{1,0:T(8,128)S(1)}, f32[32,384]{1,0:T(8,128)S(1)}, u32[]{:S(2)}, u32[]{:S(2)}) collective-permute-start(f32[32,384]{1,0:T(8,128)S(1)} %get-tuple-element.37.own), channel_id=1, source_target_pairs={{0,3},{1,2},{2,1},{3,0},{4,7},{5,6},{6,5},{7,4},{8,11},{9,10},{10,... | collective-permute-start | bytes 147464 | tf_op jit(solution)/shard_map/ppermute | solution.py:445
  35.3 2.7 %collective-permute-done.8.r2 = f32[32,384]{1,0:T(8,128)S(1)} collective-permute-done((f32[32,384]{1,0:T(8,128)S(1)}, f32[32,384]{1,0:T(8,128)S(1)}, u32[]{:S(2)}, u32[]{:S(2)}) %collective-permute-start.8) | collective-permute-done | bytes 49184 | tf_op jit(solution)/shard_map/ppermute | solution.py:445
  37.9 0.3 collective-permute-done.9.r3
  38.2 1.4 %local.1 = (f32[32,1024]{1,0:T(8,128)S(1)}, f32[32,128]{1,0:T(8,128)S(1)}) custom-call(f32[32,1024]{1,0:T(8,128)S(1)} %get-tuple-element.26.vec_ref.rhs_ref, f32[32,1024]{1,0:T(8,128)S(1)} %get-tuple-element.36.vec_ref.first_ref, f32[32,384]{1,0:T(8,128)S(1)} %get-tuple-element.37.own, f32[32,896]{1,0:T(8,128)S(1)} %collective-permute-done.7.r1, ...), custom_call_target="tpu_custom_call" | custom-call | bytes 1000000 | tf_op jit(solution)/shard_map/local/pallas_call | solution.py:430
  39.6 2.4 %collective-permute-start.11 = (f32[1,32,128]{2,1,0:T(8,128)S(1)}, f32[1,32,128]{2,1,0:T(8,128)S(1)}, u32[]{:S(2)}, u32[]{:S(2)}) collective-permute-start(f32[1,32,128]{2,1,0:T(8,128)S(1)} %bitcast.14), channel_id=1, source_target_pairs={{0,4},{4,0},{8,12},{12,8},{16,20},{20,16},{24,28},{28,24},{1,5},{5... | collective-permute-start | bytes 49160 | tf_op jit(solution)/shard_map/ppermute | solution.py:445
  42.0 1.7 %collective-permute-done.11 = f32[1,32,128]{2,1,0:T(8,128)S(1)} collective-permute-done((f32[1,32,128]{2,1,0:T(8,128)S(1)}, f32[1,32,128]{2,1,0:T(8,128)S(1)}, u32[]{:S(2)}, u32[]{:S(2)}) %collective-permute-start.11) | collective-permute-done | bytes 16416 | tf_op jit(solution)/shard_map/ppermute | solution.py:445
  43.7 1.4 %collective-permute-start.12 = (f32[2,32,128]{2,1,0:T(8,128)S(1)}, f32[2,32,128]{2,1,0:T(8,128)S(1)}, u32[]{:S(2)}, u32[]{:S(2)}) collective-permute-start(f32[2,32,128]{2,1,0:T(8,128)S(1)} %pad_maximum_fusion.5), channel_id=1, source_target_pairs={{0,8},{4,12},{8,0},{12,4},{16,24},{20,28},{24,16},{28,20},{1,9},{5... | collective-permute-start | bytes 98312 | tf_op jit(solution)/shard_map/ppermute | solution.py:445
  45.0 2.6 %collective-permute-done.12 = f32[2,32,128]{2,1,0:T(8,128)S(1)} collective-permute-done((f32[2,32,128]{2,1,0:T(8,128)S(1)}, f32[2,32,128]{2,1,0:T(8,128)S(1)}, u32[]{:S(2)}, u32[]{:S(2)}) %collective-permute-start.12) | collective-permute-done | bytes 32800 | tf_op jit(solution)/shard_map/ppermute | solution.py:445
  47.6 1.7 %collective-permute-start.13 = (f32[4,32,128]{2,1,0:T(8,128)S(1)}, f32[4,32,128]{2,1,0:T(8,128)S(1)}, u32[]{:S(2)}, u32[]{:S(2)}) collective-permute-start(f32[4,32,128]{2,1,0:T(8,128)S(1)} %pad_maximum_fusion.3), channel_id=1, source_target_pairs={{0,16},{4,20},{8,24},{12,28},{16,0},{20,4},{24,8},{28,12},{1,17},{... | collective-permute-start | bytes 196616 | tf_op jit(solution)/shard_map/ppermute | solution.py:445
  49.4 1.1 %groups.1 = (bf16[512,512]{1,0:T(8,128)(2,1)S(1)}, bf16[512,512]{1,0:T(8,128)(2,1)S(1)}) custom-call(f32[8,40,128]{2,1,0:T(8,128)S(1)} %pad_maximum_fusion.group_ref), custom_call_target="tpu_custom_call" | custom-call | flops 2000000000 | bytes 1000000 | tf_op jit(solution)/shard_map/groups/pallas_call | solution.py:430
  50.5 2.3 %collective-permute-done.13 = f32[4,32,128]{2,1,0:T(8,128)S(1)} collective-permute-done((f32[4,32,128]{2,1,0:T(8,128)S(1)}, f32[4,32,128]{2,1,0:T(8,128)S(1)}, u32[]{:S(2)}, u32[]{:S(2)}) %collective-permute-start.13) | collective-permute-done | bytes 65568 | tf_op jit(solution)/shard_map/ppermute | solution.py:445
  52.9 2.7 %collective-permute-start.15 = (f32[32,128]{1,0:T(8,128)S(1)}, f32[32,128]{1,0:T(8,128)S(1)}, u32[]{:S(2)}, u32[]{:S(2)}) collective-permute-start(f32[32,128]{1,0:T(8,128)S(1)} %fusion.1.own), channel_id=1, source_target_pairs={{0,2},{1,3},{2,0},{3,1},{4,6},{5,7},{6,4},{7,5},{8,10},{9,11},{10,... | collective-permute-start | bytes 49160 | tf_op jit(solution)/shard_map/ppermute | solution.py:445
  55.7 0.6 last.1
  56.3 1.1 %collective-permute-done.15.s2 = f32[32,128]{1,0:T(8,128)S(1)} collective-permute-done((f32[32,128]{1,0:T(8,128)S(1)}, f32[32,128]{1,0:T(8,128)S(1)}, u32[]{:S(2)}, u32[]{:S(2)}) %collective-permute-start.15) | collective-permute-done | bytes 16416 | tf_op jit(solution)/shard_map/ppermute | solution.py:445
  57.3 1.4 %collective-permute-done.16.s3 = f32[32,128]{1,0:T(8,128)S(1)} collective-permute-done((f32[32,128]{1,0:T(8,128)S(1)}, f32[32,128]{1,0:T(8,128)S(1)}, u32[]{:S(2)}, u32[]{:S(2)}) %collective-permute-start.16) | collective-permute-done | bytes 16416 | tf_op jit(solution)/shard_map/ppermute | solution.py:445
  58.8 0.9 %update.1 = (f32[32,1024]{1,0:T(8,128)}, f32[32,1024]{1,0:T(8,128)}) custom-call(f32[32,128]{1,0:T(8,128)S(1)} %fusion.1.own, f32[32,128]{1,0:T(8,128)S(1)} %collective-permute-done.14.s1, f32[32,128]{1,0:T(8,128)S(1)} %collective-permute-done.15.s2, f32[32,128]{1,0:T(8,128)S(1)} %collective-permute-done.16.s3, f32[32,128]{1,0:T(8,128)S(1)} %get-tuple-element.48.pair_ref, ...), custom_call_target="tpu_custom_call" | custom-call | bytes 1000000 | tf_op jit(solution)/shard_map/update/pallas_call | solution.py:430
  (24 shorter events, 0.3 us)
Async XLA Ops:
  2.5 7.1 %collective-permute-start = (f32[40,896]{1,0:T(8,128)S(1)}, f32[40,896]{1,0:T(8,128)S(1)}, u32[]{:S(2)}, u32[]{:S(2)}) collective-permute-start(f32[40,896]{1,0:T(8,128)S(1)} %get-tuple-element.28), channel_id=1, source_target_pairs={{0,1},{1,0},{2,3},{3,2},{4,5},{5,4},{6,7},{7,6},{8,9},{9,8},{10,11... | collective-permute-start | bytes 430088 | tf_op jit(solution)/shard_map/ppermute | solution.py:445
  3.0 5.2 %collective-permute-start.1 = (f32[40,384]{1,0:T(8,128)S(1)}, f32[40,384]{1,0:T(8,128)S(1)}, u32[]{:S(2)}, u32[]{:S(2)}) collective-permute-start(f32[40,384]{1,0:T(8,128)S(1)} %get-tuple-element.27.own), channel_id=1, source_target_pairs={{0,2},{1,3},{2,0},{3,1},{4,6},{5,7},{6,4},{7,5},{8,10},{9,11},{10,... | collective-permute-start | bytes 184328 | tf_op jit(solution)/shard_map/ppermute | solution.py:445
  5.6 4.0 %collective-permute-start.2 = (f32[40,384]{1,0:T(8,128)S(1)}, f32[40,384]{1,0:T(8,128)S(1)}, u32[]{:S(2)}, u32[]{:S(2)}) collective-permute-start(f32[40,384]{1,0:T(8,128)S(1)} %get-tuple-element.27.own), channel_id=1, source_target_pairs={{0,3},{1,2},{2,1},{3,0},{4,7},{5,6},{6,5},{7,4},{8,11},{9,10},{10,... | collective-permute-start | bytes 184328 | tf_op jit(solution)/shard_map/ppermute | solution.py:445
  9.6 3.8 %collective-permute-start.4 = (f32[1,40,128]{2,1,0:T(8,128)S(1)}, f32[1,40,128]{2,1,0:T(8,128)S(1)}, u32[]{:S(2)}, u32[]{:S(2)}) collective-permute-start(f32[1,40,128]{2,1,0:T(8,128)S(1)} %bitcast.10), channel_id=1, source_target_pairs={{0,4},{4,0},{8,12},{12,8},{16,20},{20,16},{24,28},{28,24},{1,5},{5... | collective-permute-start | bytes 61448 | tf_op jit(solution)/shard_map/ppermute | solution.py:445
  11.2 13.0 %collective-permute-start.3 = (f32[40,512]{1,0:T(8,128)S(1)}, f32[40,512]{1,0:T(8,128)S(1)}, u32[]{:S(2)}, u32[]{:S(2)}) collective-permute-start(f32[40,512]{1,0:T(8,128)S(1)} %get-tuple-element.29), channel_id=1, source_target_pairs={{1,2},{3,4},{5,6},{7,8},{9,10},{11,12},{13,14},{15,16},{17,18},{19... | collective-permute-start | bytes 245768 | tf_op jit(solution)/shard_map/ppermute | solution.py:456
  13.5 10.7 %copy-start = (s32[4,5]{1,0:T(4,128)S(1)}, s32[4,5]{1,0:T(4,128)}, u32[]{:S(2)}) copy-start(s32[4,5]{1,0:T(4,128)} %near_ref.3) | copy-start | bytes 244
  13.5 10.7 %copy-start.1 = (s32[4,8]{1,0:T(4,128)S(1)}, s32[4,8]{1,0:T(4,128)}, u32[]{:S(2)}) copy-start(s32[4,8]{1,0:T(4,128)} %far_ref.1) | copy-start | bytes 388
  13.5 8.0 %collective-permute-start.5 = (f32[2,40,128]{2,1,0:T(8,128)S(1)}, f32[2,40,128]{2,1,0:T(8,128)S(1)}, u32[]{:S(2)}, u32[]{:S(2)}) collective-permute-start(f32[2,40,128]{2,1,0:T(8,128)S(1)} %pad_maximum_fusion.4), channel_id=1, source_target_pairs={{0,8},{4,12},{8,0},{12,4},{16,24},{20,28},{24,16},{28,20},{1,9},{5... | collective-permute-start | bytes 122888 | tf_op jit(solution)/shard_map/ppermute | solution.py:445
  21.5 7.8 %collective-permute-start.6 = (f32[4,40,128]{2,1,0:T(8,128)S(1)}, f32[4,40,128]{2,1,0:T(8,128)S(1)}, u32[]{:S(2)}, u32[]{:S(2)}) collective-permute-start(f32[4,40,128]{2,1,0:T(8,128)S(1)} %pad_maximum_fusion.2), channel_id=1, source_target_pairs={{0,16},{4,20},{8,24},{12,28},{16,0},{20,4},{24,8},{28,12},{1,17},{... | collective-permute-start | bytes 245768 | tf_op jit(solution)/shard_map/ppermute | solution.py:445
  30.3 7.9 %collective-permute-start.7 = (f32[32,896]{1,0:T(8,128)S(1)}, f32[32,896]{1,0:T(8,128)S(1)}, u32[]{:S(2)}, u32[]{:S(2)}) collective-permute-start(f32[32,896]{1,0:T(8,128)S(1)} %get-tuple-element.38), channel_id=1, source_target_pairs={{0,1},{1,0},{2,3},{3,2},{4,5},{5,4},{6,7},{7,6},{8,9},{9,8},{10,11... | collective-permute-start | bytes 344072 | tf_op jit(solution)/shard_map/ppermute | solution.py:445
  30.4 7.8 %collective-permute-start.10 = (f32[32,512]{1,0:T(8,128)S(1)}, f32[32,512]{1,0:T(8,128)S(1)}, u32[]{:S(2)}, u32[]{:S(2)}) collective-permute-start(f32[32,512]{1,0:T(8,128)S(1)} %get-tuple-element.39), channel_id=1, source_target_pairs={{1,2},{3,4},{5,6},{7,8},{9,10},{11,12},{13,14},{15,16},{17,18},{19... | collective-permute-start | bytes 196616 | tf_op jit(solution)/shard_map/ppermute | solution.py:456
  31.1 6.8 %collective-permute-start.8 = (f32[32,384]{1,0:T(8,128)S(1)}, f32[32,384]{1,0:T(8,128)S(1)}, u32[]{:S(2)}, u32[]{:S(2)}) collective-permute-start(f32[32,384]{1,0:T(8,128)S(1)} %get-tuple-element.37.own), channel_id=1, source_target_pairs={{0,2},{1,3},{2,0},{3,1},{4,6},{5,7},{6,4},{7,5},{8,10},{9,11},{10,... | collective-permute-start | bytes 147464 | tf_op jit(solution)/shard_map/ppermute | solution.py:445
  34.5 3.7 %collective-permute-start.9 = (f32[32,384]{1,0:T(8,128)S(1)}, f32[32,384]{1,0:T(8,128)S(1)}, u32[]{:S(2)}, u32[]{:S(2)}) collective-permute-start(f32[32,384]{1,0:T(8,128)S(1)} %get-tuple-element.37.own), channel_id=1, source_target_pairs={{0,3},{1,2},{2,1},{3,0},{4,7},{5,6},{6,5},{7,4},{8,11},{9,10},{10,... | collective-permute-start | bytes 147464 | tf_op jit(solution)/shard_map/ppermute | solution.py:445
  39.6 4.1 %collective-permute-start.11 = (f32[1,32,128]{2,1,0:T(8,128)S(1)}, f32[1,32,128]{2,1,0:T(8,128)S(1)}, u32[]{:S(2)}, u32[]{:S(2)}) collective-permute-start(f32[1,32,128]{2,1,0:T(8,128)S(1)} %bitcast.14), channel_id=1, source_target_pairs={{0,4},{4,0},{8,12},{12,8},{16,20},{20,16},{24,28},{28,24},{1,5},{5... | collective-permute-start | bytes 49160 | tf_op jit(solution)/shard_map/ppermute | solution.py:445
  43.7 3.9 %collective-permute-start.12 = (f32[2,32,128]{2,1,0:T(8,128)S(1)}, f32[2,32,128]{2,1,0:T(8,128)S(1)}, u32[]{:S(2)}, u32[]{:S(2)}) collective-permute-start(f32[2,32,128]{2,1,0:T(8,128)S(1)} %pad_maximum_fusion.5), channel_id=1, source_target_pairs={{0,8},{4,12},{8,0},{12,4},{16,24},{20,28},{24,16},{28,20},{1,9},{5... | collective-permute-start | bytes 98312 | tf_op jit(solution)/shard_map/ppermute | solution.py:445
  47.6 5.2 %collective-permute-start.13 = (f32[4,32,128]{2,1,0:T(8,128)S(1)}, f32[4,32,128]{2,1,0:T(8,128)S(1)}, u32[]{:S(2)}, u32[]{:S(2)}) collective-permute-start(f32[4,32,128]{2,1,0:T(8,128)S(1)} %pad_maximum_fusion.3), channel_id=1, source_target_pairs={{0,16},{4,20},{8,24},{12,28},{16,0},{20,4},{24,8},{28,12},{1,17},{... | collective-permute-start | bytes 196616 | tf_op jit(solution)/shard_map/ppermute | solution.py:445
  52.8 3.5 %collective-permute-start.14 = (f32[32,128]{1,0:T(8,128)S(1)}, f32[32,128]{1,0:T(8,128)S(1)}, u32[]{:S(2)}, u32[]{:S(2)}) collective-permute-start(f32[32,128]{1,0:T(8,128)S(1)} %fusion.1.own), channel_id=1, source_target_pairs={{0,1},{1,0},{2,3},{3,2},{4,5},{5,4},{6,7},{7,6},{8,9},{9,8},{10,11... | collective-permute-start | bytes 49160 | tf_op jit(solution)/shard_map/ppermute | solution.py:445
  52.9 4.4 %collective-permute-start.15 = (f32[32,128]{1,0:T(8,128)S(1)}, f32[32,128]{1,0:T(8,128)S(1)}, u32[]{:S(2)}, u32[]{:S(2)}) collective-permute-start(f32[32,128]{1,0:T(8,128)S(1)} %fusion.1.own), channel_id=1, source_target_pairs={{0,2},{1,3},{2,0},{3,1},{4,6},{5,7},{6,4},{7,5},{8,10},{9,11},{10,... | collective-permute-start | bytes 49160 | tf_op jit(solution)/shard_map/ppermute | solution.py:445
  55.6 3.2 %collective-permute-start.16 = (f32[32,128]{1,0:T(8,128)S(1)}, f32[32,128]{1,0:T(8,128)S(1)}, u32[]{:S(2)}, u32[]{:S(2)}) collective-permute-start(f32[32,128]{1,0:T(8,128)S(1)} %fusion.1.own), channel_id=1, source_target_pairs={{0,3},{1,2},{2,1},{3,0},{4,7},{5,6},{6,5},{7,4},{8,11},{9,10},{10,... | collective-permute-start | bytes 49160 | tf_op jit(solution)/shard_map/ppermute | solution.py:445

commit v3 on v2

v3 whole, which is shorter than its diff:
```python
import jax
import jax.numpy as jnp
from jax import lax
from jax.experimental import pallas as pl
from jax.experimental.pallas import tpu as pltpu
from jax.sharding import PartitionSpec as P

REACH = 2
NOISE = 1.0
ROOT_FIVE = 5.0**0.5
LOG2_E = 1.4426950408889634
HIGHEST = lax.Precision.HIGHEST
F32 = jnp.float32
BF16 = jnp.bfloat16
DOWN = 2.0**-40
UP = 2.0**20
LANE = 128
EXTRA = 8
CHUNK = 32
SHARES = 4
GRANT = 16 * 2**20
DENSE = 1024


def dot(a, b, ca=1, cb=0):
    return lax.dot_general(
        a, b, (((ca,), (cb,)), ((), ())), precision=HIGHEST, preferred_element_type=F32
    )


def split(x):
    high = x.astype(BF16)
    return high, (x - high.astype(F32)).astype(BF16)


def stacked(x):
    return jnp.concatenate(split(x), axis=0)


def product(stack, high, low, transposed=False):
    rows = stack.shape[0] // 2
    dims = (((1,), (1 if transposed else 0,)), ((), ()))
    both = lax.dot_general(stack, high, dims, preferred_element_type=F32)
    more = lax.dot_general(stack[:rows], low, dims, preferred_element_type=F32)
    return (both[:rows] + both[rows:]) + more


def matern(rows, cols, weight):
    total = None
    for row, col in zip(rows, cols):
        spread = row - col
        total = spread * spread if total is None else total + spread * spread
    distance = total * lax.rsqrt(jnp.maximum(total, 1e-35))
    poly = (weight + (ROOT_FIVE * weight) * distance) + ((5.0 / 3.0) * weight) * total
    return poly * jnp.exp2((-ROOT_FIVE * LOG2_E) * distance)


def named(list_ref, row, index):
    hit = list_ref[row, 0] == index
    for column in range(1, list_ref.shape[1]):
        hit = jnp.logical_or(hit, list_ref[row, column] == index)
    return jnp.where(hit, 1.0, 0.0).astype(F32)


def padded_lanes(x, lanes):
    return jnp.concatenate(
        [x, jnp.zeros((x.shape[0], lanes - x.shape[1]), x.dtype)], axis=1
    )


def padded_rows(x, rows):
    return jnp.concatenate(
        [x, jnp.zeros((rows - x.shape[0], x.shape[1]), x.dtype)], axis=0
    )


def write_messages(vec, coefs, term, outs, half, rows):
    m1, own, m4 = outs
    count = vec.shape[1]
    even = lax.axis_index("sub") % 2 == 0
    low = vec[:, :half]
    high = vec[:, count - half :]
    span = coefs.shape[1]
    base = own.shape[1]
    for ref in (m1, own):
        ref[rows, 0:span] = coefs
        ref[rows, span:base] = term
    m1[rows, base : base + half] = jnp.where(even, high, low)
    m4[rows, :] = jnp.where(even, low, high)


def halos(r1, r4, rows, base):
    odd = lax.axis_index("sub") % 2 == 1
    from_a = r1[rows, base:]
    from_b = r4[rows, :]
    return jnp.where(odd, from_a, from_b), jnp.where(odd, from_b, from_a)


def first_kernel(
    list_ref, vec_ref, coords_ref, skel_ref, gskel_ref, basis_ref, transfer_ref, device_ref,
    m1_ref, own_ref, m4_ref, rhs_ref, points_ref, basis_out, transfer_out, device_out,
):
    outs = (m1_ref, own_ref, m4_ref)
    leaves, _, leaf = basis_ref.shape
    probes = vec_ref.shape[0]
    half = REACH * leaf
    vec = vec_ref[...]
    coefs = jnp.concatenate(
        [dot(vec[:, i * leaf : (i + 1) * leaf], basis_ref[i], 1, 1) for i in range(leaves)],
        axis=1,
    )
    term = padded_lanes(dot(dot(coefs, transfer_ref[...]), device_ref[...]), LANE)
    write_messages(vec, coefs, term, outs, half, slice(0, probes))
    relative = lax.axis_index("leaf") ^ lax.broadcasted_iota(jnp.int32, (1, LANE), 1)
    listed = jnp.zeros((1, LANE), F32)
    for column in range(list_ref.shape[1]):
        listed = jnp.where(relative == list_ref[0, column], 1.0, listed)
    group_rows = jnp.concatenate([padded_lanes(gskel_ref[...], LANE), listed], axis=0)
    write_messages(
        padded_rows(coords_ref[...], EXTRA),
        padded_rows(skel_ref[...], EXTRA),
        padded_rows(group_rows, EXTRA),
        outs,
        half,
        slice(probes, probes + EXTRA),
    )
    rhs_ref[...] = vec
    points_ref[...] = padded_rows(coords_ref[...], EXTRA)
    basis_out[...] = basis_ref[...]
    transfer_out[...] = transfer_ref[...]
    device_out[...] = device_ref[...]


def spread_columns(points, wide_ref):
    columns = points.T
    for axis in range(3):
        wide_ref[axis] = jnp.broadcast_to(
            columns[:, axis : axis + 1], (columns.shape[0], LANE)
        )


def fill_tile(wide_ref, source, points_ref, top_row, lane, width, weight, pair, row, size):
    high_ref, low_ref = pair

    def body(step, _):
        start = pl.multiple_of(source + step * CHUNK, CHUNK)
        target = pl.multiple_of(row + step * CHUNK, CHUNK)
        rows = [wide_ref[axis, pl.ds(start, CHUNK), :] for axis in range(3)]
        for at in range(0, width, LANE):
            cols = [
                points_ref[top_row + axis : top_row + axis + 1, lane + at : lane + at + LANE]
                for axis in range(3)
            ]
            factor = weight[:, at : at + LANE] if weight.ndim else weight
            top, rest = split(matern(rows, cols, factor))
            high_ref[pl.ds(target, CHUNK), at : at + LANE] = top
            low_ref[pl.ds(target, CHUNK), at : at + LANE] = rest
        return 0

    lax.fori_loop(0, size // CHUNK, body, 0, unroll=2)


def window_tiles(leaves):
    inside = []
    across = []
    for i in range(leaves):
        for j in range(i - REACH, i + REACH + 1):
            if not 0 <= j < leaves:
                across.append((i, j))
            elif j >= i:
                inside.append((i, j))
    return inside, across


def prepare_kernel(
    near_ref, points_ref, basis_ref, transfer_ref, device_ref,
    th_ref, tl_ref, ubh_ref, ubl_ref, wide_ref,
):
    leaves, rank, leaf = basis_ref.shape
    first = (lax.axis_index("leaf") * lax.axis_size("sub") + lax.axis_index("sub")) * leaves
    spread_columns(points_ref[...], wide_ref)
    for at, (i, j) in enumerate(window_tiles(leaves)[0]):
        fill_tile(
            wide_ref, j * leaf, points_ref, 0, i * leaf, leaf, named(near_ref, i, first + j),
            (th_ref, tl_ref), at * leaf, leaf,
        )
    chain = dot(transfer_ref[...], device_ref[...])
    for i in range(leaves):
        basis = basis_ref[i]
        group_basis = dot(chain[i * rank : (i + 1) * rank], basis, 0, 0)
        top, rest = split(jnp.concatenate([basis, group_basis], axis=0))
        ubh_ref[i] = top
        ubl_ref[i] = rest


def folded(x, rank):
    half = x.shape[0] // 2
    return jnp.concatenate([x[:half, :rank], x[half:, :rank]], axis=1)


def summed_terms(own, r1, r2, r3, rows, span):
    lanes = slice(span, span + LANE)
    return (own[rows, lanes] + r1[rows, lanes]) + (r2[rows, lanes] + r3[rows, lanes])


def term_kernel(own, r1, r2, r3, out_ref):
    half = out_ref.shape[0] - EXTRA
    span = own.shape[1] - LANE
    out_ref[half:, :] = own[2 * half :, span:]
    out_ref[0:half, :] = folded(
        summed_terms(own, r1, r2, r3, slice(0, 2 * half), span), LANE // 2
    )


def leaf_slice(x, i, leaf):
    return x[:, i * leaf : (i + 1) * leaf]


def inner_kernel(vec_ref, th_ref, tl_ref, out_ref):
    vec = vec_ref[...]
    leaf = th_ref.shape[1]
    leaves = vec.shape[1] // leaf
    stack = stacked(vec)
    totals = [NOISE * leaf_slice(vec, i, leaf) for i in range(leaves)]
    for at, (i, j) in enumerate(window_tiles(leaves)[0]):
        rows = slice(at * leaf, (at + 1) * leaf)
        high, low = th_ref[rows, :], tl_ref[rows, :]
        totals[i] = totals[i] + product(leaf_slice(stack, j, leaf), high, low)
        if j > i:
            totals[j] = totals[j] + product(leaf_slice(stack, i, leaf), high, low, True)
    out_ref[...] = jnp.concatenate(totals, axis=1)


def local_part(inner_ref, low, high, blocks, tiles, bases, out_ref):
    hh_ref, hl_ref, klh_ref, kll_ref = tiles
    ubh_ref, ubl_ref = bases
    leaves, double, leaf = ubh_ref.shape
    rank = double // 2
    across = window_tiles(leaves)[1]
    low, high = stacked(low), stacked(high)

    def piece(j):
        return leaf_slice(low, j + REACH, leaf) if j < 0 else leaf_slice(high, j - leaves, leaf)

    far = product(stacked(jnp.concatenate(blocks, axis=1)), klh_ref[...], kll_ref[...])
    far_stack = stacked(far)
    near = []
    for i in range(leaves):
        total = inner_ref[:, i * leaf : (i + 1) * leaf]
        at = [n for n, pair in enumerate(across) if pair[0] == i]
        if at:
            where = slice(at[0] * leaf, (at[-1] + 1) * leaf)
            wide = jnp.concatenate([piece(across[n][1]) for n in at], axis=1)
            total = total + product(wide, hh_ref[where, :], hl_ref[where, :])
        near.append(total)
        out_ref[:, i * leaf : (i + 1) * leaf] = total + product(
            far_stack[:, i * rank : (i + 1) * rank], ubh_ref[i, 0:rank, :], ubl_ref[i, 0:rank, :]
        )
    return jnp.concatenate(near, axis=1), far


def skeleton_kernel(far_ref, own, r1, r2, r3, klh_ref, kll_ref, wide_ref):
    leaves = far_ref.shape[0]
    span = klh_ref.shape[1]
    rank = span // leaves
    probes = own.shape[0] - EXTRA
    sub = lax.axis_index("sub")
    group_first = lax.axis_index("leaf") * lax.axis_size("sub") * leaves
    messages = (own, r1, r2, r3)
    lane_leaf = lax.broadcasted_iota(jnp.int32, (1, span), 1) // rank
    for m, message in enumerate(messages):
        spread_columns(message[probes : probes + EXTRA, 0:span], wide_ref.at[m])
    for m in range(len(messages)):
        for j in range(leaves):
            index = group_first + (sub ^ m) * leaves + j
            mask = jnp.zeros((1, span), F32)
            for i in range(leaves):
                mask = jnp.where(lane_leaf == i, named(far_ref, i, index), mask)
            fill_tile(
                wide_ref.at[m], j * rank, own, probes, 0, span, mask,
                (klh_ref, kll_ref), m * span + j * rank, rank,
            )


def border_kernel(near_ref, r1, r4, points_ref, hh_ref, hl_ref, ends_ref, wide_ref):
    leaves = near_ref.shape[0]
    count = points_ref.shape[1]
    leaf = count // leaves
    half = REACH * leaf
    probes = r4.shape[0] - EXTRA
    first = (lax.axis_index("leaf") * lax.axis_size("sub") + lax.axis_index("sub")) * leaves
    low, high = halos(r1, r4, slice(probes, probes + EXTRA), r1.shape[1] - half)
    ends_ref[:, 0:half] = low
    ends_ref[:, half:] = high
    spread_columns(ends_ref[...], wide_ref)
    for at, (i, j) in enumerate(window_tiles(leaves)[1]):
        source = (j + REACH) * leaf if j < 0 else half + (j - leaves) * leaf
        fill_tile(
            wide_ref, source, points_ref, 0, i * leaf, leaf, named(near_ref, i, first + j),
            (hh_ref, hl_ref), at * leaf, leaf,
        )


def outer_kernel(
    inner_ref, own, r1, r2, r3, r4, hh_ref, hl_ref, klh_ref, kll_ref, ubh_ref, ubl_ref, part_ref,
):
    span = klh_ref.shape[1]
    rows = slice(0, inner_ref.shape[0])
    low, high = halos(r1, r4, rows, own.shape[1])
    local_part(
        inner_ref, low, high, [r[rows, 0:span] for r in (own, r1, r2, r3)],
        (hh_ref, hl_ref, klh_ref, kll_ref), (ubh_ref, ubl_ref), part_ref,
    )


def row_sum(x):
    return jnp.sum(x, axis=1, keepdims=True)


def local_kernel(
    rhs_ref, vec_ref, inner_ref, own, r1, r2, r3, r4, hh_ref, hl_ref, klh_ref, kll_ref,
    ubh_ref, ubl_ref, part_ref, message_ref,
):
    base = own.shape[1]
    span = klh_ref.shape[1]
    rank = ubh_ref.shape[1] // 2
    rows = slice(0, vec_ref.shape[0])
    rhs = rhs_ref[...]
    vec = vec_ref[...]
    low, high = halos(r1, r4, rows, base)
    blocks = [r[rows, 0:span] for r in (own, r1, r2, r3)]
    near, far = local_part(
        inner_ref, low, high, blocks,
        (hh_ref, hl_ref, klh_ref, kll_ref), (ubh_ref, ubl_ref), part_ref,
    )
    shares = (
        row_sum(rhs * rhs),
        row_sum(rhs * vec),
        row_sum(vec * vec),
        row_sum((DOWN * vec) * near) + row_sum((DOWN * blocks[0]) * far),
    )
    lane = lax.broadcasted_iota(jnp.int32, (vec.shape[0], LANE), 1)
    columns = jnp.zeros((vec.shape[0], LANE), F32)
    for at, share in enumerate(shares):
        columns = jnp.where(lane == at, share, columns)
    term = folded(summed_terms(own, r1, r2, r3, rows, span), rank)
    size = term.shape[0] // lax.axis_size("sub")
    sub = lax.axis_index("sub")
    mine = term[0:size]
    for m in range(1, lax.axis_size("sub")):
        mine = jnp.where(sub == m, term[m * size : (m + 1) * size], mine)
    message = jnp.concatenate([mine, padded_lanes(columns.T[0:SHARES], LANE)], axis=0)
    for m in range(message_ref.shape[0]):
        message_ref[m] = message


def exchange_order(groups):
    order = [0]
    for offsets in exchange_rounds(groups):
        order = order + [m ^ offset for offset in offsets for m in order]
    return order


def exchange_rounds(groups):
    if groups == 8:
        return [[2, 4, 6], [1]]
    return [[groups >> n] for n in range(1, groups.bit_length())]


def group_points(group_ref, half, rank):
    groups = group_ref.shape[0]
    return jnp.concatenate(
        [group_ref[m, half : half + EXTRA, 0:rank] for m in range(groups)], axis=1
    )


def group_row(group_ref, half, rank, places):
    return jnp.concatenate(
        [
            jnp.concatenate(
                [group_ref[m, 0:half, at : at + rank] for m in places], axis=1
            )
            for at in (0, rank)
        ],
        axis=0,
    )


def group_mask(group_ref, row, block, rank):
    groups = group_ref.shape[0]
    order = exchange_order(groups)
    listed = group_ref[block, row : row + 1, :]
    lane_group = lax.broadcasted_iota(jnp.int32, (1, groups * rank), 1) // rank
    mask = jnp.zeros((1, groups * rank), F32)
    for m in range(groups):
        at = order[block] ^ order[m]
        mask = jnp.where(lane_group == m, listed[:, at : at + 1], mask)
    return mask


def middle_kernel(
    part_ref, group_ref, ubh_ref, ubl_ref, image_ref, kgh_ref, kgl_ref, *rest,
):
    outs = rest[:3]
    points_ref, wide_ref = rest[3:]
    leaves, double, leaf = ubh_ref.shape
    rank = double // 2
    groups = group_ref.shape[0]
    probes = part_ref.shape[0]
    half = probes // 2
    points_ref[...] = group_points(group_ref, half, rank)
    spread_columns(group_ref[0, half : half + EXTRA, :], wide_ref)
    fill_tile(
        wide_ref, 0, points_ref, 0, 0, groups * rank,
        group_mask(group_ref, half + 3, 0, rank), (kgh_ref, kgl_ref), 0, rank,
    )
    held = group_row(group_ref, half, rank, range(groups))
    group_far = product(stacked(held), kgh_ref[...], kgl_ref[...], True)
    group_stack = stacked(group_far)
    image = []
    coefs = []
    term = None
    for i in range(leaves):
        piece = part_ref[:, i * leaf : (i + 1) * leaf] + product(
            group_stack, ubh_ref[i, rank:, :], ubl_ref[i, rank:, :]
        )
        image.append(piece)
        both = product(stacked(piece), ubh_ref[i], ubl_ref[i], True)
        coefs.append(both[:, :rank])
        term = both if term is None else term + both
    image = jnp.concatenate(image, axis=1)
    image_ref[...] = image
    write_messages(
        image, jnp.concatenate(coefs, axis=1), padded_lanes(term[:, rank:], LANE), outs,
        REACH * leaf, slice(0, probes),
    )


def groups_kernel(group_ref, kah_ref, kal_ref, points_ref, wide_ref):
    groups, rows, _ = group_ref.shape
    rank = kah_ref.shape[0] // groups
    half = rows - EXTRA
    points_ref[...] = group_points(group_ref, half, rank)
    spread_columns(points_ref[...], wide_ref)
    for m in range(groups):
        fill_tile(
            wide_ref, m * rank, points_ref, 0, 0, groups * rank,
            group_mask(group_ref, half + 3, m, rank), (kah_ref, kal_ref), m * rank, rank,
        )


def second_image(part_ref, group_ref, kah_ref, kal_ref, ubh_ref, ubl_ref):
    leaves, double, leaf = ubh_ref.shape
    rank = double // 2
    subs = lax.axis_size("sub")
    size = group_ref.shape[1] - SHARES
    mine = lax.axis_index("leaf")
    pieces = []
    for m in exchange_order(group_ref.shape[0] // subs):
        at = (mine ^ m) * subs
        pieces.append(jnp.concatenate([group_ref[at + k, 0:size, :] for k in range(subs)], axis=0))
    held = jnp.concatenate(
        [
            jnp.concatenate([x[:, lane : lane + rank] for x in pieces], axis=1)
            for lane in (0, rank)
        ],
        axis=0,
    )
    far = product(stacked(held), kah_ref[...], kal_ref[...], True)
    group_stack = stacked(far[:, :rank])
    second = [
        part_ref[:, i * leaf : (i + 1) * leaf]
        + product(group_stack, ubh_ref[i, rank:, :], ubl_ref[i, rank:, :])
        for i in range(leaves)
    ]
    return second, row_sum((DOWN * held[:, : far.shape[1]]) * far)


def update(group_ref, share, vec_ref, first_ref, second, solution_ref, residual_ref):
    total = group_ref[0]
    for q in range(1, group_ref.shape[0]):
        total = total + group_ref[q]
    sums = total.T[0 : vec_ref.shape[0]]
    at = group_ref.shape[1] - SHARES
    bb, bw, ww, wv = (sums[:, at + k : at + k + 1] for k in range(SHARES))
    wv = wv + share
    step = bb / bw
    rise = (step * ww) * step
    norm = rise - bb
    grow = rise / bb
    scaled = step * UP
    curvature = (grow * grow) * bw - (2.0 * grow) * (step * ww) + (scaled * wv) * scaled
    again = norm / curvature
    leaf = second[0].shape[1]
    for i, image in enumerate(second):
        lanes = slice(i * leaf, (i + 1) * leaf)
        vec = vec_ref[:, lanes]
        first = first_ref[:, lanes]
        direction = grow * vec - step * first
        solution_ref[:, lanes] = step * vec + again * direction
        residual_ref[:, lanes] = (vec - step * first) - again * (grow * first - step * image)


def final_kernel(
    part_ref, group_ref, kah_ref, kal_ref, ubh_ref, ubl_ref, vec_ref, first_ref,
    solution_ref, residual_ref,
):
    second, share = second_image(part_ref, group_ref, kah_ref, kal_ref, ubh_ref, ubl_ref)
    update(group_ref, share, vec_ref, first_ref, second, solution_ref, residual_ref)


def last_kernel(part_ref, group_ref, kah_ref, kal_ref, ubh_ref, ubl_ref, second_ref, share_ref):
    second, share = second_image(part_ref, group_ref, kah_ref, kal_ref, ubh_ref, ubl_ref)
    second_ref[...] = jnp.concatenate(second, axis=1)
    share_ref[...] = jnp.broadcast_to(share, share_ref.shape)


def update_kernel(
    group_ref, share_ref, vec_ref, first_ref, second_ref, solution_ref, residual_ref
):
    update(
        group_ref, share_ref[:, 0:1], vec_ref, first_ref, [second_ref[...]],
        solution_ref, residual_ref,
    )


def vmem(count):
    return [pl.BlockSpec(memory_space=pltpu.VMEM)] * count


def smem(count):
    return [pl.BlockSpec(memory_space=pltpu.SMEM)] * count


def shape(*dims, dtype=F32):
    return jax.ShapeDtypeStruct(dims, dtype)


def pair(*dims):
    return [shape(*dims, dtype=BF16)] * 2


def call(kernel, outs, args, scalars=0, scratch=(), flops=0):
    return pl.pallas_call(
        kernel,
        out_shape=tuple(outs),
        in_specs=smem(scalars) + vmem(len(args) - scalars),
        out_specs=tuple(vmem(len(outs))),
        scratch_shapes=[pltpu.VMEM(dims, F32) for dims in scratch],
        compiler_params=pltpu.CompilerParams(vmem_limit_bytes=GRANT),
        cost_estimate=pl.CostEstimate(
            flops=flops, transcendentals=0, bytes_accessed=1000000
        ),
    )(*args)


def swap(x, axis, m):
    return lax.ppermute(x, axis, [(i, i ^ m) for i in range(lax.axis_size(axis))])


def exchange(m1, own, m4):
    nodes = lax.axis_size("sub") * lax.axis_size("leaf")
    across = [(q, q + 1) for q in range(1, nodes - 1, 2)]
    across = across + [(target, source) for source, target in across]
    received = swap(m1, "sub", 1), swap(own, "sub", 2), swap(own, "sub", 3)
    return *received, lax.ppermute(m4, ("leaf", "sub"), across)


def spread_groups(held):
    held = held[None]
    for offsets in exchange_rounds(lax.axis_size("leaf")):
        held = jnp.concatenate([held] + [swap(held, "leaf", offset) for offset in offsets], axis=0)
    return held


def far_memory(*args):
    return [pltpu.with_memory_space_constraint(x, pltpu.HBM) for x in args]


def shards(
    probe_rhs,
    coords,
    near_list,
    far_leaf_list,
    far_group_list,
    leaf_basis,
    leaf_skeleton,
    leaf_transfer,
    device_transfer,
    group_skeleton,
):
    leaves, rank, leaf = leaf_basis.shape
    probes, count = probe_rhs.shape
    groups = lax.axis_size("leaf")
    subs = lax.axis_size("sub")
    half = REACH * leaf
    span = leaves * rank
    base = span + LANE
    inside, across = window_tiles(leaves)
    transfer = leaf_transfer.reshape(span, rank)
    device = device_transfer[0]

    def messages(rows):
        return [shape(rows, base + half), shape(rows, base), shape(rows, half)]

    *sent, rhs, points, basis, transfer, device = call(
        first_kernel,
        messages(probes + EXTRA)
        + [
            shape(probes, count),
            shape(EXTRA, count),
            shape(leaves, rank, leaf),
            shape(span, rank),
            shape(rank, rank),
        ],
        far_memory(
            far_group_list, probe_rhs, coords, leaf_skeleton, group_skeleton, leaf_basis,
            transfer, device,
        ),
        scalars=1,
    )
    own = sent[1]
    r1, r2, r3, r4 = exchange(*sent)
    th, tl, ubh, ubl = call(
        prepare_kernel,
        pair(len(inside) * leaf, leaf)
        + pair(leaves, 2 * rank, leaf),
        (near_list, points, basis, transfer, device),
        scalars=1,
        scratch=[(3, count, LANE)],
    )
    (term,) = call(term_kernel, [shape(probes // 2 + EXTRA, LANE)], (own, r1, r2, r3))
    gathered = spread_groups(term)
    klh, kll = call(
        skeleton_kernel,
        pair(subs * span, span),
        (far_leaf_list, own, r1, r2, r3),
        scalars=1,
        scratch=[(subs, 3, span, LANE)],
    )
    hh, hl = call(
        border_kernel,
        pair(len(across) * leaf, leaf),
        (near_list, r1, r4, points),
        scalars=1,
        scratch=[(EXTRA, 2 * half), (3, 2 * half, LANE)],
    )
    (inner,) = call(inner_kernel, [shape(probes, count)], (rhs, th, tl))
    (part,) = call(
        outer_kernel,
        [shape(probes, count)],
        (inner, own, r1, r2, r3, r4, hh, hl, klh, kll, ubh, ubl),
    )
    image, kgh, kgl, *sent = call(
        middle_kernel,
        [shape(probes, count)] + pair(rank, groups * rank) + messages(probes),
        (part, gathered, ubh, ubl),
        scratch=[(EXTRA, groups * rank), (3, LANE, LANE)],
    )
    own = sent[1]
    r1, r2, r3, r4 = exchange(*sent)
    dense = groups * rank <= DENSE
    if dense:
        kgh, kgl = call(
            groups_kernel,
            pair(groups * rank, groups * rank),
            (gathered,),
            scratch=[(EXTRA, groups * rank), (3, groups * rank, LANE)],
        )
    (inner,) = call(inner_kernel, [shape(probes, count)], (image, th, tl))
    part, message = call(
        local_kernel,
        [
            shape(probes, count),
            shape(groups * subs, probes // 2 // subs + SHARES, LANE),
        ],
        (rhs, image, inner, own, r1, r2, r3, r4, hh, hl, klh, kll, ubh, ubl),
    )
    gathered = lax.all_to_all(message, ("leaf", "sub"), 0, 0)
    outs = [shape(probes, count), shape(probes, count)]
    if dense:
        return call(final_kernel, outs, (part, gathered, kgh, kgl, ubh, ubl, rhs, image))
    second, share = call(
        last_kernel,
        [shape(probes, count), shape(probes, LANE)],
        (part, gathered, kgh, kgl, ubh, ubl),
    )
    share = lax.psum(share, "leaf")
    return call(update_kernel, outs, (gathered, share, rhs, image, second))


def solution(mesh):
    return jax.shard_map(
        shards,
        mesh=mesh,
        in_specs=(
            P(None, ("leaf", "sub")),
            P(None, ("leaf", "sub")),
            P(("leaf", "sub"), None),
            P(("leaf", "sub"), None),
            P("leaf", None),
            P(("leaf", "sub"), None, None),
            P(None, ("leaf", "sub")),
            P(("leaf", "sub"), None, None),
            P(("leaf", "sub"), None, None),
            P(None, "leaf"),
        ),
        out_specs=(P(None, ("leaf", "sub")), P(None, ("leaf", "sub"))),
        check_vma=False,
    )
```

time: 59.9 us -> 55 us (0.918)
  waiting for transfers between devices: 17.7 us -> 13.7 us
  starting transfers between devices: 23.2 us -> 21.2 us
  local copies, waits for them, and re-layouts: 0.01 us -> 0.7 us
    ppermute x15 -> x10, waiting for transfers between devices: 17.6 us -> 6.62 us  [swap(): lax.ppermute(x, axis, [(i, i ^ m) for i in range(lax.axis_size(axis))])]
    all_to_all x0 -> x1, waiting for transfers between devices: none -> 7.08 us  [shards(): gathered = lax.all_to_all(message, ('leaf', 'sub'), 0, 0)]
    ppermute x15 -> x10, starting transfers between devices: 21.9 us -> 15.4 us  [swap(): lax.ppermute(x, axis, [(i, i ^ m) for i in range(lax.axis_size(axis))])]
    all_to_all x0 -> x1, starting transfers between devices: none -> 4.55 us  [shards(): gathered = lax.all_to_all(message, ('leaf', 'sub'), 0, 0)]
    unnamed x4 -> x8, local copies, waits for them, and re-layouts: 0.01 us -> 0.69 us
    pallas_call x9 -> x12, Pallas kernels: 18 us -> 18.3 us  [call(): pl.pallas_call(kernel, out_shape=tuple(outs), in_specs=smem(scalars) + vm...]
  transfers between devices with their start and end apart: 17 -> 13, of which waited for: 10 -> 5; matrix products, arithmetic and copies ran while one was open for 0% -> 0% of each run, Pallas kernels for 21% -> 23%
where the time goes in v3:
time: 55 us; the launch traced here: 54.7 us
  starting transfers between devices  21.2 us (39%)
  Pallas kernels  18.3 us (33%)
  waiting for transfers between devices  13.7 us (25%)
  between operations  0.8 us (1%)
  local copies, waits for them, and re-layouts  0.7 us (1%)
    pallas_call x12, Pallas kernels, call(): pl.pallas_call(kernel, out_shape=tuple(outs), in_specs=smem(scalars) + vm...  18.3 us
    ppermute x10, starting transfers between devices, swap(): lax.ppermute(x, axis, [(i, i ^ m) for i in range(lax.axis_size(axis))])  15.4 us
    all_to_all x1, waiting for transfers between devices, shards(): gathered = lax.all_to_all(message, ('leaf', 'sub'), 0, 0)  7.08 us
    ppermute x10, waiting for transfers between devices, swap(): lax.ppermute(x, axis, [(i, i ^ m) for i in range(lax.axis_size(axis))])  6.62 us
    all_to_all x1, starting transfers between devices, shards(): gathered = lax.all_to_all(message, ('leaf', 'sub'), 0, 0)  4.55 us
    ppermute x2, starting transfers between devices, exchange(): return (*received, lax.ppermute(m4, ('leaf', 'sub'), across))  1.32 us
  transfers between devices with their start and end apart: 13, of which 5 were waited for; matrix products, arithmetic and copies ran while one was open for 0% of the time, Pallas kernels for 23%

profile of v3, /device:TPU:0, one launch (start us, length us, event | category | flops | bytes accessed | tf_op | source)
XLA Modules:
  0.0 54.7 jit_solution(8772136532870403746)
XLA Ops:
  0.6 1.8 %shard_map.113 = (f32[40,896]{1,0:T(8,128)S(1)}, f32[40,384]{1,0:T(8,128)S(1)}, f32[40,512]{1,0:T(8,128)S(1)}, f32[32,1024]{1,0:T(8,128)S(1)}, f32[8,1024]{1,0:T...) custom-call(s32[1,14]{1,0:T(1,128)} %list_ref.1, f32[32,1024]{1,0:T(8,128)} %vec_ref.1, ...), custom_call_target="tpu_custom_call" | custom-call | bytes 1000000 | tf_op jit(solution)/shard_map/pallas_call | solution.py:544
  2.5 0.6 %collective-permute-start = (f32[40,896]{1,0:T(8,128)S(1)}, f32[40,896]{1,0:T(8,128)S(1)}, u32[]{:S(2)}, u32[]{:S(2)}) collective-permute-start(f32[40,896]{1,0:T(8,128)S(1)} %get-tuple-element.34), channel_id=1, source_target_pairs={{0,1},{1,0},{2,3},{3,2},{4,5},{5,4},{6,7},{7,6},{8,9},{9,8},{10,11... | collective-permute-start | bytes 430088 | tf_op jit(solution)/shard_map/ppermute | solution.py:558
  3.1 2.6 %collective-permute-start.1 = (f32[40,384]{1,0:T(8,128)S(1)}, f32[40,384]{1,0:T(8,128)S(1)}, u32[]{:S(2)}, u32[]{:S(2)}) collective-permute-start(f32[40,384]{1,0:T(8,128)S(1)} %get-tuple-element.33.own), channel_id=1, source_target_pairs={{0,2},{1,3},{2,0},{3,1},{4,6},{5,7},{6,4},{7,5},{8,10},{9,11},{10,... | collective-permute-start | bytes 184328 | tf_op jit(solution)/shard_map/ppermute | solution.py:558
  5.6 0.0 collective-permute-start.2
  5.7 0.7 %collective-permute-start.3 = (f32[40,512]{1,0:T(8,128)S(1)}, f32[40,512]{1,0:T(8,128)S(1)}, u32[]{:S(2)}, u32[]{:S(2)}) collective-permute-start(f32[40,512]{1,0:T(8,128)S(1)} %get-tuple-element.35), channel_id=1, source_target_pairs={{1,2},{3,4},{5,6},{7,8},{9,10},{11,12},{13,14},{15,16},{17,18},{19... | collective-permute-start | bytes 245768 | tf_op jit(solution)/shard_map/ppermute | solution.py:566
  6.3 0.0 copy-start
  6.3 0.7 %copy-done = s32[4,5]{1,0:T(4,128)S(1)} copy-done((s32[4,5]{1,0:T(4,128)S(1)}, s32[4,5]{1,0:T(4,128)}, u32[]{:S(2)}) %copy-start) | copy-done | bytes 104
  7.0 4.2 %shard_map.114 = (bf16[2304,256]{1,0:T(8,128)(2,1)S(1)}, bf16[2304,256]{1,0:T(8,128)(2,1)S(1)}, bf16[4,128,256]{2,1,0:T(8,128)(2,1)S(1)}, bf16[4,128,256]{2,1,0:T(8,128)(2,1)S(1)}) custom-call(s32[4,5]{1,0:T(4,128)S(1)} %copy-done, f32[8,1024]{1,0:T(8,128)S(1)} %get-tuple-element.27.points_ref, f32[4,64,256]{2,1,0:T(8,128)S(1)} %get-tuple-element.28.basis_ref, ...), custom_call_target="tpu_custom_call" | custom-call | bytes 1000000 | tf_op jit(solution)/shard_map/pallas_call | solution.py:544
  11.3 0.0 copy-start.1
  11.3 0.9 %shard_map.115.inner_ref = f32[32,1024]{1,0:T(8,128)S(1)} custom-call(f32[32,1024]{1,0:T(8,128)S(1)} %get-tuple-element.26.vec_ref.rhs_ref, bf16[2304,256]{1,0:T(8,128)(2,1)S(1)} %get-tuple-element.31.th_ref, bf16[2304,256]{1,0:T(8,128)(2,1)S(1)} %get-tuple-element.32.tl_ref), custom_call_target="tpu_custom_call" | custom-call | bytes 1000000 | tf_op jit(solution)/shard_map/pallas_call | solution.py:544
  12.2 0.0 collective-permute-done.2.r3
  12.2 0.1 shard_map.119
  12.3 5.4 %collective-permute-start.4 = (f32[1,24,128]{2,1,0:T(8,128)S(1)}, f32[1,24,128]{2,1,0:T(8,128)S(1)}, u32[]{:S(2)}, u32[]{:S(2)}) collective-permute-start(f32[1,24,128]{2,1,0:T(8,128)S(1)} %bitcast.4), channel_id=1, source_target_pairs={{0,8},{4,12},{8,0},{12,4},{16,24},{20,28},{24,16},{28,20},{1,9},{5... | collective-permute-start | bytes 36872 | tf_op jit(solution)/shard_map/ppermute | solution.py:558
  17.6 2.6 %collective-permute-start.5 = (f32[1,24,128]{2,1,0:T(8,128)S(1)}, f32[1,24,128]{2,1,0:T(8,128)S(1)}, u32[]{:S(2)}, u32[]{:S(2)}) collective-permute-start(f32[1,24,128]{2,1,0:T(8,128)S(1)} %bitcast.5), channel_id=1, source_target_pairs={{0,16},{4,20},{8,24},{12,28},{16,0},{20,4},{24,8},{28,12},{1,17},{... | collective-permute-start | bytes 36872 | tf_op jit(solution)/shard_map/ppermute | solution.py:558
  20.2 2.7 %shard_map.116 = (bf16[1536,256]{1,0:T(8,128)(2,1)S(1)}, bf16[1536,256]{1,0:T(8,128)(2,1)S(1)}) custom-call(s32[4,5]{1,0:T(4,128)S(1)} %copy-done, f32[40,896]{1,0:T(8,128)S(1)} %collective-permute-done.r1, f32[40,512]{1,0:T(8,128)S(1)} %collective-permute-done.3.r4, f32[8,1024]{1,0:T(8,128)S(1)} %get-tuple-element.27.points_ref), custom_call_target="tpu_custom_call" | custom-call | bytes 1000000 | tf_op jit(solution)/shard_map/pallas_call | solution.py:544
  23.0 1.8 %shard_map.117 = (bf16[1024,256]{1,0:T(8,128)(2,1)S(1)}, bf16[1024,256]{1,0:T(8,128)(2,1)S(1)}) custom-call(s32[4,8]{1,0:T(4,128)S(1)} %copy-done.1, f32[40,384]{1,0:T(8,128)S(1)} %get-tuple-element.33.own, f32[40,896]{1,0:T(8,128)S(1)} %collective-permute-done.r1, f32[40,384]{1,0:T(8,128)S(1)} %collective-permute-done.1.r2, ...), custom_call_target="tpu_custom_call" | custom-call | bytes 1000000 | tf_op jit(solution)/shard_map/pallas_call | solution.py:544
  24.7 0.7 %shard_map.118.part_ref = f32[32,1024]{1,0:T(8,128)S(1)} custom-call(f32[32,1024]{1,0:T(8,128)S(1)} %shard_map.115.inner_ref, f32[40,384]{1,0:T(8,128)S(1)} %get-tuple-element.33.own, f32[40,896]{1,0:T(8,128)S(1)} %collective-permute-done.r1, f32[40,384]{1,0:T(8,128)S(1)} %collective-permute-done.1.r2, f32[40,384]{1,0:T(8,128)S(1)} %collective-permute-done.2.r3, ...), custom_call_target="tpu_custom_call" | custom-call | bytes 1000000 | tf_op jit(solution)/shard_map/pallas_call | solution.py:544
  25.5 0.2 collective-permute-done.6
  25.7 0.7 %collective-permute-start.7 = (f32[4,24,128]{2,1,0:T(8,128)S(1)}, f32[4,24,128]{2,1,0:T(8,128)S(1)}, u32[]{:S(2)}, u32[]{:S(2)}) collective-permute-start(f32[4,24,128]{2,1,0:T(8,128)S(1)} %pad_maximum_fusion), channel_id=1, source_target_pairs={{0,4},{4,0},{8,12},{12,8},{16,20},{20,16},{24,28},{28,24},{1,5},{5... | collective-permute-start | bytes 147464 | tf_op jit(solution)/shard_map/ppermute | solution.py:558
  26.5 3.3 %collective-permute-done.7 = f32[4,24,128]{2,1,0:T(8,128)S(1)} collective-permute-done((f32[4,24,128]{2,1,0:T(8,128)S(1)}, f32[4,24,128]{2,1,0:T(8,128)S(1)}, u32[]{:S(2)}, u32[]{:S(2)}) %collective-permute-start.7) | collective-permute-done | bytes 49184 | tf_op jit(solution)/shard_map/ppermute | solution.py:558
  29.8 1.0 %shard_map.120 = (f32[32,1024]{1,0:T(8,128)S(1)}, bf16[64,512]{1,0:T(8,128)(2,1)}, bf16[64,512]{1,0:T(8,128)(2,1)}, f32[32,896]{1,0:T(8,128)S(1)}, f32[32,384]{1,0:T(8,128)S(1)}, /*index=5*/f32[32,512]{1,0:T(8,128)S(1)}) custom-call(f32[32,1024]{1,0:T(8,128)S(1)} %shard_map.118.part_ref, f32[8,24,128]{2,1,0:T(8,128)S(1)} %constant_dynamic-update-slice_fusion.group_ref, ...), custom_call_target="tpu_custom_call" | custom-call | bytes 1000000 | tf_op jit(solution)/shard_map/pallas_call | solution.py:544
  30.8 0.1 collective-permute-start.8
  30.9 0.7 %collective-permute-start.11 = (f32[32,512]{1,0:T(8,128)S(1)}, f32[32,512]{1,0:T(8,128)S(1)}, u32[]{:S(2)}, u32[]{:S(2)}) collective-permute-start(f32[32,512]{1,0:T(8,128)S(1)} %get-tuple-element.45), channel_id=1, source_target_pairs={{1,2},{3,4},{5,6},{7,8},{9,10},{11,12},{13,14},{15,16},{17,18},{19... | collective-permute-start | bytes 196616 | tf_op jit(solution)/shard_map/ppermute | solution.py:566
  31.6 3.4 %collective-permute-start.9 = (f32[32,384]{1,0:T(8,128)S(1)}, f32[32,384]{1,0:T(8,128)S(1)}, u32[]{:S(2)}, u32[]{:S(2)}) collective-permute-start(f32[32,384]{1,0:T(8,128)S(1)} %get-tuple-element.43.own), channel_id=1, source_target_pairs={{0,2},{1,3},{2,0},{3,1},{4,6},{5,7},{6,4},{7,5},{8,10},{9,11},{10,... | collective-permute-start | bytes 147464 | tf_op jit(solution)/shard_map/ppermute | solution.py:558
  35.0 0.9 %shard_map.121.inner_ref = f32[32,1024]{1,0:T(8,128)S(1)} custom-call(f32[32,1024]{1,0:T(8,128)S(1)} %get-tuple-element.42.vec_ref.first_ref, bf16[2304,256]{1,0:T(8,128)(2,1)S(1)} %get-tuple-element.31.th_ref, bf16[2304,256]{1,0:T(8,128)(2,1)S(1)} %get-tuple-element.32.tl_ref), custom_call_target="tpu_custom_call" | custom-call | bytes 1000000 | tf_op jit(solution)/shard_map/pallas_call | solution.py:544
  35.9 1.9 %collective-permute-done.9.r2 = f32[32,384]{1,0:T(8,128)S(1)} collective-permute-done((f32[32,384]{1,0:T(8,128)S(1)}, f32[32,384]{1,0:T(8,128)S(1)}, u32[]{:S(2)}, u32[]{:S(2)}) %collective-permute-start.9) | collective-permute-done | bytes 49184 | tf_op jit(solution)/shard_map/ppermute | solution.py:558
  37.8 1.1 %collective-permute-done.10.r3 = f32[32,384]{1,0:T(8,128)S(1)} collective-permute-done((f32[32,384]{1,0:T(8,128)S(1)}, f32[32,384]{1,0:T(8,128)S(1)}, u32[]{:S(2)}, u32[]{:S(2)}) %collective-permute-start.10) | collective-permute-done | bytes 49184 | tf_op jit(solution)/shard_map/ppermute | solution.py:558
  38.9 1.5 %shard_map.122 = (f32[32,1024]{1,0:T(8,128)S(1)}, f32[32,8,128]{2,1,0:T(8,128)}) custom-call(f32[32,1024]{1,0:T(8,128)S(1)} %get-tuple-element.26.vec_ref.rhs_ref, f32[32,1024]{1,0:T(8,128)S(1)} %get-tuple-element.42.vec_ref.first_ref, f32[32,1024]{1,0:T(8,128)S(1)} %shard_map.121.inner_ref, f32[32,384]{1,0:T(8,128)S(1)} %get-tuple-element.43.own, ...), custom_call_target="tpu_custom_call" | custom-call | bytes 1000000 | tf_op jit(solution)/shard_map/pallas_call | solution.py:544
  40.4 4.6 %all-to-all-start = ((f32[32,8,128]{2,1,0:T(8,128)}), f32[32,8,128]{2,1,0:T(8,128)S(1)}, u32[]{:S(2)}, u32[]{:S(2)}) async-start(f32[32,8,128]{2,1,0:T(8,128)} %get-tuple-element.47), calls=%async_computation | async-start | bytes 262144 | tf_op jit(solution)/shard_map/all_to_all | solution.py:679
  45.0 1.1 %shard_map.123 = (bf16[512,512]{1,0:T(8,128)(2,1)S(1)}, bf16[512,512]{1,0:T(8,128)(2,1)S(1)}) custom-call(f32[8,24,128]{2,1,0:T(8,128)S(1)} %constant_dynamic-update-slice_fusion.group_ref), custom_call_target="tpu_custom_call" | custom-call | bytes 1000000 | tf_op jit(solution)/shard_map/pallas_call | solution.py:544
  46.1 7.1 %all-to-all-done.group_ref = f32[32,8,128]{2,1,0:T(8,128)S(1)} async-done(((f32[32,8,128]{2,1,0:T(8,128)}), f32[32,8,128]{2,1,0:T(8,128)S(1)}, u32[]{:S(2)}, u32[]{:S(2)}) %all-to-all-start) | async-done | bytes 131104 | tf_op jit(solution)/shard_map/all_to_all | solution.py:679
  53.2 1.5 %shard_map.124 = (f32[32,1024]{1,0:T(8,128)}, f32[32,1024]{1,0:T(8,128)}) custom-call(f32[32,1024]{1,0:T(8,128)S(1)} %get-tuple-element.46.part_ref, f32[32,8,128]{2,1,0:T(8,128)S(1)} %all-to-all-done.group_ref, bf16[512,512]{1,0:T(8,128)(2,1)S(1)} %get-tuple-element.48.kah_ref, bf16[512,512]{1,0:T(8,128)(2,1)S(1)} %get-tuple-element.49.kal_ref, ...), custom_call_target="tpu_custom_call" | custom-call | bytes 1000000 | tf_op jit(solution)/shard_map/pallas_call | solution.py:544
  (16 shorter events, 0.0 us)
Async XLA Ops:
  2.5 9.7 %collective-permute-start = (f32[40,896]{1,0:T(8,128)S(1)}, f32[40,896]{1,0:T(8,128)S(1)}, u32[]{:S(2)}, u32[]{:S(2)}) collective-permute-start(f32[40,896]{1,0:T(8,128)S(1)} %get-tuple-element.34), channel_id=1, source_target_pairs={{0,1},{1,0},{2,3},{3,2},{4,5},{5,4},{6,7},{7,6},{8,9},{9,8},{10,11... | collective-permute-start | bytes 430088 | tf_op jit(solution)/shard_map/ppermute | solution.py:558
  3.1 9.1 %collective-permute-start.1 = (f32[40,384]{1,0:T(8,128)S(1)}, f32[40,384]{1,0:T(8,128)S(1)}, u32[]{:S(2)}, u32[]{:S(2)}) collective-permute-start(f32[40,384]{1,0:T(8,128)S(1)} %get-tuple-element.33.own), channel_id=1, source_target_pairs={{0,2},{1,3},{2,0},{3,1},{4,6},{5,7},{6,4},{7,5},{8,10},{9,11},{10,... | collective-permute-start | bytes 184328 | tf_op jit(solution)/shard_map/ppermute | solution.py:558
  5.6 6.5 %collective-permute-start.2 = (f32[40,384]{1,0:T(8,128)S(1)}, f32[40,384]{1,0:T(8,128)S(1)}, u32[]{:S(2)}, u32[]{:S(2)}) collective-permute-start(f32[40,384]{1,0:T(8,128)S(1)} %get-tuple-element.33.own), channel_id=1, source_target_pairs={{0,3},{1,2},{2,1},{3,0},{4,7},{5,6},{6,5},{7,4},{8,11},{9,10},{10,... | collective-permute-start | bytes 184328 | tf_op jit(solution)/shard_map/ppermute | solution.py:558
  5.7 14.5 %collective-permute-start.3 = (f32[40,512]{1,0:T(8,128)S(1)}, f32[40,512]{1,0:T(8,128)S(1)}, u32[]{:S(2)}, u32[]{:S(2)}) collective-permute-start(f32[40,512]{1,0:T(8,128)S(1)} %get-tuple-element.35), channel_id=1, source_target_pairs={{1,2},{3,4},{5,6},{7,8},{9,10},{11,12},{13,14},{15,16},{17,18},{19... | collective-permute-start | bytes 245768 | tf_op jit(solution)/shard_map/ppermute | solution.py:566
  6.3 0.7 %copy-start = (s32[4,5]{1,0:T(4,128)S(1)}, s32[4,5]{1,0:T(4,128)}, u32[]{:S(2)}) copy-start(s32[4,5]{1,0:T(4,128)} %near_ref.3) | copy-start | bytes 244
  11.3 11.7 %copy-start.1 = (s32[4,8]{1,0:T(4,128)S(1)}, s32[4,8]{1,0:T(4,128)}, u32[]{:S(2)}) copy-start(s32[4,8]{1,0:T(4,128)} %far_ref.1) | copy-start | bytes 388
  12.3 13.2 %collective-permute-start.4 = (f32[1,24,128]{2,1,0:T(8,128)S(1)}, f32[1,24,128]{2,1,0:T(8,128)S(1)}, u32[]{:S(2)}, u32[]{:S(2)}) collective-permute-start(f32[1,24,128]{2,1,0:T(8,128)S(1)} %bitcast.4), channel_id=1, source_target_pairs={{0,8},{4,12},{8,0},{12,4},{16,24},{20,28},{24,16},{28,20},{1,9},{5... | collective-permute-start | bytes 36872 | tf_op jit(solution)/shard_map/ppermute | solution.py:558
  17.6 7.9 %collective-permute-start.5 = (f32[1,24,128]{2,1,0:T(8,128)S(1)}, f32[1,24,128]{2,1,0:T(8,128)S(1)}, u32[]{:S(2)}, u32[]{:S(2)}) collective-permute-start(f32[1,24,128]{2,1,0:T(8,128)S(1)} %bitcast.5), channel_id=1, source_target_pairs={{0,16},{4,20},{8,24},{12,28},{16,0},{20,4},{24,8},{28,12},{1,17},{... | collective-permute-start | bytes 36872 | tf_op jit(solution)/shard_map/ppermute | solution.py:558
  20.2 5.5 %collective-permute-start.6 = (f32[1,24,128]{2,1,0:T(8,128)S(1)}, f32[1,24,128]{2,1,0:T(8,128)S(1)}, u32[]{:S(2)}, u32[]{:S(2)}) collective-permute-start(f32[1,24,128]{2,1,0:T(8,128)S(1)} %bitcast.6), channel_id=1, source_target_pairs={{0,24},{4,28},{8,16},{12,20},{16,8},{20,12},{24,0},{28,4},{1,25},{... | collective-permute-start | bytes 36872 | tf_op jit(solution)/shard_map/ppermute | solution.py:558
  25.7 4.1 %collective-permute-start.7 = (f32[4,24,128]{2,1,0:T(8,128)S(1)}, f32[4,24,128]{2,1,0:T(8,128)S(1)}, u32[]{:S(2)}, u32[]{:S(2)}) collective-permute-start(f32[4,24,128]{2,1,0:T(8,128)S(1)} %pad_maximum_fusion), channel_id=1, source_target_pairs={{0,4},{4,0},{8,12},{12,8},{16,20},{20,16},{24,28},{28,24},{1,5},{5... | collective-permute-start | bytes 147464 | tf_op jit(solution)/shard_map/ppermute | solution.py:558
  30.8 8.1 %collective-permute-start.8 = (f32[32,896]{1,0:T(8,128)S(1)}, f32[32,896]{1,0:T(8,128)S(1)}, u32[]{:S(2)}, u32[]{:S(2)}) collective-permute-start(f32[32,896]{1,0:T(8,128)S(1)} %get-tuple-element.44), channel_id=1, source_target_pairs={{0,1},{1,0},{2,3},{3,2},{4,5},{5,4},{6,7},{7,6},{8,9},{9,8},{10,11... | collective-permute-start | bytes 344072 | tf_op jit(solution)/shard_map/ppermute | solution.py:558
  30.9 8.0 %collective-permute-start.11 = (f32[32,512]{1,0:T(8,128)S(1)}, f32[32,512]{1,0:T(8,128)S(1)}, u32[]{:S(2)}, u32[]{:S(2)}) collective-permute-start(f32[32,512]{1,0:T(8,128)S(1)} %get-tuple-element.45), channel_id=1, source_target_pairs={{1,2},{3,4},{5,6},{7,8},{9,10},{11,12},{13,14},{15,16},{17,18},{19... | collective-permute-start | bytes 196616 | tf_op jit(solution)/shard_map/ppermute | solution.py:566
  31.6 6.2 %collective-permute-start.9 = (f32[32,384]{1,0:T(8,128)S(1)}, f32[32,384]{1,0:T(8,128)S(1)}, u32[]{:S(2)}, u32[]{:S(2)}) collective-permute-start(f32[32,384]{1,0:T(8,128)S(1)} %get-tuple-element.43.own), channel_id=1, source_target_pairs={{0,2},{1,3},{2,0},{3,1},{4,6},{5,7},{6,4},{7,5},{8,10},{9,11},{10,... | collective-permute-start | bytes 147464 | tf_op jit(solution)/shard_map/ppermute | solution.py:558
  35.0 3.9 %collective-permute-start.10 = (f32[32,384]{1,0:T(8,128)S(1)}, f32[32,384]{1,0:T(8,128)S(1)}, u32[]{:S(2)}, u32[]{:S(2)}) collective-permute-start(f32[32,384]{1,0:T(8,128)S(1)} %get-tuple-element.43.own), channel_id=1, source_target_pairs={{0,3},{1,2},{2,1},{3,0},{4,7},{5,6},{6,5},{7,4},{8,11},{9,10},{10,... | collective-permute-start | bytes 147464 | tf_op jit(solution)/shard_map/ppermute | solution.py:558
  40.4 12.8 %all-to-all-start = ((f32[32,8,128]{2,1,0:T(8,128)}), f32[32,8,128]{2,1,0:T(8,128)S(1)}, u32[]{:S(2)}, u32[]{:S(2)}) async-start(f32[32,8,128]{2,1,0:T(8,128)} %get-tuple-element.47), calls=%async_computation | async-start | bytes 262144 | tf_op jit(solution)/shard_map/all_to_all | solution.py:679

commit v4 on v3

--- a/solution.py
+++ b/solution.py
@@ -17,6 +17,7 @@
 LANE = 128
 EXTRA = 8
 CHUNK = 32
+UNROLL = 1024
 SHARES = 4
 GRANT = 16 * 2**20
 DENSE = 1024
@@ -55,11 +56,16 @@
     return poly * jnp.exp2((-ROOT_FIVE * LOG2_E) * distance)
 
 
-def named(list_ref, row, index):
-    hit = list_ref[row, 0] == index
-    for column in range(1, list_ref.shape[1]):
-        hit = jnp.logical_or(hit, list_ref[row, column] == index)
-    return jnp.where(hit, 1.0, 0.0).astype(F32)
+def slot_columns(list_ref):
+    leaves, slots = list_ref.shape
+    block = jnp.full((EXTRA, LANE), -2, jnp.int32)
+    tall = jnp.concatenate([list_ref[...], block[leaves:, 0:slots]], axis=0)
+    wide = jnp.concatenate([tall, block[:, 0 : LANE - slots]], axis=1)
+    return wide.T[0 : -(-slots // EXTRA) * EXTRA]
+
+
+def named(columns, index):
+    return jnp.max(jnp.where(columns == index, 1.0, 0.0).astype(F32), axis=0, keepdims=True)
 
 
 def padded_lanes(x, lanes):
@@ -74,33 +80,32 @@
     )
 
 
-def write_messages(vec, coefs, term, outs, half, rows):
-    m1, own, m4 = outs
-    count = vec.shape[1]
+def ends(vec, half):
     even = lax.axis_index("sub") % 2 == 0
     low = vec[:, :half]
-    high = vec[:, count - half :]
-    span = coefs.shape[1]
-    base = own.shape[1]
-    for ref in (m1, own):
-        ref[rows, 0:span] = coefs
-        ref[rows, span:base] = term
-    m1[rows, base : base + half] = jnp.where(even, high, low)
-    m4[rows, :] = jnp.where(even, low, high)
-
-
-def halos(r1, r4, rows, base):
+    high = vec[:, vec.shape[1] - half :]
+    return jnp.where(even, high, low), jnp.where(even, low, high)
+
+
+def write_row(ref, rows, *pieces):
+    at = 0
+    for piece in pieces:
+        ref[rows, at : at + piece.shape[1]] = piece
+        at = at + piece.shape[1]
+
+
+def halos(r1, from_b, rows, base):
     odd = lax.axis_index("sub") % 2 == 1
     from_a = r1[rows, base:]
-    from_b = r4[rows, :]
     return jnp.where(odd, from_a, from_b), jnp.where(odd, from_b, from_a)
 
 
 def first_kernel(
     list_ref, vec_ref, coords_ref, skel_ref, gskel_ref, basis_ref, transfer_ref, device_ref,
+    near_ref, far_ref,
     m1_ref, own_ref, m4_ref, rhs_ref, points_ref, basis_out, transfer_out, device_out,
+    near_out, far_out,
 ):
-    outs = (m1_ref, own_ref, m4_ref)
     leaves, _, leaf = basis_ref.shape
     probes = vec_ref.shape[0]
     half = REACH * leaf
@@ -110,25 +115,29 @@
         axis=1,
     )
     term = padded_lanes(dot(dot(coefs, transfer_ref[...]), device_ref[...]), LANE)
-    write_messages(vec, coefs, term, outs, half, slice(0, probes))
     relative = lax.axis_index("leaf") ^ lax.broadcasted_iota(jnp.int32, (1, LANE), 1)
     listed = jnp.zeros((1, LANE), F32)
     for column in range(list_ref.shape[1]):
         listed = jnp.where(relative == list_ref[0, column], 1.0, listed)
     group_rows = jnp.concatenate([padded_lanes(gskel_ref[...], LANE), listed], axis=0)
-    write_messages(
-        padded_rows(coords_ref[...], EXTRA),
-        padded_rows(skel_ref[...], EXTRA),
-        padded_rows(group_rows, EXTRA),
-        outs,
-        half,
-        slice(probes, probes + EXTRA),
-    )
+    points = padded_rows(coords_ref[...], EXTRA)
+    skel = padded_rows(skel_ref[...], EXTRA)
+    group_rows = padded_rows(group_rows, EXTRA)
+    for rows, block in (
+        (slice(0, probes), (vec, coefs, term)),
+        (slice(probes, probes + EXTRA), (points, skel, group_rows)),
+    ):
+        part_a, part_b = ends(block[0], half)
+        write_row(m1_ref, rows, *block[1:], part_a)
+        write_row(own_ref, rows, *block[1:])
+        write_row(m4_ref, rows, part_b)
     rhs_ref[...] = vec
-    points_ref[...] = padded_rows(coords_ref[...], EXTRA)
+    points_ref[...] = points
     basis_out[...] = basis_ref[...]
     transfer_out[...] = transfer_ref[...]
     device_out[...] = device_ref[...]
+    near_out[...] = near_ref[...]
+    far_out[...] = far_ref[...]
 
 
 def spread_columns(points, wide_ref):
@@ -151,13 +160,13 @@
                 points_ref[top_row + axis : top_row + axis + 1, lane + at : lane + at + LANE]
                 for axis in range(3)
             ]
-            factor = weight[:, at : at + LANE] if weight.ndim else weight
+            factor = weight if weight.shape[1] == LANE else weight[:, at : at + LANE]
             top, rest = split(matern(rows, cols, factor))
             high_ref[pl.ds(target, CHUNK), at : at + LANE] = top
             low_ref[pl.ds(target, CHUNK), at : at + LANE] = rest
         return 0
 
-    lax.fori_loop(0, size // CHUNK, body, 0, unroll=2)
+    lax.fori_loop(0, size // CHUNK, body, 0, unroll=min(size // CHUNK, UNROLL // width))
 
 
 def window_tiles(leaves):
@@ -173,17 +182,23 @@
 
 
 def prepare_kernel(
-    near_ref, points_ref, basis_ref, transfer_ref, device_ref,
-    th_ref, tl_ref, ubh_ref, ubl_ref, wide_ref,
+    near_ref, points_ref, th_ref, tl_ref, wide_ref,
 ):
-    leaves, rank, leaf = basis_ref.shape
+    leaves = near_ref.shape[0]
+    leaf = points_ref.shape[1] // leaves
     first = (lax.axis_index("leaf") * lax.axis_size("sub") + lax.axis_index("sub")) * leaves
     spread_columns(points_ref[...], wide_ref)
+    slots = slot_columns(near_ref)
     for at, (i, j) in enumerate(window_tiles(leaves)[0]):
+        listed = jnp.broadcast_to(slots[:, i : i + 1], (slots.shape[0], LANE))
         fill_tile(
-            wide_ref, j * leaf, points_ref, 0, i * leaf, leaf, named(near_ref, i, first + j),
+            wide_ref, j * leaf, points_ref, 0, i * leaf, leaf, named(listed, first + j),
             (th_ref, tl_ref), at * leaf, leaf,
         )
+
+
+def bases_kernel(basis_ref, transfer_ref, device_ref, ubh_ref, ubl_ref):
+    leaves, rank, _ = basis_ref.shape
     chain = dot(transfer_ref[...], device_ref[...])
     for i in range(leaves):
         basis = basis_ref[i]
@@ -267,17 +282,18 @@
     sub = lax.axis_index("sub")
     group_first = lax.axis_index("leaf") * lax.axis_size("sub") * leaves
     messages = (own, r1, r2, r3)
-    lane_leaf = lax.broadcasted_iota(jnp.int32, (1, span), 1) // rank
+    slots = slot_columns(far_ref)
+    listed = jnp.concatenate(
+        [jnp.broadcast_to(slots[:, i : i + 1], (slots.shape[0], rank)) for i in range(leaves)],
+        axis=1,
+    )
     for m, message in enumerate(messages):
         spread_columns(message[probes : probes + EXTRA, 0:span], wide_ref.at[m])
     for m in range(len(messages)):
         for j in range(leaves):
             index = group_first + (sub ^ m) * leaves + j
-            mask = jnp.zeros((1, span), F32)
-            for i in range(leaves):
-                mask = jnp.where(lane_leaf == i, named(far_ref, i, index), mask)
             fill_tile(
-                wide_ref.at[m], j * rank, own, probes, 0, span, mask,
+                wide_ref.at[m], j * rank, own, probes, 0, span, named(listed, index),
                 (klh_ref, kll_ref), m * span + j * rank, rank,
             )
 
@@ -289,24 +305,28 @@
     half = REACH * leaf
     probes = r4.shape[0] - EXTRA
     first = (lax.axis_index("leaf") * lax.axis_size("sub") + lax.axis_index("sub")) * leaves
-    low, high = halos(r1, r4, slice(probes, probes + EXTRA), r1.shape[1] - half)
+    rows = slice(probes, probes + EXTRA)
+    low, high = halos(r1, r4[rows, :], rows, r1.shape[1] - half)
     ends_ref[:, 0:half] = low
     ends_ref[:, half:] = high
     spread_columns(ends_ref[...], wide_ref)
+    slots = slot_columns(near_ref)
     for at, (i, j) in enumerate(window_tiles(leaves)[1]):
+        listed = jnp.broadcast_to(slots[:, i : i + 1], (slots.shape[0], LANE))
         source = (j + REACH) * leaf if j < 0 else half + (j - leaves) * leaf
         fill_tile(
-            wide_ref, source, points_ref, 0, i * leaf, leaf, named(near_ref, i, first + j),
+            wide_ref, source, points_ref, 0, i * leaf, leaf, named(listed, first + j),
             (hh_ref, hl_ref), at * leaf, leaf,
         )
 
 
 def outer_kernel(
-    inner_ref, own, r1, r2, r3, r4, hh_ref, hl_ref, klh_ref, kll_ref, ubh_ref, ubl_ref, part_ref,
+    inner_ref, own, r1, r2, r3, r4, hh_ref, hl_ref, klh_ref, kll_ref, ubh_ref, ubl_ref,
+    part_ref,
 ):
     span = klh_ref.shape[1]
     rows = slice(0, inner_ref.shape[0])
-    low, high = halos(r1, r4, rows, own.shape[1])
+    low, high = halos(r1, r4[rows, :], rows, own.shape[1])
     local_part(
         inner_ref, low, high, [r[rows, 0:span] for r in (own, r1, r2, r3)],
         (hh_ref, hl_ref, klh_ref, kll_ref), (ubh_ref, ubl_ref), part_ref,
@@ -327,7 +347,7 @@
     rows = slice(0, vec_ref.shape[0])
     rhs = rhs_ref[...]
     vec = vec_ref[...]
-    low, high = halos(r1, r4, rows, base)
+    low, high = halos(r1, r4[...], rows, base)
     blocks = [r[rows, 0:span] for r in (own, r1, r2, r3)]
     near, far = local_part(
         inner_ref, low, high, blocks,
@@ -362,8 +382,6 @@
 
 
 def exchange_rounds(groups):
-    if groups == 8:
-        return [[2, 4, 6], [1]]
     return [[groups >> n] for n in range(1, groups.bit_length())]
 
 
@@ -399,15 +417,13 @@
 
 
 def middle_kernel(
-    part_ref, group_ref, ubh_ref, ubl_ref, image_ref, kgh_ref, kgl_ref, *rest,
+    part_ref, group_ref, ubh_ref, ubl_ref, image_ref, kgh_ref, kgl_ref, m4_ref,
+    points_ref, wide_ref,
 ):
-    outs = rest[:3]
-    points_ref, wide_ref = rest[3:]
     leaves, double, leaf = ubh_ref.shape
     rank = double // 2
     groups = group_ref.shape[0]
-    probes = part_ref.shape[0]
-    half = probes // 2
+    half = part_ref.shape[0] // 2
     points_ref[...] = group_points(group_ref, half, rank)
     spread_columns(group_ref[0, half : half + EXTRA, :], wide_ref)
     fill_tile(
@@ -417,23 +433,32 @@
     held = group_row(group_ref, half, rank, range(groups))
     group_far = product(stacked(held), kgh_ref[...], kgl_ref[...], True)
     group_stack = stacked(group_far)
-    image = []
+    image = jnp.concatenate(
+        [
+            part_ref[:, i * leaf : (i + 1) * leaf]
+            + product(group_stack, ubh_ref[i, rank:, :], ubl_ref[i, rank:, :])
+            for i in range(leaves)
+        ],
+        axis=1,
+    )
+    image_ref[...] = image
+    m4_ref[...] = ends(image, m4_ref.shape[1])[1]
+
+
+def second_kernel(vec_ref, ubh_ref, ubl_ref, m1_ref, own_ref):
+    leaves, double, leaf = ubh_ref.shape
+    rank = double // 2
+    vec = vec_ref[...]
     coefs = []
     term = None
     for i in range(leaves):
-        piece = part_ref[:, i * leaf : (i + 1) * leaf] + product(
-            group_stack, ubh_ref[i, rank:, :], ubl_ref[i, rank:, :]
-        )
-        image.append(piece)
-        both = product(stacked(piece), ubh_ref[i], ubl_ref[i], True)
+        both = product(stacked(leaf_slice(vec, i, leaf)), ubh_ref[i], ubl_ref[i], True)
         coefs.append(both[:, :rank])
         term = both if term is None else term + both
-    image = jnp.concatenate(image, axis=1)
-    image_ref[...] = image
-    write_messages(
-        image, jnp.concatenate(coefs, axis=1), padded_lanes(term[:, rank:], LANE), outs,
-        REACH * leaf, slice(0, probes),
-    )
+    pieces = jnp.concatenate(coefs, axis=1), padded_lanes(term[:, rank:], LANE)
+    rows = slice(0, vec.shape[0])
+    write_row(own_ref, rows, *pieces)
+    write_row(m1_ref, rows, *pieces, ends(vec, REACH * leaf)[0])
 
 
 def groups_kernel(group_ref, kah_ref, kal_ref, points_ref, wide_ref):
@@ -558,12 +583,11 @@
     return lax.ppermute(x, axis, [(i, i ^ m) for i in range(lax.axis_size(axis))])
 
 
-def exchange(m1, own, m4):
+def sides(m4):
     nodes = lax.axis_size("sub") * lax.axis_size("leaf")
     across = [(q, q + 1) for q in range(1, nodes - 1, 2)]
     across = across + [(target, source) for source, target in across]
-    received = swap(m1, "sub", 1), swap(own, "sub", 2), swap(own, "sub", 3)
-    return *received, lax.ppermute(m4, ("leaf", "sub"), across)
+    return lax.ppermute(m4, ("leaf", "sub"), across)
 
 
 def spread_groups(held):
@@ -600,49 +624,44 @@
     transfer = leaf_transfer.reshape(span, rank)
     device = device_transfer[0]
 
-    def messages(rows):
-        return [shape(rows, base + half), shape(rows, base), shape(rows, half)]
-
-    *sent, rhs, points, basis, transfer, device = call(
+    m1, own, m4, rhs, points, basis, transfer, device, near, far = call(
         first_kernel,
-        messages(probes + EXTRA)
-        + [
+        [
+            shape(probes + EXTRA, base + half),
+            shape(probes + EXTRA, base),
+            shape(probes + EXTRA, half),
             shape(probes, count),
             shape(EXTRA, count),
             shape(leaves, rank, leaf),
             shape(span, rank),
             shape(rank, rank),
+            shape(*near_list.shape, dtype=jnp.int32),
+            shape(*far_leaf_list.shape, dtype=jnp.int32),
         ],
         far_memory(
             far_group_list, probe_rhs, coords, leaf_skeleton, group_skeleton, leaf_basis,
-            transfer, device,
+            transfer, device, near_list, far_leaf_list,
         ),
         scalars=1,
     )
-    own = sent[1]
-    r1, r2, r3, r4 = exchange(*sent)
-    th, tl, ubh, ubl = call(
-        prepare_kernel,
-        pair(len(inside) * leaf, leaf)
-        + pair(leaves, 2 * rank, leaf),
-        (near_list, points, basis, transfer, device),
-        scalars=1,
-        scratch=[(3, count, LANE)],
+    r1, r2, r3 = swap(m1, "sub", 1), swap(own, "sub", 2), swap(own, "sub", 3)
+    r4 = sides(m4)
+    ubh, ubl = call(bases_kernel, pair(leaves, 2 * rank, leaf), (basis, transfer, device))
+    th, tl = call(
+        prepare_kernel, pair(len(inside) * leaf, leaf), (near, points), scratch=[(3, count, LANE)]
     )
     (term,) = call(term_kernel, [shape(probes // 2 + EXTRA, LANE)], (own, r1, r2, r3))
     gathered = spread_groups(term)
     klh, kll = call(
         skeleton_kernel,
         pair(subs * span, span),
-        (far_leaf_list, own, r1, r2, r3),
-        scalars=1,
+        (far, own, r1, r2, r3),
         scratch=[(subs, 3, span, LANE)],
     )
     hh, hl = call(
         border_kernel,
         pair(len(across) * leaf, leaf),
-        (near_list, r1, r4, points),
-        scalars=1,
+        (near, r1, r4, points),
         scratch=[(EXTRA, 2 * half), (3, 2 * half, LANE)],
     )
     (inner,) = call(inner_kernel, [shape(probes, count)], (rhs, th, tl))
@@ -651,14 +670,17 @@
         [shape(probes, count)],
         (inner, own, r1, r2, r3, r4, hh, hl, klh, kll, ubh, ubl),
     )
-    image, kgh, kgl, *sent = call(
+    image, kgh, kgl, m4 = call(
         middle_kernel,
-        [shape(probes, count)] + pair(rank, groups * rank) + messages(probes),
+        [shape(probes, count)] + pair(rank, groups * rank) + [shape(probes, half)],
         (part, gathered, ubh, ubl),
         scratch=[(EXTRA, groups * rank), (3, LANE, LANE)],
     )
-    own = sent[1]
-    r1, r2, r3, r4 = exchange(*sent)
+    r4 = sides(m4)
+    m1, own = call(
+        second_kernel, [shape(probes, base + half), shape(probes, base)], (image, ubh, ubl)
+    )
+    r1, r2, r3 = swap(m1, "sub", 1), swap(own, "sub", 2), swap(own, "sub", 3)
     dense = groups * rank <= DENSE
     if dense:
         kgh, kgl = call(

time: 55 us -> 54.5 us (level)
  waiting for transfers between devices: 13.7 us -> 17.2 us
  starting transfers between devices: 21.2 us -> 19.4 us
  Pallas kernels: 18.3 us -> 16.9 us
  local copies, waits for them, and re-layouts: 0.7 us -> 0 us
    ppermute x10 -> x9, waiting for transfers between devices: 6.62 us -> 10.1 us  [swap(): lax.ppermute(x, axis, [(i, i ^ m) for i in range(lax.axis_size(axis))])]
    ppermute x10 -> x9, starting transfers between devices: 15.4 us -> 13.1 us  [swap(): lax.ppermute(x, axis, [(i, i ^ m) for i in range(lax.axis_size(axis))])]
    pallas_call x12 -> x14, Pallas kernels: 18.3 us -> 16.9 us  [call(): pl.pallas_call(kernel, out_shape=tuple(outs), in_specs=smem(scalars) + vm...]
    unnamed x8 -> x0, local copies, waits for them, and re-layouts: 0.69 us -> none
  transfers between devices with their start and end apart: 13 -> 12, of which waited for: 5 -> 7; matrix products, arithmetic and copies ran while one was open for 0% -> 0% of each run, Pallas kernels for 23% -> 19%
where the time goes in v4:
time: 54.5 us; the launch traced here: 54.3 us
  starting transfers between devices  19.4 us (36%)
  waiting for transfers between devices  17.2 us (32%)
  Pallas kernels  16.9 us (31%)
  between operations  0.75 us (1%)
    pallas_call x14, Pallas kernels, call(): pl.pallas_call(kernel, out_shape=tuple(outs), in_specs=smem(scalars) + vm...  16.9 us
    ppermute x9, starting transfers between devices, swap(): lax.ppermute(x, axis, [(i, i ^ m) for i in range(lax.axis_size(axis))])  13.1 us
    ppermute x9, waiting for transfers between devices, swap(): lax.ppermute(x, axis, [(i, i ^ m) for i in range(lax.axis_size(axis))])  10.1 us
    all_to_all x1, waiting for transfers between devices, shards(): gathered = lax.all_to_all(message, ('leaf', 'sub'), 0, 0)  7.1 us
    all_to_all x1, starting transfers between devices, shards(): gathered = lax.all_to_all(message, ('leaf', 'sub'), 0, 0)  4.92 us
    ppermute x2, starting transfers between devices, sides(): return lax.ppermute(m4, ('leaf', 'sub'), across)  1.31 us
  transfers between devices with their start and end apart: 12, of which 7 were waited for; matrix products, arithmetic and copies ran while one was open for 0% of the time, Pallas kernels for 19%

profile of v4, /device:TPU:0, one launch (start us, length us, event | category | flops | bytes accessed | tf_op | source)
XLA Modules:
  0.0 54.3 jit_solution(18161926872510053020)
XLA Ops:
  0.6 1.9 %shard_map.113 = (f32[40,896]{1,0:T(8,128)S(1)}, f32[40,384]{1,0:T(8,128)S(1)}, f32[40,512]{1,0:T(8,128)S(1)}, f32[32,1024]{1,0:T(8,128)S(1)}, f32[8,1024]{1,0:T...) custom-call(s32[1,14]{1,0:T(1,128)} %list_ref.1, ...), custom_call_target="tpu_custom_call" | custom-call | bytes 1000000 | tf_op jit(solution)/shard_map/pallas_call | solution.py:569
  2.5 0.6 %collective-permute-start = (f32[40,896]{1,0:T(8,128)S(1)}, f32[40,896]{1,0:T(8,128)S(1)}, u32[]{:S(2)}, u32[]{:S(2)}) collective-permute-start(f32[40,896]{1,0:T(8,128)S(1)} %get-tuple-element.34), channel_id=1, source_target_pairs={{0,1},{1,0},{2,3},{3,2},{4,5},{5,4},{6,7},{7,6},{8,9},{9,8},{10,11... | collective-permute-start | bytes 430088 | tf_op jit(solution)/shard_map/ppermute | solution.py:583
  3.1 2.6 %collective-permute-start.1 = (f32[40,384]{1,0:T(8,128)S(1)}, f32[40,384]{1,0:T(8,128)S(1)}, u32[]{:S(2)}, u32[]{:S(2)}) collective-permute-start(f32[40,384]{1,0:T(8,128)S(1)} %get-tuple-element.33.own), channel_id=1, source_target_pairs={{0,2},{1,3},{2,0},{3,1},{4,6},{5,7},{6,4},{7,5},{8,10},{9,11},{10,... | collective-permute-start | bytes 184328 | tf_op jit(solution)/shard_map/ppermute | solution.py:583
  5.7 2.6 %collective-permute-done.1.r2 = f32[40,384]{1,0:T(8,128)S(1)} collective-permute-done((f32[40,384]{1,0:T(8,128)S(1)}, f32[40,384]{1,0:T(8,128)S(1)}, u32[]{:S(2)}, u32[]{:S(2)}) %collective-permute-start.1) | collective-permute-done | bytes 61472 | tf_op jit(solution)/shard_map/ppermute | solution.py:583
  8.3 1.4 %collective-permute-done.2.r3 = f32[40,384]{1,0:T(8,128)S(1)} collective-permute-done((f32[40,384]{1,0:T(8,128)S(1)}, f32[40,384]{1,0:T(8,128)S(1)}, u32[]{:S(2)}, u32[]{:S(2)}) %collective-permute-start.2) | collective-permute-done | bytes 61472 | tf_op jit(solution)/shard_map/ppermute | solution.py:583
  9.6 0.1 shard_map.120
  9.7 2.6 %collective-permute-start.4 = (f32[1,24,128]{2,1,0:T(8,128)S(1)}, f32[1,24,128]{2,1,0:T(8,128)S(1)}, u32[]{:S(2)}, u32[]{:S(2)}) collective-permute-start(f32[1,24,128]{2,1,0:T(8,128)S(1)} %bitcast.3), channel_id=1, source_target_pairs={{0,16},{4,20},{8,24},{12,28},{16,0},{20,4},{24,8},{28,12},{1,17},{... | collective-permute-start | bytes 36872 | tf_op jit(solution)/shard_map/ppermute | solution.py:583
  12.3 2.0 %collective-permute-done.4 = f32[1,24,128]{2,1,0:T(8,128)S(1)} collective-permute-done((f32[1,24,128]{2,1,0:T(8,128)S(1)}, f32[1,24,128]{2,1,0:T(8,128)S(1)}, u32[]{:S(2)}, u32[]{:S(2)}) %collective-permute-start.4) | collective-permute-done | bytes 12320 | tf_op jit(solution)/shard_map/ppermute | solution.py:583
  14.3 1.6 %collective-permute-start.5 = (f32[2,24,128]{2,1,0:T(8,128)S(1)}, f32[2,24,128]{2,1,0:T(8,128)S(1)}, u32[]{:S(2)}, u32[]{:S(2)}) collective-permute-start(f32[2,24,128]{2,1,0:T(8,128)S(1)} %pad_maximum_fusion.2), channel_id=1, source_target_pairs={{0,8},{4,12},{8,0},{12,4},{16,24},{20,28},{24,16},{28,20},{1,9},{5... | collective-permute-start | bytes 73736 | tf_op jit(solution)/shard_map/ppermute | solution.py:583
  15.9 0.7 %collective-permute-start.3 = (f32[40,512]{1,0:T(8,128)S(1)}, f32[40,512]{1,0:T(8,128)S(1)}, u32[]{:S(2)}, u32[]{:S(2)}) collective-permute-start(f32[40,512]{1,0:T(8,128)S(1)} %get-tuple-element.35), channel_id=1, source_target_pairs={{1,2},{3,4},{5,6},{7,8},{9,10},{11,12},{13,14},{15,16},{17,18},{19... | collective-permute-start | bytes 245768 | tf_op jit(solution)/shard_map/ppermute | solution.py:590
  16.5 1.6 %collective-permute-done.5 = f32[2,24,128]{2,1,0:T(8,128)S(1)} collective-permute-done((f32[2,24,128]{2,1,0:T(8,128)S(1)}, f32[2,24,128]{2,1,0:T(8,128)S(1)}, u32[]{:S(2)}, u32[]{:S(2)}) %collective-permute-start.5) | collective-permute-done | bytes 24608 | tf_op jit(solution)/shard_map/ppermute | solution.py:583
  18.1 1.5 %collective-permute-start.6 = (f32[4,24,128]{2,1,0:T(8,128)S(1)}, f32[4,24,128]{2,1,0:T(8,128)S(1)}, u32[]{:S(2)}, u32[]{:S(2)}) collective-permute-start(f32[4,24,128]{2,1,0:T(8,128)S(1)} %pad_maximum_fusion.1), channel_id=1, source_target_pairs={{0,4},{4,0},{8,12},{12,8},{16,20},{20,16},{24,28},{28,24},{1,5},{5... | collective-permute-start | bytes 147464 | tf_op jit(solution)/shard_map/ppermute | solution.py:583
  19.6 2.8 %shard_map.114 = (bf16[2304,256]{1,0:T(8,128)(2,1)S(1)}, bf16[2304,256]{1,0:T(8,128)(2,1)S(1)}) custom-call(s32[4,5]{1,0:T(4,128)S(1)} %get-tuple-element.29.near_ref, f32[8,1024]{1,0:T(8,128)S(1)} %get-tuple-element.30.points_ref), custom_call_target="tpu_custom_call" | custom-call | bytes 1000000 | tf_op jit(solution)/shard_map/pallas_call | solution.py:569
  22.5 0.9 %shard_map.115.inner_ref = f32[32,1024]{1,0:T(8,128)S(1)} custom-call(f32[32,1024]{1,0:T(8,128)S(1)} %get-tuple-element.28.vec_ref.rhs_ref, bf16[2304,256]{1,0:T(8,128)(2,1)S(1)} %get-tuple-element.31.th_ref, bf16[2304,256]{1,0:T(8,128)(2,1)S(1)} %get-tuple-element.32.tl_ref), custom_call_target="tpu_custom_call" | custom-call | bytes 1000000 | tf_op jit(solution)/shard_map/pallas_call | solution.py:569
  23.4 0.8 %shard_map.118 = (bf16[4,128,256]{2,1,0:T(8,128)(2,1)S(1)}, bf16[4,128,256]{2,1,0:T(8,128)(2,1)S(1)}) custom-call(f32[4,64,256]{2,1,0:T(8,128)S(1)} %get-tuple-element.41.basis_ref, f32[256,64]{1,0:T(8,128)S(1)} %get-tuple-element.42.transfer_ref, f32[64,64]{1,0:T(8,128)S(1)} %get-tuple-element.43.device_ref), custom_call_target="tpu_custom_call" | custom-call | bytes 1000000 | tf_op jit(solution)/shard_map/pallas_call | solution.py:569
  24.2 2.2 %shard_map.116 = (bf16[1536,256]{1,0:T(8,128)(2,1)S(1)}, bf16[1536,256]{1,0:T(8,128)(2,1)S(1)}) custom-call(s32[4,5]{1,0:T(4,128)S(1)} %get-tuple-element.29.near_ref, f32[40,896]{1,0:T(8,128)S(1)} %collective-permute-done.r1, f32[40,512]{1,0:T(8,128)S(1)} %collective-permute-done.3.r4, f32[8,1024]{1,0:T(8,128)S(1)} %get-tuple-element.30.points_ref), custom_call_target="tpu_custom_call" | custom-call | bytes 1000000 | tf_op jit(solution)/shard_map/pallas_call | solution.py:569
  26.4 1.2 %shard_map.117 = (bf16[1024,256]{1,0:T(8,128)(2,1)S(1)}, bf16[1024,256]{1,0:T(8,128)(2,1)S(1)}) custom-call(s32[4,8]{1,0:T(4,128)S(1)} %get-tuple-element.38.far_ref, f32[40,384]{1,0:T(8,128)S(1)} %get-tuple-element.33.own, f32[40,896]{1,0:T(8,128)S(1)} %collective-permute-done.r1, f32[40,384]{1,0:T(8,128)S(1)} %collective-permute-done.1.r2, ...), custom_call_target="tpu_custom_call" | custom-call | bytes 1000000 | tf_op jit(solution)/shard_map/pallas_call | solution.py:569
  27.5 0.7 %shard_map.119.part_ref = f32[32,1024]{1,0:T(8,128)S(1)} custom-call(f32[32,1024]{1,0:T(8,128)S(1)} %shard_map.115.inner_ref, f32[40,384]{1,0:T(8,128)S(1)} %get-tuple-element.33.own, f32[40,896]{1,0:T(8,128)S(1)} %collective-permute-done.r1, f32[40,384]{1,0:T(8,128)S(1)} %collective-permute-done.1.r2, f32[40,384]{1,0:T(8,128)S(1)} %collective-permute-done.2.r3, ...), custom_call_target="tpu_custom_call" | custom-call | bytes 1000000 | tf_op jit(solution)/shard_map/pallas_call | solution.py:569
  28.3 1.1 %shard_map.121 = (f32[32,1024]{1,0:T(8,128)S(1)}, bf16[64,512]{1,0:T(8,128)(2,1)}, bf16[64,512]{1,0:T(8,128)(2,1)}, f32[32,512]{1,0:T(8,128)S(1)}) custom-call(f32[32,1024]{1,0:T(8,128)S(1)} %shard_map.119.part_ref, f32[8,24,128]{2,1,0:T(8,128)S(1)} %pad_maximum_fusion.group_ref, bf16[4,128,256]{2,1,0:T(8,128)(2,1)S(1)} %get-tuple-element.44.ubh_ref, ...), custom_call_target="tpu_custom_call" | custom-call | bytes 1000000 | tf_op jit(solution)/shard_map/pallas_call | solution.py:569
  29.4 0.3 shard_map.123
  29.7 0.8 %collective-permute-start.7 = (f32[32,896]{1,0:T(8,128)S(1)}, f32[32,896]{1,0:T(8,128)S(1)}, u32[]{:S(2)}, u32[]{:S(2)}) collective-permute-start(f32[32,896]{1,0:T(8,128)S(1)} %get-tuple-element.48), channel_id=1, source_target_pairs={{0,1},{1,0},{2,3},{3,2},{4,5},{5,4},{6,7},{7,6},{8,9},{9,8},{10,11... | collective-permute-start | bytes 344072 | tf_op jit(solution)/shard_map/ppermute | solution.py:583
  30.5 0.7 %collective-permute-start.10 = (f32[32,512]{1,0:T(8,128)S(1)}, f32[32,512]{1,0:T(8,128)S(1)}, u32[]{:S(2)}, u32[]{:S(2)}) collective-permute-start(f32[32,512]{1,0:T(8,128)S(1)} %get-tuple-element.49), channel_id=1, source_target_pairs={{1,2},{3,4},{5,6},{7,8},{9,10},{11,12},{13,14},{15,16},{17,18},{19... | collective-permute-start | bytes 196616 | tf_op jit(solution)/shard_map/ppermute | solution.py:590
  31.1 3.0 %collective-permute-start.8 = (f32[32,384]{1,0:T(8,128)S(1)}, f32[32,384]{1,0:T(8,128)S(1)}, u32[]{:S(2)}, u32[]{:S(2)}) collective-permute-start(f32[32,384]{1,0:T(8,128)S(1)} %get-tuple-element.47.own), channel_id=1, source_target_pairs={{0,2},{1,3},{2,0},{3,1},{4,6},{5,7},{6,4},{7,5},{8,10},{9,11},{10,... | collective-permute-start | bytes 147464 | tf_op jit(solution)/shard_map/ppermute | solution.py:583
  34.1 0.5 %collective-permute-start.9 = (f32[32,384]{1,0:T(8,128)S(1)}, f32[32,384]{1,0:T(8,128)S(1)}, u32[]{:S(2)}, u32[]{:S(2)}) collective-permute-start(f32[32,384]{1,0:T(8,128)S(1)} %get-tuple-element.47.own), channel_id=1, source_target_pairs={{0,3},{1,2},{2,1},{3,0},{4,7},{5,6},{6,5},{7,4},{8,11},{9,10},{10,... | collective-permute-start | bytes 147464 | tf_op jit(solution)/shard_map/ppermute | solution.py:583
  34.7 0.9 %shard_map.122.inner_ref = f32[32,1024]{1,0:T(8,128)S(1)} custom-call(f32[32,1024]{1,0:T(8,128)S(1)} %get-tuple-element.46.vec_ref.first_ref, bf16[2304,256]{1,0:T(8,128)(2,1)S(1)} %get-tuple-element.31.th_ref, bf16[2304,256]{1,0:T(8,128)(2,1)S(1)} %get-tuple-element.32.tl_ref), custom_call_target="tpu_custom_call" | custom-call | bytes 1000000 | tf_op jit(solution)/shard_map/pallas_call | solution.py:569
  35.5 2.0 %collective-permute-done.8.r2 = f32[32,384]{1,0:T(8,128)S(1)} collective-permute-done((f32[32,384]{1,0:T(8,128)S(1)}, f32[32,384]{1,0:T(8,128)S(1)}, u32[]{:S(2)}, u32[]{:S(2)}) %collective-permute-start.8) | collective-permute-done | bytes 49184 | tf_op jit(solution)/shard_map/ppermute | solution.py:583
  37.5 0.6 %collective-permute-done.9.r3 = f32[32,384]{1,0:T(8,128)S(1)} collective-permute-done((f32[32,384]{1,0:T(8,128)S(1)}, f32[32,384]{1,0:T(8,128)S(1)}, u32[]{:S(2)}, u32[]{:S(2)}) %collective-permute-start.9) | collective-permute-done | bytes 49184 | tf_op jit(solution)/shard_map/ppermute | solution.py:583
  38.2 1.5 %shard_map.124 = (f32[32,1024]{1,0:T(8,128)S(1)}, f32[32,8,128]{2,1,0:T(8,128)}) custom-call(f32[32,1024]{1,0:T(8,128)S(1)} %get-tuple-element.28.vec_ref.rhs_ref, f32[32,1024]{1,0:T(8,128)S(1)} %get-tuple-element.46.vec_ref.first_ref, f32[32,1024]{1,0:T(8,128)S(1)} %shard_map.122.inner_ref, f32[32,384]{1,0:T(8,128)S(1)} %get-tuple-element.47.own, ...), custom_call_target="tpu_custom_call" | custom-call | bytes 1000000 | tf_op jit(solution)/shard_map/pallas_call | solution.py:569
  39.7 4.9 %all-to-all-start = ((f32[32,8,128]{2,1,0:T(8,128)}), f32[32,8,128]{2,1,0:T(8,128)S(1)}, u32[]{:S(2)}, u32[]{:S(2)}) async-start(f32[32,8,128]{2,1,0:T(8,128)} %get-tuple-element.51), calls=%async_computation | async-start | bytes 262144 | tf_op jit(solution)/shard_map/all_to_all | solution.py:701
  44.6 1.1 %shard_map.125 = (bf16[512,512]{1,0:T(8,128)(2,1)S(1)}, bf16[512,512]{1,0:T(8,128)(2,1)S(1)}) custom-call(f32[8,24,128]{2,1,0:T(8,128)S(1)} %pad_maximum_fusion.group_ref), custom_call_target="tpu_custom_call" | custom-call | bytes 1000000 | tf_op jit(solution)/shard_map/pallas_call | solution.py:569
  45.7 7.1 %all-to-all-done.group_ref = f32[32,8,128]{2,1,0:T(8,128)S(1)} async-done(((f32[32,8,128]{2,1,0:T(8,128)}), f32[32,8,128]{2,1,0:T(8,128)S(1)}, u32[]{:S(2)}, u32[]{:S(2)}) %all-to-all-start) | async-done | bytes 131104 | tf_op jit(solution)/shard_map/all_to_all | solution.py:701
  52.8 1.5 %shard_map.126 = (f32[32,1024]{1,0:T(8,128)}, f32[32,1024]{1,0:T(8,128)}) custom-call(f32[32,1024]{1,0:T(8,128)S(1)} %get-tuple-element.50.part_ref, f32[32,8,128]{2,1,0:T(8,128)S(1)} %all-to-all-done.group_ref, bf16[512,512]{1,0:T(8,128)(2,1)S(1)} %get-tuple-element.52.kah_ref, bf16[512,512]{1,0:T(8,128)(2,1)S(1)} %get-tuple-element.53.kal_ref, ...), custom_call_target="tpu_custom_call" | custom-call | bytes 1000000 | tf_op jit(solution)/shard_map/pallas_call | solution.py:569
  (9 shorter events, 0.1 us)
Async XLA Ops:
  2.5 7.1 %collective-permute-start = (f32[40,896]{1,0:T(8,128)S(1)}, f32[40,896]{1,0:T(8,128)S(1)}, u32[]{:S(2)}, u32[]{:S(2)}) collective-permute-start(f32[40,896]{1,0:T(8,128)S(1)} %get-tuple-element.34), channel_id=1, source_target_pairs={{0,1},{1,0},{2,3},{3,2},{4,5},{5,4},{6,7},{7,6},{8,9},{9,8},{10,11... | collective-permute-start | bytes 430088 | tf_op jit(solution)/shard_map/ppermute | solution.py:583
  3.1 5.2 %collective-permute-start.1 = (f32[40,384]{1,0:T(8,128)S(1)}, f32[40,384]{1,0:T(8,128)S(1)}, u32[]{:S(2)}, u32[]{:S(2)}) collective-permute-start(f32[40,384]{1,0:T(8,128)S(1)} %get-tuple-element.33.own), channel_id=1, source_target_pairs={{0,2},{1,3},{2,0},{3,1},{4,6},{5,7},{6,4},{7,5},{8,10},{9,11},{10,... | collective-permute-start | bytes 184328 | tf_op jit(solution)/shard_map/ppermute | solution.py:583
  5.7 4.0 %collective-permute-start.2 = (f32[40,384]{1,0:T(8,128)S(1)}, f32[40,384]{1,0:T(8,128)S(1)}, u32[]{:S(2)}, u32[]{:S(2)}) collective-permute-start(f32[40,384]{1,0:T(8,128)S(1)} %get-tuple-element.33.own), channel_id=1, source_target_pairs={{0,3},{1,2},{2,1},{3,0},{4,7},{5,6},{6,5},{7,4},{8,11},{9,10},{10,... | collective-permute-start | bytes 184328 | tf_op jit(solution)/shard_map/ppermute | solution.py:583
  9.7 4.6 %collective-permute-start.4 = (f32[1,24,128]{2,1,0:T(8,128)S(1)}, f32[1,24,128]{2,1,0:T(8,128)S(1)}, u32[]{:S(2)}, u32[]{:S(2)}) collective-permute-start(f32[1,24,128]{2,1,0:T(8,128)S(1)} %bitcast.3), channel_id=1, source_target_pairs={{0,16},{4,20},{8,24},{12,28},{16,0},{20,4},{24,8},{28,12},{1,17},{... | collective-permute-start | bytes 36872 | tf_op jit(solution)/shard_map/ppermute | solution.py:583
  14.3 3.8 %collective-permute-start.5 = (f32[2,24,128]{2,1,0:T(8,128)S(1)}, f32[2,24,128]{2,1,0:T(8,128)S(1)}, u32[]{:S(2)}, u32[]{:S(2)}) collective-permute-start(f32[2,24,128]{2,1,0:T(8,128)S(1)} %pad_maximum_fusion.2), channel_id=1, source_target_pairs={{0,8},{4,12},{8,0},{12,4},{16,24},{20,28},{24,16},{28,20},{1,9},{5... | collective-permute-start | bytes 73736 | tf_op jit(solution)/shard_map/ppermute | solution.py:583
  15.9 8.3 %collective-permute-start.3 = (f32[40,512]{1,0:T(8,128)S(1)}, f32[40,512]{1,0:T(8,128)S(1)}, u32[]{:S(2)}, u32[]{:S(2)}) collective-permute-start(f32[40,512]{1,0:T(8,128)S(1)} %get-tuple-element.35), channel_id=1, source_target_pairs={{1,2},{3,4},{5,6},{7,8},{9,10},{11,12},{13,14},{15,16},{17,18},{19... | collective-permute-start | bytes 245768 | tf_op jit(solution)/shard_map/ppermute | solution.py:590
  18.1 10.1 %collective-permute-start.6 = (f32[4,24,128]{2,1,0:T(8,128)S(1)}, f32[4,24,128]{2,1,0:T(8,128)S(1)}, u32[]{:S(2)}, u32[]{:S(2)}) collective-permute-start(f32[4,24,128]{2,1,0:T(8,128)S(1)} %pad_maximum_fusion.1), channel_id=1, source_target_pairs={{0,4},{4,0},{8,12},{12,8},{16,20},{20,16},{24,28},{28,24},{1,5},{5... | collective-permute-start | bytes 147464 | tf_op jit(solution)/shard_map/ppermute | solution.py:583
  29.7 8.5 %collective-permute-start.7 = (f32[32,896]{1,0:T(8,128)S(1)}, f32[32,896]{1,0:T(8,128)S(1)}, u32[]{:S(2)}, u32[]{:S(2)}) collective-permute-start(f32[32,896]{1,0:T(8,128)S(1)} %get-tuple-element.48), channel_id=1, source_target_pairs={{0,1},{1,0},{2,3},{3,2},{4,5},{5,4},{6,7},{7,6},{8,9},{9,8},{10,11... | collective-permute-start | bytes 344072 | tf_op jit(solution)/shard_map/ppermute | solution.py:583
  30.5 7.7 %collective-permute-start.10 = (f32[32,512]{1,0:T(8,128)S(1)}, f32[32,512]{1,0:T(8,128)S(1)}, u32[]{:S(2)}, u32[]{:S(2)}) collective-permute-start(f32[32,512]{1,0:T(8,128)S(1)} %get-tuple-element.49), channel_id=1, source_target_pairs={{1,2},{3,4},{5,6},{7,8},{9,10},{11,12},{13,14},{15,16},{17,18},{19... | collective-permute-start | bytes 196616 | tf_op jit(solution)/shard_map/ppermute | solution.py:590
  31.1 6.4 %collective-permute-start.8 = (f32[32,384]{1,0:T(8,128)S(1)}, f32[32,384]{1,0:T(8,128)S(1)}, u32[]{:S(2)}, u32[]{:S(2)}) collective-permute-start(f32[32,384]{1,0:T(8,128)S(1)} %get-tuple-element.47.own), channel_id=1, source_target_pairs={{0,2},{1,3},{2,0},{3,1},{4,6},{5,7},{6,4},{7,5},{8,10},{9,11},{10,... | collective-permute-start | bytes 147464 | tf_op jit(solution)/shard_map/ppermute | solution.py:583
  34.1 4.0 %collective-permute-start.9 = (f32[32,384]{1,0:T(8,128)S(1)}, f32[32,384]{1,0:T(8,128)S(1)}, u32[]{:S(2)}, u32[]{:S(2)}) collective-permute-start(f32[32,384]{1,0:T(8,128)S(1)} %get-tuple-element.47.own), channel_id=1, source_target_pairs={{0,3},{1,2},{2,1},{3,0},{4,7},{5,6},{6,5},{7,4},{8,11},{9,10},{10,... | collective-permute-start | bytes 147464 | tf_op jit(solution)/shard_map/ppermute | solution.py:583
  39.7 13.1 %all-to-all-start = ((f32[32,8,128]{2,1,0:T(8,128)}), f32[32,8,128]{2,1,0:T(8,128)S(1)}, u32[]{:S(2)}, u32[]{:S(2)}) async-start(f32[32,8,128]{2,1,0:T(8,128)} %get-tuple-element.51), calls=%async_computation | async-start | bytes 262144 | tf_op jit(solution)/shard_map/all_to_all | solution.py:701

commit v5 on v4

--- a/solution.py
+++ b/solution.py
@@ -104,7 +104,7 @@
     list_ref, vec_ref, coords_ref, skel_ref, gskel_ref, basis_ref, transfer_ref, device_ref,
     near_ref, far_ref,
     m1_ref, own_ref, m4_ref, rhs_ref, points_ref, basis_out, transfer_out, device_out,
-    near_out, far_out,
+    near_out, far_out, group_out,
 ):
     leaves, _, leaf = basis_ref.shape
     probes = vec_ref.shape[0]
@@ -114,7 +114,7 @@
         [dot(vec[:, i * leaf : (i + 1) * leaf], basis_ref[i], 1, 1) for i in range(leaves)],
         axis=1,
     )
-    term = padded_lanes(dot(dot(coefs, transfer_ref[...]), device_ref[...]), LANE)
+    term = fold_rows(dot(dot(coefs, transfer_ref[...]), device_ref[...]), leaves)
     relative = lax.axis_index("leaf") ^ lax.broadcasted_iota(jnp.int32, (1, LANE), 1)
     listed = jnp.zeros((1, LANE), F32)
     for column in range(list_ref.shape[1]):
@@ -123,14 +123,19 @@
     points = padded_rows(coords_ref[...], EXTRA)
     skel = padded_rows(skel_ref[...], EXTRA)
     group_rows = padded_rows(group_rows, EXTRA)
-    for rows, block in (
-        (slice(0, probes), (vec, coefs, term)),
-        (slice(probes, probes + EXTRA), (points, skel, group_rows)),
+    below = probes + term.shape[0]
+    blank = jnp.zeros((EXTRA, 2 * half), F32)
+    for rows, block, coordinates in (
+        (slice(0, probes), coefs, vec),
+        (slice(probes, below), term, points),
+        (slice(below, below + EXTRA), skel, blank),
     ):
-        part_a, part_b = ends(block[0], half)
-        write_row(m1_ref, rows, *block[1:], part_a)
-        write_row(own_ref, rows, *block[1:])
-        write_row(m4_ref, rows, part_b)
+        part_a, part_b = ends(coordinates, half)
+        write_row(m1_ref, rows, block, part_a)
+        write_row(own_ref, rows, block)
+        if rows.start < below:
+            write_row(m4_ref, rows, part_b)
+    group_out[...] = group_rows
     rhs_ref[...] = vec
     points_ref[...] = points
     basis_out[...] = basis_ref[...]
@@ -148,7 +153,9 @@
         )
 
 
-def fill_tile(wide_ref, source, points_ref, top_row, lane, width, weight, pair, row, size):
+def fill_tile(
+    wide_ref, source, points_ref, top_row, lane, width, weight, pair, row, size, to=0
+):
     high_ref, low_ref = pair
 
     def body(step, _):
@@ -162,8 +169,8 @@
             ]
             factor = weight if weight.shape[1] == LANE else weight[:, at : at + LANE]
             top, rest = split(matern(rows, cols, factor))
-            high_ref[pl.ds(target, CHUNK), at : at + LANE] = top
-            low_ref[pl.ds(target, CHUNK), at : at + LANE] = rest
+            high_ref[pl.ds(target, CHUNK), to + at : to + at + LANE] = top
+            low_ref[pl.ds(target, CHUNK), to + at : to + at + LANE] = rest
         return 0
 
     lax.fori_loop(0, size // CHUNK, body, 0, unroll=min(size // CHUNK, UNROLL // width))
@@ -208,23 +215,22 @@
         ubl_ref[i] = rest
 
 
-def folded(x, rank):
-    half = x.shape[0] // 2
-    return jnp.concatenate([x[:half, :rank], x[half:, :rank]], axis=1)
-
-
-def summed_terms(own, r1, r2, r3, rows, span):
-    lanes = slice(span, span + LANE)
-    return (own[rows, lanes] + r1[rows, lanes]) + (r2[rows, lanes] + r3[rows, lanes])
-
-
-def term_kernel(own, r1, r2, r3, out_ref):
+def fold_rows(x, parts):
+    rows = x.shape[0] // parts
+    return jnp.concatenate([x[r * rows : (r + 1) * rows] for r in range(parts)], axis=1)
+
+
+def summed_terms(messages, probes, span):
+    own, r1, r2, r3 = (ref[probes : probes + EXTRA, 0:span] for ref in messages)
+    total = (own + r1) + (r2 + r3)
+    return jnp.concatenate([total[:, at : at + LANE] for at in range(0, span, LANE)], axis=0)
+
+
+def term_kernel(own, r1, r2, r3, group_rows, out_ref):
     half = out_ref.shape[0] - EXTRA
-    span = own.shape[1] - LANE
-    out_ref[half:, :] = own[2 * half :, span:]
-    out_ref[0:half, :] = folded(
-        summed_terms(own, r1, r2, r3, slice(0, 2 * half), span), LANE // 2
-    )
+    probes = own.shape[0] - 2 * EXTRA
+    out_ref[half:, :] = group_rows[...]
+    out_ref[0:half, :] = summed_terms((own, r1, r2, r3), probes, own.shape[1])
 
 
 def leaf_slice(x, i, leaf):
@@ -278,7 +284,7 @@
     leaves = far_ref.shape[0]
     span = klh_ref.shape[1]
     rank = span // leaves
-    probes = own.shape[0] - EXTRA
+    top = own.shape[0] - EXTRA
     sub = lax.axis_index("sub")
     group_first = lax.axis_index("leaf") * lax.axis_size("sub") * leaves
     messages = (own, r1, r2, r3)
@@ -288,12 +294,12 @@
         axis=1,
     )
     for m, message in enumerate(messages):
-        spread_columns(message[probes : probes + EXTRA, 0:span], wide_ref.at[m])
+        spread_columns(message[top : top + EXTRA, 0:span], wide_ref.at[m])
     for m in range(len(messages)):
         for j in range(leaves):
             index = group_first + (sub ^ m) * leaves + j
             fill_tile(
-                wide_ref.at[m], j * rank, own, probes, 0, span, named(listed, index),
+                wide_ref.at[m], j * rank, own, top, 0, span, named(listed, index),
                 (klh_ref, kll_ref), m * span + j * rank, rank,
             )
 
@@ -343,7 +349,6 @@
 ):
     base = own.shape[1]
     span = klh_ref.shape[1]
-    rank = ubh_ref.shape[1] // 2
     rows = slice(0, vec_ref.shape[0])
     rhs = rhs_ref[...]
     vec = vec_ref[...]
@@ -363,13 +368,16 @@
     columns = jnp.zeros((vec.shape[0], LANE), F32)
     for at, share in enumerate(shares):
         columns = jnp.where(lane == at, share, columns)
-    term = folded(summed_terms(own, r1, r2, r3, rows, span), rank)
+    term = summed_terms((own, r1, r2, r3), vec.shape[0], span)
     size = term.shape[0] // lax.axis_size("sub")
     sub = lax.axis_index("sub")
     mine = term[0:size]
     for m in range(1, lax.axis_size("sub")):
         mine = jnp.where(sub == m, term[m * size : (m + 1) * size], mine)
-    message = jnp.concatenate([mine, padded_lanes(columns.T[0:SHARES], LANE)], axis=0)
+    flat = columns.T
+    pieces = [mine[r : r + 1] for r in range(size)]
+    pieces = pieces + [flat[at : at + 1, 0 : vec.shape[0]] for at in range(SHARES)]
+    message = jnp.concatenate(pieces, axis=1)
     for m in range(message_ref.shape[0]):
         message_ref[m] = message
 
@@ -392,13 +400,16 @@
     )
 
 
-def group_row(group_ref, half, rank, places):
+def group_row(group_ref, half, rank, leaves):
+    size = half * LANE // (leaves * rank)
     return jnp.concatenate(
         [
             jnp.concatenate(
-                [group_ref[m, 0:half, at : at + rank] for m in places], axis=1
+                [group_ref[m, row : row + size, at : at + rank] for m in range(group_ref.shape[0])],
+                axis=1,
             )
-            for at in (0, rank)
+            for row in range(0, half, size)
+            for at in range(0, LANE, rank)
         ],
         axis=0,
     )
@@ -410,7 +421,7 @@
     listed = group_ref[block, row : row + 1, :]
     lane_group = lax.broadcasted_iota(jnp.int32, (1, groups * rank), 1) // rank
     mask = jnp.zeros((1, groups * rank), F32)
-    for m in range(groups):
+    for m in range(block + 1, groups):
         at = order[block] ^ order[m]
         mask = jnp.where(lane_group == m, listed[:, at : at + 1], mask)
     return mask
@@ -430,7 +441,7 @@
         wide_ref, 0, points_ref, 0, 0, groups * rank,
         group_mask(group_ref, half + 3, 0, rank), (kgh_ref, kgl_ref), 0, rank,
     )
-    held = group_row(group_ref, half, rank, range(groups))
+    held = group_row(group_ref, half, rank, leaves)
     group_far = product(stacked(held), kgh_ref[...], kgl_ref[...], True)
     group_stack = stacked(group_far)
     image = jnp.concatenate(
@@ -455,10 +466,14 @@
         both = product(stacked(leaf_slice(vec, i, leaf)), ubh_ref[i], ubl_ref[i], True)
         coefs.append(both[:, :rank])
         term = both if term is None else term + both
-    pieces = jnp.concatenate(coefs, axis=1), padded_lanes(term[:, rank:], LANE)
-    rows = slice(0, vec.shape[0])
-    write_row(own_ref, rows, *pieces)
-    write_row(m1_ref, rows, *pieces, ends(vec, REACH * leaf)[0])
+    coefs = jnp.concatenate(coefs, axis=1)
+    term = fold_rows(term[:, rank:], leaves)
+    probes = vec.shape[0]
+    write_row(own_ref, slice(0, probes), coefs)
+    write_row(own_ref, slice(probes, probes + EXTRA), term)
+    write_row(m1_ref, slice(0, probes), coefs, ends(vec, REACH * leaf)[0])
+    blank = jnp.zeros((EXTRA, REACH * leaf), F32)
+    write_row(m1_ref, slice(probes, probes + EXTRA), term, blank)
 
 
 def groups_kernel(group_ref, kah_ref, kal_ref, points_ref, wide_ref):
@@ -467,47 +482,54 @@
     half = rows - EXTRA
     points_ref[...] = group_points(group_ref, half, rank)
     spread_columns(points_ref[...], wide_ref)
-    for m in range(groups):
+    kah_ref[...] = jnp.zeros(kah_ref.shape, BF16)
+    kal_ref[...] = jnp.zeros(kal_ref.shape, BF16)
+    for m in range(groups - 1):
+        lane = (m + 1) * rank // LANE * LANE
+        mask = group_mask(group_ref, half + 3, m, rank)
         fill_tile(
-            wide_ref, m * rank, points_ref, 0, 0, groups * rank,
-            group_mask(group_ref, half + 3, m, rank), (kah_ref, kal_ref), m * rank, rank,
+            wide_ref, m * rank, points_ref, 0, lane, groups * rank - lane, mask[:, lane:],
+            (kah_ref, kal_ref), m * rank, rank, lane,
         )
 
 
-def second_image(part_ref, group_ref, kah_ref, kal_ref, ubh_ref, ubl_ref):
+def second_image(part_ref, group_ref, kgh_ref, kgl_ref, ubh_ref, ubl_ref, rows_ref, pairs):
     leaves, double, leaf = ubh_ref.shape
     rank = double // 2
     subs = lax.axis_size("sub")
-    size = group_ref.shape[1] - SHARES
+    groups, half, _ = rows_ref.shape
+    size = half // subs
     mine = lax.axis_index("leaf")
-    pieces = []
-    for m in exchange_order(group_ref.shape[0] // subs):
-        at = (mine ^ m) * subs
-        pieces.append(jnp.concatenate([group_ref[at + k, 0:size, :] for k in range(subs)], axis=0))
-    held = jnp.concatenate(
-        [
-            jnp.concatenate([x[:, lane : lane + rank] for x in pieces], axis=1)
-            for lane in (0, rank)
-        ],
-        axis=0,
-    )
-    far = product(stacked(held), kah_ref[...], kal_ref[...], True)
-    group_stack = stacked(far[:, :rank])
+    for place, m in enumerate(exchange_order(groups)):
+        for row in range(half):
+            lane = row % size * LANE
+            rows_ref[place, row : row + 1, :] = group_ref[
+                (mine ^ m) * subs + row // size, :, lane : lane + LANE
+            ]
+    held = group_row(rows_ref, half, rank, leaves)
+    stack = stacked(held)
+    far = product(stack, kgh_ref[...], kgl_ref[...], True)
+    group_stack = stacked(far)
     second = [
         part_ref[:, i * leaf : (i + 1) * leaf]
         + product(group_stack, ubh_ref[i, rank:, :], ubl_ref[i, rank:, :])
         for i in range(leaves)
     ]
-    return second, row_sum((DOWN * held[:, : far.shape[1]]) * far)
+    if not pairs:
+        return second, row_sum((DOWN * held[:, :rank]) * far)
+    ahead = product(stack, *(ref[...] for ref in pairs))
+    return second, row_sum((2.0 * DOWN * held) * ahead)
 
 
 def update(group_ref, share, vec_ref, first_ref, second, solution_ref, residual_ref):
-    total = group_ref[0]
+    probes = vec_ref.shape[0]
+    start = group_ref.shape[2] - SHARES * probes
+    total = group_ref[0, :, start:]
     for q in range(1, group_ref.shape[0]):
-        total = total + group_ref[q]
-    sums = total.T[0 : vec_ref.shape[0]]
-    at = group_ref.shape[1] - SHARES
-    bb, bw, ww, wv = (sums[:, at + k : at + k + 1] for k in range(SHARES))
+        total = total + group_ref[q, :, start:]
+    pieces = [total[:, at : at + probes] for at in range(0, SHARES * probes, probes)]
+    sums = padded_lanes(padded_rows(jnp.concatenate(pieces, axis=0), EXTRA), LANE).T
+    bb, bw, ww, wv = (sums[0:probes, k : k + 1] for k in range(SHARES))
     wv = wv + share
     step = bb / bw
     rise = (step * ww) * step
@@ -527,15 +549,21 @@
 
 
 def final_kernel(
-    part_ref, group_ref, kah_ref, kal_ref, ubh_ref, ubl_ref, vec_ref, first_ref,
-    solution_ref, residual_ref,
-):
-    second, share = second_image(part_ref, group_ref, kah_ref, kal_ref, ubh_ref, ubl_ref)
+    part_ref, group_ref, kgh_ref, kgl_ref, kah_ref, kal_ref, ubh_ref, ubl_ref, vec_ref,
+    first_ref, solution_ref, residual_ref, rows_ref,
+):
+    second, share = second_image(
+        part_ref, group_ref, kgh_ref, kgl_ref, ubh_ref, ubl_ref, rows_ref, (kah_ref, kal_ref)
+    )
     update(group_ref, share, vec_ref, first_ref, second, solution_ref, residual_ref)
 
 
-def last_kernel(part_ref, group_ref, kah_ref, kal_ref, ubh_ref, ubl_ref, second_ref, share_ref):
-    second, share = second_image(part_ref, group_ref, kah_ref, kal_ref, ubh_ref, ubl_ref)
+def last_kernel(
+    part_ref, group_ref, kgh_ref, kgl_ref, ubh_ref, ubl_ref, second_ref, share_ref, rows_ref
+):
+    second, share = second_image(
+        part_ref, group_ref, kgh_ref, kgl_ref, ubh_ref, ubl_ref, rows_ref, None
+    )
     second_ref[...] = jnp.concatenate(second, axis=1)
     share_ref[...] = jnp.broadcast_to(share, share_ref.shape)
 
@@ -619,16 +647,15 @@
     subs = lax.axis_size("sub")
     half = REACH * leaf
     span = leaves * rank
-    base = span + LANE
     inside, across = window_tiles(leaves)
     transfer = leaf_transfer.reshape(span, rank)
     device = device_transfer[0]
 
-    m1, own, m4, rhs, points, basis, transfer, device, near, far = call(
+    m1, own, m4, rhs, points, basis, transfer, device, near, far, group_rows = call(
         first_kernel,
         [
-            shape(probes + EXTRA, base + half),
-            shape(probes + EXTRA, base),
+            shape(probes + 2 * EXTRA, span + half),
+            shape(probes + 2 * EXTRA, span),
             shape(probes + EXTRA, half),
             shape(probes, count),
             shape(EXTRA, count),
@@ -637,6 +664,7 @@
             shape(rank, rank),
             shape(*near_list.shape, dtype=jnp.int32),
             shape(*far_leaf_list.shape, dtype=jnp.int32),
+            shape(EXTRA, LANE),
         ],
         far_memory(
             far_group_list, probe_rhs, coords, leaf_skeleton, group_skeleton, leaf_basis,
@@ -650,7 +678,7 @@
     th, tl = call(
         prepare_kernel, pair(len(inside) * leaf, leaf), (near, points), scratch=[(3, count, LANE)]
     )
-    (term,) = call(term_kernel, [shape(probes // 2 + EXTRA, LANE)], (own, r1, r2, r3))
+    (term,) = call(term_kernel, [shape(probes // 2 + EXTRA, LANE)], (own, r1, r2, r3, group_rows))
     gathered = spread_groups(term)
     klh, kll = call(
         skeleton_kernel,
@@ -678,12 +706,14 @@
     )
     r4 = sides(m4)
     m1, own = call(
-        second_kernel, [shape(probes, base + half), shape(probes, base)], (image, ubh, ubl)
+        second_kernel,
+        [shape(probes + EXTRA, span + half), shape(probes + EXTRA, span)],
+        (image, ubh, ubl),
     )
     r1, r2, r3 = swap(m1, "sub", 1), swap(own, "sub", 2), swap(own, "sub", 3)
     dense = groups * rank <= DENSE
     if dense:
-        kgh, kgl = call(
+        kah, kal = call(
             groups_kernel,
             pair(groups * rank, groups * rank),
             (gathered,),
@@ -694,18 +724,24 @@
         local_kernel,
         [
             shape(probes, count),
-            shape(groups * subs, probes // 2 // subs + SHARES, LANE),
+            shape(groups * subs, 1, probes // 2 // subs * LANE + SHARES * probes),
         ],
         (rhs, image, inner, own, r1, r2, r3, r4, hh, hl, klh, kll, ubh, ubl),
     )
     gathered = lax.all_to_all(message, ("leaf", "sub"), 0, 0)
     outs = [shape(probes, count), shape(probes, count)]
     if dense:
-        return call(final_kernel, outs, (part, gathered, kgh, kgl, ubh, ubl, rhs, image))
+        return call(
+            final_kernel,
+            outs,
+            (part, gathered, kgh, kgl, kah, kal, ubh, ubl, rhs, image),
+            scratch=[(groups, probes // 2, LANE)],
+        )
     second, share = call(
         last_kernel,
         [shape(probes, count), shape(probes, LANE)],
         (part, gathered, kgh, kgl, ubh, ubl),
+        scratch=[(groups, probes // 2, LANE)],
     )
     share = lax.psum(share, "leaf")
     return call(update_kernel, outs, (gathered, share, rhs, image, second))

time: 54.5 us -> 52.9 us (0.971)
  waiting for transfers between devices: 17.2 us -> 16 us
  Pallas kernels: 16.9 us -> 16.3 us
    ppermute x9, waiting for transfers between devices: 10.1 us -> 9.18 us  [swap(): lax.ppermute(x, axis, [(i, i ^ m) for i in range(lax.axis_size(axis))])]
    pallas_call x14, Pallas kernels: 16.9 us -> 16.3 us  [call(): pl.pallas_call(kernel, out_shape=tuple(outs), in_specs=smem(scalars) + vm...]
where the time goes in v5:
time: 52.9 us; the launch traced here: 52.7 us
  starting transfers between devices  19.6 us (37%)
  Pallas kernels  16.3 us (31%)
  waiting for transfers between devices  16 us (30%)
  between operations  0.76 us (1%)
    pallas_call x14, Pallas kernels, call(): pl.pallas_call(kernel, out_shape=tuple(outs), in_specs=smem(scalars) + vm...  16.3 us
    ppermute x9, starting transfers between devices, swap(): lax.ppermute(x, axis, [(i, i ^ m) for i in range(lax.axis_size(axis))])  13.1 us
    ppermute x9, waiting for transfers between devices, swap(): lax.ppermute(x, axis, [(i, i ^ m) for i in range(lax.axis_size(axis))])  9.18 us
    all_to_all x1, waiting for transfers between devices, shards(): gathered = lax.all_to_all(message, ('leaf', 'sub'), 0, 0)  6.81 us
    all_to_all x1, starting transfers between devices, shards(): gathered = lax.all_to_all(message, ('leaf', 'sub'), 0, 0)  5.16 us
    ppermute x2, starting transfers between devices, sides(): return lax.ppermute(m4, ('leaf', 'sub'), across)  1.31 us
  transfers between devices with their start and end apart: 12, of which 7 were waited for; matrix products, arithmetic and copies ran while one was open for 0% of the time, Pallas kernels for 19%

profile of v5, /device:TPU:0, one launch (start us, length us, event | category | flops | bytes accessed | tf_op | source)
XLA Modules:
  0.0 52.7 jit_solution(17115513025897217499)
XLA Ops:
  0.6 1.9 %shard_map.113 = (f32[48,768]{1,0:T(8,128)S(1)}, f32[48,256]{1,0:T(8,128)S(1)}, f32[40,512]{1,0:T(8,128)S(1)}, f32[32,1024]{1,0:T(8,128)S(1)}, f32[8,1024]{1,0:T...) custom-call(s32[1,14]{1,0:T(1,128)} %list_ref.1, ...), custom_call_target="tpu_custom_call" | custom-call | bytes 1000000 | tf_op jit(solution)/shard_map/pallas_call | solution.py:597
  2.5 0.5 %collective-permute-start = (f32[48,768]{1,0:T(8,128)S(1)}, f32[48,768]{1,0:T(8,128)S(1)}, u32[]{:S(2)}, u32[]{:S(2)}) collective-permute-start(f32[48,768]{1,0:T(8,128)S(1)} %get-tuple-element.37), channel_id=1, source_target_pairs={{0,1},{1,0},{2,3},{3,2},{4,5},{5,4},{6,7},{7,6},{8,9},{9,8},{10,11... | collective-permute-start | bytes 442376 | tf_op jit(solution)/shard_map/ppermute | solution.py:611
  3.1 2.6 %collective-permute-start.1 = (f32[48,256]{1,0:T(8,128)S(1)}, f32[48,256]{1,0:T(8,128)S(1)}, u32[]{:S(2)}, u32[]{:S(2)}) collective-permute-start(f32[48,256]{1,0:T(8,128)S(1)} %get-tuple-element.36.own), channel_id=1, source_target_pairs={{0,2},{1,3},{2,0},{3,1},{4,6},{5,7},{6,4},{7,5},{8,10},{9,11},{10,... | collective-permute-start | bytes 147464 | tf_op jit(solution)/shard_map/ppermute | solution.py:611
  5.6 0.0 collective-permute-start.2
  5.7 2.3 %collective-permute-done.1.r2 = f32[48,256]{1,0:T(8,128)S(1)} collective-permute-done((f32[48,256]{1,0:T(8,128)S(1)}, f32[48,256]{1,0:T(8,128)S(1)}, u32[]{:S(2)}, u32[]{:S(2)}) %collective-permute-start.1) | collective-permute-done | bytes 49184 | tf_op jit(solution)/shard_map/ppermute | solution.py:611
  8.0 1.4 %collective-permute-done.2.r3 = f32[48,256]{1,0:T(8,128)S(1)} collective-permute-done((f32[48,256]{1,0:T(8,128)S(1)}, f32[48,256]{1,0:T(8,128)S(1)}, u32[]{:S(2)}, u32[]{:S(2)}) %collective-permute-start.2) | collective-permute-done | bytes 49184 | tf_op jit(solution)/shard_map/ppermute | solution.py:611
  9.4 2.7 %collective-permute-start.4 = (f32[1,24,128]{2,1,0:T(8,128)S(1)}, f32[1,24,128]{2,1,0:T(8,128)S(1)}, u32[]{:S(2)}, u32[]{:S(2)}) collective-permute-start(f32[1,24,128]{2,1,0:T(8,128)S(1)} %bitcast.3), channel_id=1, source_target_pairs={{0,16},{4,20},{8,24},{12,28},{16,0},{20,4},{24,8},{28,12},{1,17},{... | collective-permute-start | bytes 36872 | tf_op jit(solution)/shard_map/ppermute | solution.py:611
  12.0 2.0 %collective-permute-done.4 = f32[1,24,128]{2,1,0:T(8,128)S(1)} collective-permute-done((f32[1,24,128]{2,1,0:T(8,128)S(1)}, f32[1,24,128]{2,1,0:T(8,128)S(1)}, u32[]{:S(2)}, u32[]{:S(2)}) %collective-permute-start.4) | collective-permute-done | bytes 12320 | tf_op jit(solution)/shard_map/ppermute | solution.py:611
  14.0 1.6 %collective-permute-start.5 = (f32[2,24,128]{2,1,0:T(8,128)S(1)}, f32[2,24,128]{2,1,0:T(8,128)S(1)}, u32[]{:S(2)}, u32[]{:S(2)}) collective-permute-start(f32[2,24,128]{2,1,0:T(8,128)S(1)} %pad_maximum_fusion.2), channel_id=1, source_target_pairs={{0,8},{4,12},{8,0},{12,4},{16,24},{20,28},{24,16},{28,20},{1,9},{5... | collective-permute-start | bytes 73736 | tf_op jit(solution)/shard_map/ppermute | solution.py:611
  15.6 0.7 %collective-permute-start.3 = (f32[40,512]{1,0:T(8,128)S(1)}, f32[40,512]{1,0:T(8,128)S(1)}, u32[]{:S(2)}, u32[]{:S(2)}) collective-permute-start(f32[40,512]{1,0:T(8,128)S(1)} %get-tuple-element.38), channel_id=1, source_target_pairs={{1,2},{3,4},{5,6},{7,8},{9,10},{11,12},{13,14},{15,16},{17,18},{19... | collective-permute-start | bytes 245768 | tf_op jit(solution)/shard_map/ppermute | solution.py:618
  16.3 1.6 %collective-permute-done.5 = f32[2,24,128]{2,1,0:T(8,128)S(1)} collective-permute-done((f32[2,24,128]{2,1,0:T(8,128)S(1)}, f32[2,24,128]{2,1,0:T(8,128)S(1)}, u32[]{:S(2)}, u32[]{:S(2)}) %collective-permute-start.5) | collective-permute-done | bytes 24608 | tf_op jit(solution)/shard_map/ppermute | solution.py:611
  17.9 1.5 %collective-permute-start.6 = (f32[4,24,128]{2,1,0:T(8,128)S(1)}, f32[4,24,128]{2,1,0:T(8,128)S(1)}, u32[]{:S(2)}, u32[]{:S(2)}) collective-permute-start(f32[4,24,128]{2,1,0:T(8,128)S(1)} %pad_maximum_fusion.1), channel_id=1, source_target_pairs={{0,4},{4,0},{8,12},{12,8},{16,20},{20,16},{24,28},{28,24},{1,5},{5... | collective-permute-start | bytes 147464 | tf_op jit(solution)/shard_map/ppermute | solution.py:611
  19.4 2.8 %shard_map.114 = (bf16[2304,256]{1,0:T(8,128)(2,1)S(1)}, bf16[2304,256]{1,0:T(8,128)(2,1)S(1)}) custom-call(s32[4,5]{1,0:T(4,128)S(1)} %get-tuple-element.32.near_ref, f32[8,1024]{1,0:T(8,128)S(1)} %get-tuple-element.33.points_ref), custom_call_target="tpu_custom_call" | custom-call | bytes 1000000 | tf_op jit(solution)/shard_map/pallas_call | solution.py:597
  22.2 0.9 %shard_map.115.inner_ref = f32[32,1024]{1,0:T(8,128)S(1)} custom-call(f32[32,1024]{1,0:T(8,128)S(1)} %get-tuple-element.31.vec_ref.rhs_ref, bf16[2304,256]{1,0:T(8,128)(2,1)S(1)} %get-tuple-element.34.th_ref, bf16[2304,256]{1,0:T(8,128)(2,1)S(1)} %get-tuple-element.35.tl_ref), custom_call_target="tpu_custom_call" | custom-call | bytes 1000000 | tf_op jit(solution)/shard_map/pallas_call | solution.py:597
  23.1 0.8 %shard_map.118 = (bf16[4,128,256]{2,1,0:T(8,128)(2,1)S(1)}, bf16[4,128,256]{2,1,0:T(8,128)(2,1)S(1)}) custom-call(f32[4,64,256]{2,1,0:T(8,128)S(1)} %get-tuple-element.44.basis_ref, f32[256,64]{1,0:T(8,128)S(1)} %get-tuple-element.45.transfer_ref, f32[64,64]{1,0:T(8,128)S(1)} %get-tuple-element.46.device_ref), custom_call_target="tpu_custom_call" | custom-call | bytes 1000000 | tf_op jit(solution)/shard_map/pallas_call | solution.py:597
  23.9 2.2 %shard_map.116 = (bf16[1536,256]{1,0:T(8,128)(2,1)S(1)}, bf16[1536,256]{1,0:T(8,128)(2,1)S(1)}) custom-call(s32[4,5]{1,0:T(4,128)S(1)} %get-tuple-element.32.near_ref, f32[48,768]{1,0:T(8,128)S(1)} %collective-permute-done.r1, f32[40,512]{1,0:T(8,128)S(1)} %collective-permute-done.3.r4, f32[8,1024]{1,0:T(8,128)S(1)} %get-tuple-element.33.points_ref), custom_call_target="tpu_custom_call" | custom-call | bytes 1000000 | tf_op jit(solution)/shard_map/pallas_call | solution.py:597
  26.1 1.2 %shard_map.117 = (bf16[1024,256]{1,0:T(8,128)(2,1)S(1)}, bf16[1024,256]{1,0:T(8,128)(2,1)S(1)}) custom-call(s32[4,8]{1,0:T(4,128)S(1)} %get-tuple-element.41.far_ref, f32[48,256]{1,0:T(8,128)S(1)} %get-tuple-element.36.own, f32[48,768]{1,0:T(8,128)S(1)} %collective-permute-done.r1, f32[48,256]{1,0:T(8,128)S(1)} %collective-permute-done.1.r2, ...), custom_call_target="tpu_custom_call" | custom-call | bytes 1000000 | tf_op jit(solution)/shard_map/pallas_call | solution.py:597
  27.3 0.7 %shard_map.119.part_ref = f32[32,1024]{1,0:T(8,128)S(1)} custom-call(f32[32,1024]{1,0:T(8,128)S(1)} %shard_map.115.inner_ref, f32[48,256]{1,0:T(8,128)S(1)} %get-tuple-element.36.own, f32[48,768]{1,0:T(8,128)S(1)} %collective-permute-done.r1, f32[48,256]{1,0:T(8,128)S(1)} %collective-permute-done.1.r2, f32[48,256]{1,0:T(8,128)S(1)} %collective-permute-done.2.r3, ...), custom_call_target="tpu_custom_call" | custom-call | bytes 1000000 | tf_op jit(solution)/shard_map/pallas_call | solution.py:597
  28.0 0.6 %shard_map.121 = (f32[32,1024]{1,0:T(8,128)S(1)}, bf16[64,512]{1,0:T(8,128)(2,1)S(1)}, bf16[64,512]{1,0:T(8,128)(2,1)S(1)}, f32[32,512]{1,0:T(8,128)S(1)}) custom-call(f32[32,1024]{1,0:T(8,128)S(1)} %shard_map.119.part_ref, f32[8,24,128]{2,1,0:T(8,128)S(1)} %pad_maximum_fusion.group_ref, bf16[4,128,256]{2,1,0:T(8,128)(2,1)S(1)} %get-tuple-element.47.ubh_ref, ...), custom_call_target="tpu_custom_call" | custom-call | bytes 1000000 | tf_op jit(solution)/shard_map/pallas_call | solution.py:597
  28.7 0.3 shard_map.123
  29.0 0.5 collective-permute-start.7
  29.5 0.7 %collective-permute-start.10 = (f32[32,512]{1,0:T(8,128)S(1)}, f32[32,512]{1,0:T(8,128)S(1)}, u32[]{:S(2)}, u32[]{:S(2)}) collective-permute-start(f32[32,512]{1,0:T(8,128)S(1)} %get-tuple-element.53), channel_id=1, source_target_pairs={{1,2},{3,4},{5,6},{7,8},{9,10},{11,12},{13,14},{15,16},{17,18},{19... | collective-permute-start | bytes 196616 | tf_op jit(solution)/shard_map/ppermute | solution.py:618
  30.2 3.0 %collective-permute-start.8 = (f32[40,256]{1,0:T(8,128)S(1)}, f32[40,256]{1,0:T(8,128)S(1)}, u32[]{:S(2)}, u32[]{:S(2)}) collective-permute-start(f32[40,256]{1,0:T(8,128)S(1)} %get-tuple-element.51.own), channel_id=1, source_target_pairs={{0,2},{1,3},{2,0},{3,1},{4,6},{5,7},{6,4},{7,5},{8,10},{9,11},{10,... | collective-permute-start | bytes 122888 | tf_op jit(solution)/shard_map/ppermute | solution.py:611
  33.1 0.8 %collective-permute-start.9 = (f32[40,256]{1,0:T(8,128)S(1)}, f32[40,256]{1,0:T(8,128)S(1)}, u32[]{:S(2)}, u32[]{:S(2)}) collective-permute-start(f32[40,256]{1,0:T(8,128)S(1)} %get-tuple-element.51.own), channel_id=1, source_target_pairs={{0,3},{1,2},{2,1},{3,0},{4,7},{5,6},{6,5},{7,4},{8,11},{9,10},{10,... | collective-permute-start | bytes 122888 | tf_op jit(solution)/shard_map/ppermute | solution.py:611
  33.9 0.9 %shard_map.122.inner_ref = f32[32,1024]{1,0:T(8,128)S(1)} custom-call(f32[32,1024]{1,0:T(8,128)S(1)} %get-tuple-element.50.vec_ref.first_ref, bf16[2304,256]{1,0:T(8,128)(2,1)S(1)} %get-tuple-element.34.th_ref, bf16[2304,256]{1,0:T(8,128)(2,1)S(1)} %get-tuple-element.35.tl_ref), custom_call_target="tpu_custom_call" | custom-call | bytes 1000000 | tf_op jit(solution)/shard_map/pallas_call | solution.py:597
  34.8 1.4 %collective-permute-done.8.r2 = f32[40,256]{1,0:T(8,128)S(1)} collective-permute-done((f32[40,256]{1,0:T(8,128)S(1)}, f32[40,256]{1,0:T(8,128)S(1)}, u32[]{:S(2)}, u32[]{:S(2)}) %collective-permute-start.8) | collective-permute-done | bytes 40992 | tf_op jit(solution)/shard_map/ppermute | solution.py:611
  36.2 0.5 collective-permute-done.9.r3
  36.7 1.6 %shard_map.124 = (f32[32,1024]{1,0:T(8,128)S(1)}, f32[32,1,640]{2,1,0:T(1,128)}) custom-call(f32[32,1024]{1,0:T(8,128)S(1)} %get-tuple-element.31.vec_ref.rhs_ref, f32[32,1024]{1,0:T(8,128)S(1)} %get-tuple-element.50.vec_ref.first_ref, f32[32,1024]{1,0:T(8,128)S(1)} %shard_map.122.inner_ref, f32[40,256]{1,0:T(8,128)S(1)} %get-tuple-element.51.own, ...), custom_call_target="tpu_custom_call" | custom-call | bytes 1000000 | tf_op jit(solution)/shard_map/pallas_call | solution.py:597
  38.3 5.2 %all-to-all-start = ((f32[32,1,640]{2,1,0:T(1,128)}), f32[32,1,640]{2,1,0:T(1,128)S(1)}, u32[]{:S(2)}, u32[]{:S(2)}) async-start(f32[32,1,640]{2,1,0:T(1,128)} %get-tuple-element.55), calls=%async_computation | async-start | bytes 163840 | tf_op jit(solution)/shard_map/all_to_all | solution.py:731
  43.5 0.8 %shard_map.125 = (bf16[512,512]{1,0:T(8,128)(2,1)S(1)}, bf16[512,512]{1,0:T(8,128)(2,1)S(1)}) custom-call(f32[8,24,128]{2,1,0:T(8,128)S(1)} %pad_maximum_fusion.group_ref), custom_call_target="tpu_custom_call" | custom-call | bytes 1000000 | tf_op jit(solution)/shard_map/pallas_call | solution.py:597
  44.3 6.8 %all-to-all-done.group_ref = f32[32,1,640]{2,1,0:T(1,128)S(1)} async-done(((f32[32,1,640]{2,1,0:T(1,128)}), f32[32,1,640]{2,1,0:T(1,128)S(1)}, u32[]{:S(2)}, u32[]{:S(2)}) %all-to-all-start) | async-done | bytes 81952 | tf_op jit(solution)/shard_map/all_to_all | solution.py:731
  51.1 1.6 %shard_map.126 = (f32[32,1024]{1,0:T(8,128)}, f32[32,1024]{1,0:T(8,128)}) custom-call(f32[32,1024]{1,0:T(8,128)S(1)} %get-tuple-element.54.part_ref, f32[32,1,640]{2,1,0:T(1,128)S(1)} %all-to-all-done.group_ref, bf16[64,512]{1,0:T(8,128)(2,1)S(1)} %get-tuple-element.56.kgh_ref, bf16[64,512]{1,0:T(8,128)(2,1)S(1)} %get-tuple-element.57.kgl_ref, ...), custom_call_target="tpu_custom_call" | custom-call | bytes 1000000 | tf_op jit(solution)/shard_map/pallas_call | solution.py:597
  (9 shorter events, 0.0 us)
Async XLA Ops:
  2.5 6.8 %collective-permute-start = (f32[48,768]{1,0:T(8,128)S(1)}, f32[48,768]{1,0:T(8,128)S(1)}, u32[]{:S(2)}, u32[]{:S(2)}) collective-permute-start(f32[48,768]{1,0:T(8,128)S(1)} %get-tuple-element.37), channel_id=1, source_target_pairs={{0,1},{1,0},{2,3},{3,2},{4,5},{5,4},{6,7},{7,6},{8,9},{9,8},{10,11... | collective-permute-start | bytes 442376 | tf_op jit(solution)/shard_map/ppermute | solution.py:611
  3.1 4.9 %collective-permute-start.1 = (f32[48,256]{1,0:T(8,128)S(1)}, f32[48,256]{1,0:T(8,128)S(1)}, u32[]{:S(2)}, u32[]{:S(2)}) collective-permute-start(f32[48,256]{1,0:T(8,128)S(1)} %get-tuple-element.36.own), channel_id=1, source_target_pairs={{0,2},{1,3},{2,0},{3,1},{4,6},{5,7},{6,4},{7,5},{8,10},{9,11},{10,... | collective-permute-start | bytes 147464 | tf_op jit(solution)/shard_map/ppermute | solution.py:611
  5.6 3.7 %collective-permute-start.2 = (f32[48,256]{1,0:T(8,128)S(1)}, f32[48,256]{1,0:T(8,128)S(1)}, u32[]{:S(2)}, u32[]{:S(2)}) collective-permute-start(f32[48,256]{1,0:T(8,128)S(1)} %get-tuple-element.36.own), channel_id=1, source_target_pairs={{0,3},{1,2},{2,1},{3,0},{4,7},{5,6},{6,5},{7,4},{8,11},{9,10},{10,... | collective-permute-start | bytes 147464 | tf_op jit(solution)/shard_map/ppermute | solution.py:611
  9.4 4.7 %collective-permute-start.4 = (f32[1,24,128]{2,1,0:T(8,128)S(1)}, f32[1,24,128]{2,1,0:T(8,128)S(1)}, u32[]{:S(2)}, u32[]{:S(2)}) collective-permute-start(f32[1,24,128]{2,1,0:T(8,128)S(1)} %bitcast.3), channel_id=1, source_target_pairs={{0,16},{4,20},{8,24},{12,28},{16,0},{20,4},{24,8},{28,12},{1,17},{... | collective-permute-start | bytes 36872 | tf_op jit(solution)/shard_map/ppermute | solution.py:611
  14.0 3.8 %collective-permute-start.5 = (f32[2,24,128]{2,1,0:T(8,128)S(1)}, f32[2,24,128]{2,1,0:T(8,128)S(1)}, u32[]{:S(2)}, u32[]{:S(2)}) collective-permute-start(f32[2,24,128]{2,1,0:T(8,128)S(1)} %pad_maximum_fusion.2), channel_id=1, source_target_pairs={{0,8},{4,12},{8,0},{12,4},{16,24},{20,28},{24,16},{28,20},{1,9},{5... | collective-permute-start | bytes 73736 | tf_op jit(solution)/shard_map/ppermute | solution.py:611
  15.6 8.3 %collective-permute-start.3 = (f32[40,512]{1,0:T(8,128)S(1)}, f32[40,512]{1,0:T(8,128)S(1)}, u32[]{:S(2)}, u32[]{:S(2)}) collective-permute-start(f32[40,512]{1,0:T(8,128)S(1)} %get-tuple-element.38), channel_id=1, source_target_pairs={{1,2},{3,4},{5,6},{7,8},{9,10},{11,12},{13,14},{15,16},{17,18},{19... | collective-permute-start | bytes 245768 | tf_op jit(solution)/shard_map/ppermute | solution.py:618
  17.9 10.1 %collective-permute-start.6 = (f32[4,24,128]{2,1,0:T(8,128)S(1)}, f32[4,24,128]{2,1,0:T(8,128)S(1)}, u32[]{:S(2)}, u32[]{:S(2)}) collective-permute-start(f32[4,24,128]{2,1,0:T(8,128)S(1)} %pad_maximum_fusion.1), channel_id=1, source_target_pairs={{0,4},{4,0},{8,12},{12,8},{16,20},{20,16},{24,28},{28,24},{1,5},{5... | collective-permute-start | bytes 147464 | tf_op jit(solution)/shard_map/ppermute | solution.py:611
  29.0 7.7 %collective-permute-start.7 = (f32[40,768]{1,0:T(8,128)S(1)}, f32[40,768]{1,0:T(8,128)S(1)}, u32[]{:S(2)}, u32[]{:S(2)}) collective-permute-start(f32[40,768]{1,0:T(8,128)S(1)} %get-tuple-element.52), channel_id=1, source_target_pairs={{0,1},{1,0},{2,3},{3,2},{4,5},{5,4},{6,7},{7,6},{8,9},{9,8},{10,11... | collective-permute-start | bytes 368648 | tf_op jit(solution)/shard_map/ppermute | solution.py:611
  29.5 7.2 %collective-permute-start.10 = (f32[32,512]{1,0:T(8,128)S(1)}, f32[32,512]{1,0:T(8,128)S(1)}, u32[]{:S(2)}, u32[]{:S(2)}) collective-permute-start(f32[32,512]{1,0:T(8,128)S(1)} %get-tuple-element.53), channel_id=1, source_target_pairs={{1,2},{3,4},{5,6},{7,8},{9,10},{11,12},{13,14},{15,16},{17,18},{19... | collective-permute-start | bytes 196616 | tf_op jit(solution)/shard_map/ppermute | solution.py:618
  30.2 6.0 %collective-permute-start.8 = (f32[40,256]{1,0:T(8,128)S(1)}, f32[40,256]{1,0:T(8,128)S(1)}, u32[]{:S(2)}, u32[]{:S(2)}) collective-permute-start(f32[40,256]{1,0:T(8,128)S(1)} %get-tuple-element.51.own), channel_id=1, source_target_pairs={{0,2},{1,3},{2,0},{3,1},{4,6},{5,7},{6,4},{7,5},{8,10},{9,11},{10,... | collective-permute-start | bytes 122888 | tf_op jit(solution)/shard_map/ppermute | solution.py:611
  33.1 3.6 %collective-permute-start.9 = (f32[40,256]{1,0:T(8,128)S(1)}, f32[40,256]{1,0:T(8,128)S(1)}, u32[]{:S(2)}, u32[]{:S(2)}) collective-permute-start(f32[40,256]{1,0:T(8,128)S(1)} %get-tuple-element.51.own), channel_id=1, source_target_pairs={{0,3},{1,2},{2,1},{3,0},{4,7},{5,6},{6,5},{7,4},{8,11},{9,10},{10,... | collective-permute-start | bytes 122888 | tf_op jit(solution)/shard_map/ppermute | solution.py:611
  38.3 12.8 %all-to-all-start = ((f32[32,1,640]{2,1,0:T(1,128)}), f32[32,1,640]{2,1,0:T(1,128)S(1)}, u32[]{:S(2)}, u32[]{:S(2)}) async-start(f32[32,1,640]{2,1,0:T(1,128)} %get-tuple-element.55), calls=%async_computation | async-start | bytes 163840 | tf_op jit(solution)/shard_map/all_to_all | solution.py:731

commit v6 on v5

--- a/solution.py
+++ b/solution.py
@@ -17,7 +17,7 @@
 LANE = 128
 EXTRA = 8
 CHUNK = 32
-UNROLL = 1024
+UNROLL = 2048
 SHARES = 4
 GRANT = 16 * 2**20
 DENSE = 1024
@@ -68,6 +68,15 @@
     return jnp.max(jnp.where(columns == index, 1.0, 0.0).astype(F32), axis=0, keepdims=True)
 
 
+def near_weights(near_ref, first, pairs):
+    slots = slot_columns(near_ref)
+    listed = [
+        jnp.broadcast_to(slots[:, i : i + 1], (slots.shape[0], LANE))
+        for i in range(near_ref.shape[0])
+    ]
+    return [named(listed[i], first + j) for i, j in pairs]
+
+
 def padded_lanes(x, lanes):
     return jnp.concatenate(
         [x, jnp.zeros((x.shape[0], lanes - x.shape[1]), x.dtype)], axis=1
@@ -111,7 +120,10 @@
     half = REACH * leaf
     vec = vec_ref[...]
     coefs = jnp.concatenate(
-        [dot(vec[:, i * leaf : (i + 1) * leaf], basis_ref[i], 1, 1) for i in range(leaves)],
+        [
+            product(stacked(vec[:, i * leaf : (i + 1) * leaf]), *split(basis_ref[i]), True)
+            for i in range(leaves)
+        ],
         axis=1,
     )
     term = fold_rows(dot(dot(coefs, transfer_ref[...]), device_ref[...]), leaves)
@@ -195,24 +207,24 @@
     leaf = points_ref.shape[1] // leaves
     first = (lax.axis_index("leaf") * lax.axis_size("sub") + lax.axis_index("sub")) * leaves
     spread_columns(points_ref[...], wide_ref)
-    slots = slot_columns(near_ref)
-    for at, (i, j) in enumerate(window_tiles(leaves)[0]):
-        listed = jnp.broadcast_to(slots[:, i : i + 1], (slots.shape[0], LANE))
+    pairs = window_tiles(leaves)[0]
+    weights = near_weights(near_ref, first, pairs)
+    for at, (i, j) in enumerate(pairs):
         fill_tile(
-            wide_ref, j * leaf, points_ref, 0, i * leaf, leaf, named(listed, first + j),
+            wide_ref, j * leaf, points_ref, 0, i * leaf, leaf, weights[at],
             (th_ref, tl_ref), at * leaf, leaf,
         )
 
 
 def bases_kernel(basis_ref, transfer_ref, device_ref, ubh_ref, ubl_ref):
     leaves, rank, _ = basis_ref.shape
-    chain = dot(transfer_ref[...], device_ref[...])
+    chain = stacked(dot(device_ref[...], transfer_ref[...], 0, 1))
     for i in range(leaves):
-        basis = basis_ref[i]
-        group_basis = dot(chain[i * rank : (i + 1) * rank], basis, 0, 0)
-        top, rest = split(jnp.concatenate([basis, group_basis], axis=0))
-        ubh_ref[i] = top
-        ubl_ref[i] = rest
+        top, rest = split(basis_ref[i])
+        group_basis = product(chain[:, i * rank : (i + 1) * rank], top, rest)
+        group_top, group_rest = split(group_basis)
+        ubh_ref[i] = jnp.concatenate([top, group_top], axis=0)
+        ubl_ref[i] = jnp.concatenate([rest, group_rest], axis=0)
 
 
 def fold_rows(x, parts):
@@ -235,6 +247,22 @@
 
 def leaf_slice(x, i, leaf):
     return x[:, i * leaf : (i + 1) * leaf]
+
+
+def columns_of(shares, rows):
+    lane = lax.broadcasted_iota(jnp.int32, (rows, LANE), 1)
+    columns = jnp.zeros((rows, LANE), F32)
+    for at, share in enumerate(shares):
+        columns = jnp.where(lane == at, share, columns)
+    return columns
+
+
+def again_kernel(rhs_ref, vec_ref, th_ref, tl_ref, out_ref, columns_ref):
+    rhs = rhs_ref[...]
+    vec = vec_ref[...]
+    shares = row_sum(rhs * rhs), row_sum(rhs * vec), row_sum(vec * vec)
+    columns_ref[...] = columns_of(shares, vec.shape[0])
+    inner_kernel(vec_ref, th_ref, tl_ref, out_ref)
 
 
 def inner_kernel(vec_ref, th_ref, tl_ref, out_ref):
@@ -295,13 +323,13 @@
     )
     for m, message in enumerate(messages):
         spread_columns(message[top : top + EXTRA, 0:span], wide_ref.at[m])
-    for m in range(len(messages)):
-        for j in range(leaves):
-            index = group_first + (sub ^ m) * leaves + j
-            fill_tile(
-                wide_ref.at[m], j * rank, own, top, 0, span, named(listed, index),
-                (klh_ref, kll_ref), m * span + j * rank, rank,
-            )
+    places = [(m, j) for m in range(len(messages)) for j in range(leaves)]
+    masks = [named(listed, group_first + (sub ^ m) * leaves + j) for m, j in places]
+    for mask, (m, j) in zip(masks, places):
+        fill_tile(
+            wide_ref.at[m], j * rank, own, top, 0, span, mask,
+            (klh_ref, kll_ref), m * span + j * rank, rank,
+        )
 
 
 def border_kernel(near_ref, r1, r4, points_ref, hh_ref, hl_ref, ends_ref, wide_ref):
@@ -316,12 +344,12 @@
     ends_ref[:, 0:half] = low
     ends_ref[:, half:] = high
     spread_columns(ends_ref[...], wide_ref)
-    slots = slot_columns(near_ref)
-    for at, (i, j) in enumerate(window_tiles(leaves)[1]):
-        listed = jnp.broadcast_to(slots[:, i : i + 1], (slots.shape[0], LANE))
+    pairs = window_tiles(leaves)[1]
+    weights = near_weights(near_ref, first, pairs)
+    for at, (i, j) in enumerate(pairs):
         source = (j + REACH) * leaf if j < 0 else half + (j - leaves) * leaf
         fill_tile(
-            wide_ref, source, points_ref, 0, i * leaf, leaf, named(listed, first + j),
+            wide_ref, source, points_ref, 0, i * leaf, leaf, weights[at],
             (hh_ref, hl_ref), at * leaf, leaf,
         )
 
@@ -344,13 +372,12 @@
 
 
 def local_kernel(
-    rhs_ref, vec_ref, inner_ref, own, r1, r2, r3, r4, hh_ref, hl_ref, klh_ref, kll_ref,
+    columns_ref, vec_ref, inner_ref, own, r1, r2, r3, r4, hh_ref, hl_ref, klh_ref, kll_ref,
     ubh_ref, ubl_ref, part_ref, message_ref,
 ):
     base = own.shape[1]
     span = klh_ref.shape[1]
     rows = slice(0, vec_ref.shape[0])
-    rhs = rhs_ref[...]
     vec = vec_ref[...]
     low, high = halos(r1, r4[...], rows, base)
     blocks = [r[rows, 0:span] for r in (own, r1, r2, r3)]
@@ -358,16 +385,9 @@
         inner_ref, low, high, blocks,
         (hh_ref, hl_ref, klh_ref, kll_ref), (ubh_ref, ubl_ref), part_ref,
     )
-    shares = (
-        row_sum(rhs * rhs),
-        row_sum(rhs * vec),
-        row_sum(vec * vec),
-        row_sum((DOWN * vec) * near) + row_sum((DOWN * blocks[0]) * far),
-    )
-    lane = lax.broadcasted_iota(jnp.int32, (vec.shape[0], LANE), 1)
-    columns = jnp.zeros((vec.shape[0], LANE), F32)
-    for at, share in enumerate(shares):
-        columns = jnp.where(lane == at, share, columns)
+    share = row_sum((DOWN * vec) * near) + row_sum((DOWN * blocks[0]) * far)
+    lane = lax.broadcasted_iota(jnp.int32, columns_ref.shape, 1)
+    columns = jnp.where(lane == SHARES - 1, share, columns_ref[...])
     term = summed_terms((own, r1, r2, r3), vec.shape[0], span)
     size = term.shape[0] // lax.axis_size("sub")
     sub = lax.axis_index("sub")
@@ -390,6 +410,8 @@
 
 
 def exchange_rounds(groups):
+    if groups == 8:
+        return [[2, 4, 6], [1]]
     return [[groups >> n] for n in range(1, groups.bit_length())]
 
 
@@ -484,9 +506,9 @@
     spread_columns(points_ref[...], wide_ref)
     kah_ref[...] = jnp.zeros(kah_ref.shape, BF16)
     kal_ref[...] = jnp.zeros(kal_ref.shape, BF16)
-    for m in range(groups - 1):
+    masks = [group_mask(group_ref, half + 3, m, rank) for m in range(groups - 1)]
+    for m, mask in enumerate(masks):
         lane = (m + 1) * rank // LANE * LANE
-        mask = group_mask(group_ref, half + 3, m, rank)
         fill_tile(
             wide_ref, m * rank, points_ref, 0, lane, groups * rank - lane, mask[:, lane:],
             (kah_ref, kal_ref), m * rank, rank, lane,
@@ -719,14 +741,16 @@
             (gathered,),
             scratch=[(EXTRA, groups * rank), (3, groups * rank, LANE)],
         )
-    (inner,) = call(inner_kernel, [shape(probes, count)], (image, th, tl))
+    inner, columns = call(
+        again_kernel, [shape(probes, count), shape(probes, LANE)], (rhs, image, th, tl)
+    )
     part, message = call(
         local_kernel,
         [
             shape(probes, count),
             shape(groups * subs, 1, probes // 2 // subs * LANE + SHARES * probes),
         ],
-        (rhs, image, inner, own, r1, r2, r3, r4, hh, hl, klh, kll, ubh, ubl),
+        (columns, image, inner, own, r1, r2, r3, r4, hh, hl, klh, kll, ubh, ubl),
     )
     gathered = lax.all_to_all(message, ("leaf", "sub"), 0, 0)
     outs = [shape(probes, count), shape(probes, count)]

time: 52.9 us -> 50.2 us (0.949)
  Pallas kernels: 16.3 us -> 14.8 us
  waiting for transfers between devices: 16 us -> 15.1 us
    all_to_all x1, starting transfers between devices: 5.16 us -> 2.63 us  [shards(): gathered = lax.all_to_all(message, ('leaf', 'sub'), 0, 0)]
    ppermute x9 -> x10, starting transfers between devices: 13.1 us -> 15.3 us  [swap(): lax.ppermute(x, axis, [(i, i ^ m) for i in range(lax.axis_size(axis))])]
    pallas_call x14, Pallas kernels: 16.3 us -> 14.8 us  [call(): pl.pallas_call(kernel, out_shape=tuple(outs), in_specs=smem(scalars) + vm...]
    ppermute x9 -> x10, waiting for transfers between devices: 9.18 us -> 8.35 us  [swap(): lax.ppermute(x, axis, [(i, i ^ m) for i in range(lax.axis_size(axis))])]
  transfers between devices with their start and end apart: 12 -> 13, of which waited for: 7 -> 5; matrix products, arithmetic and copies ran while one was open for 0% -> 0% of each run, Pallas kernels for 19% -> 18%
where the time goes in v6:
time: 50.2 us; the launch traced here: 50 us
  starting transfers between devices  19.2 us (38%)
  waiting for transfers between devices  15.1 us (30%)
  Pallas kernels  14.8 us (29%)
  between operations  0.8 us (2%)
    ppermute x10, starting transfers between devices, swap(): lax.ppermute(x, axis, [(i, i ^ m) for i in range(lax.axis_size(axis))])  15.3 us
    pallas_call x14, Pallas kernels, call(): pl.pallas_call(kernel, out_shape=tuple(outs), in_specs=smem(scalars) + vm...  14.8 us
    ppermute x10, waiting for transfers between devices, swap(): lax.ppermute(x, axis, [(i, i ^ m) for i in range(lax.axis_size(axis))])  8.35 us
    all_to_all x1, waiting for transfers between devices, shards(): gathered = lax.all_to_all(message, ('leaf', 'sub'), 0, 0)  6.79 us
    all_to_all x1, starting transfers between devices, shards(): gathered = lax.all_to_all(message, ('leaf', 'sub'), 0, 0)  2.63 us
    ppermute x2, starting transfers between devices, sides(): return lax.ppermute(m4, ('leaf', 'sub'), across)  1.32 us
  transfers between devices with their start and end apart: 13, of which 5 were waited for; matrix products, arithmetic and copies ran while one was open for 0% of the time, Pallas kernels for 18%

profile of v6, /device:TPU:0, one launch (start us, length us, event | category | flops | bytes accessed | tf_op | source)
XLA Modules:
  0.0 50.0 jit_solution(4898700640277314805)
XLA Ops:
  0.6 1.8 %shard_map.113 = (f32[48,768]{1,0:T(8,128)S(1)}, f32[48,256]{1,0:T(8,128)S(1)}, f32[40,512]{1,0:T(8,128)S(1)}, f32[32,1024]{1,0:T(8,128)S(1)}, f32[8,1024]{1,0:T...) custom-call(s32[1,14]{1,0:T(1,128)} %list_ref.1, ...), custom_call_target="tpu_custom_call" | custom-call | bytes 1000000 | tf_op jit(solution)/shard_map/pallas_call | solution.py:619
  2.4 0.5 %collective-permute-start = (f32[48,768]{1,0:T(8,128)S(1)}, f32[48,768]{1,0:T(8,128)S(1)}, u32[]{:S(2)}, u32[]{:S(2)}) collective-permute-start(f32[48,768]{1,0:T(8,128)S(1)} %get-tuple-element.39), channel_id=1, source_target_pairs={{0,1},{1,0},{2,3},{3,2},{4,5},{5,4},{6,7},{7,6},{8,9},{9,8},{10,11... | collective-permute-start | bytes 442376 | tf_op jit(solution)/shard_map/ppermute | solution.py:633
  2.9 2.6 %collective-permute-start.1 = (f32[48,256]{1,0:T(8,128)S(1)}, f32[48,256]{1,0:T(8,128)S(1)}, u32[]{:S(2)}, u32[]{:S(2)}) collective-permute-start(f32[48,256]{1,0:T(8,128)S(1)} %get-tuple-element.38.own), channel_id=1, source_target_pairs={{0,2},{1,3},{2,0},{3,1},{4,6},{5,7},{6,4},{7,5},{8,10},{9,11},{10,... | collective-permute-start | bytes 147464 | tf_op jit(solution)/shard_map/ppermute | solution.py:633
  5.5 0.0 collective-permute-start.2
  5.5 0.7 %collective-permute-start.3 = (f32[40,512]{1,0:T(8,128)S(1)}, f32[40,512]{1,0:T(8,128)S(1)}, u32[]{:S(2)}, u32[]{:S(2)}) collective-permute-start(f32[40,512]{1,0:T(8,128)S(1)} %get-tuple-element.40), channel_id=1, source_target_pairs={{1,2},{3,4},{5,6},{7,8},{9,10},{11,12},{13,14},{15,16},{17,18},{19... | collective-permute-start | bytes 245768 | tf_op jit(solution)/shard_map/ppermute | solution.py:640
  6.2 2.1 %shard_map.114 = (bf16[2304,256]{1,0:T(8,128)(2,1)S(1)}, bf16[2304,256]{1,0:T(8,128)(2,1)S(1)}) custom-call(s32[4,5]{1,0:T(4,128)S(1)} %get-tuple-element.34.near_ref, f32[8,1024]{1,0:T(8,128)S(1)} %get-tuple-element.35.points_ref), custom_call_target="tpu_custom_call" | custom-call | bytes 1000000 | tf_op jit(solution)/shard_map/pallas_call | solution.py:619
  8.4 0.9 %shard_map.115.inner_ref = f32[32,1024]{1,0:T(8,128)S(1)} custom-call(f32[32,1024]{1,0:T(8,128)S(1)} %get-tuple-element.33.vec_ref.rhs_ref, bf16[2304,256]{1,0:T(8,128)(2,1)S(1)} %get-tuple-element.36.th_ref, bf16[2304,256]{1,0:T(8,128)(2,1)S(1)} %get-tuple-element.37.tl_ref), custom_call_target="tpu_custom_call" | custom-call | bytes 1000000 | tf_op jit(solution)/shard_map/pallas_call | solution.py:619
  9.2 0.7 %shard_map.118 = (bf16[4,128,256]{2,1,0:T(8,128)(2,1)S(1)}, bf16[4,128,256]{2,1,0:T(8,128)(2,1)S(1)}) custom-call(f32[4,64,256]{2,1,0:T(8,128)S(1)} %get-tuple-element.46.basis_ref, f32[256,64]{1,0:T(8,128)S(1)} %get-tuple-element.47.transfer_ref, f32[64,64]{1,0:T(8,128)S(1)} %get-tuple-element.48.device_ref), custom_call_target="tpu_custom_call" | custom-call | bytes 1000000 | tf_op jit(solution)/shard_map/pallas_call | solution.py:619
  9.9 0.0 collective-permute-done.1.r2
  10.0 0.0 collective-permute-done.2.r3
  10.0 5.4 %collective-permute-start.4 = (f32[1,24,128]{2,1,0:T(8,128)S(1)}, f32[1,24,128]{2,1,0:T(8,128)S(1)}, u32[]{:S(2)}, u32[]{:S(2)}) collective-permute-start(f32[1,24,128]{2,1,0:T(8,128)S(1)} %bitcast.4), channel_id=1, source_target_pairs={{0,8},{4,12},{8,0},{12,4},{16,24},{20,28},{24,16},{28,20},{1,9},{5... | collective-permute-start | bytes 36872 | tf_op jit(solution)/shard_map/ppermute | solution.py:633
  15.4 2.6 %collective-permute-start.5 = (f32[1,24,128]{2,1,0:T(8,128)S(1)}, f32[1,24,128]{2,1,0:T(8,128)S(1)}, u32[]{:S(2)}, u32[]{:S(2)}) collective-permute-start(f32[1,24,128]{2,1,0:T(8,128)S(1)} %bitcast.5), channel_id=1, source_target_pairs={{0,16},{4,20},{8,24},{12,28},{16,0},{20,4},{24,8},{28,12},{1,17},{... | collective-permute-start | bytes 36872 | tf_op jit(solution)/shard_map/ppermute | solution.py:633
  18.0 0.0 collective-permute-done.3.r4
  18.0 1.6 %shard_map.116 = (bf16[1536,256]{1,0:T(8,128)(2,1)S(1)}, bf16[1536,256]{1,0:T(8,128)(2,1)S(1)}) custom-call(s32[4,5]{1,0:T(4,128)S(1)} %get-tuple-element.34.near_ref, f32[48,768]{1,0:T(8,128)S(1)} %collective-permute-done.r1, f32[40,512]{1,0:T(8,128)S(1)} %collective-permute-done.3.r4, f32[8,1024]{1,0:T(8,128)S(1)} %get-tuple-element.35.points_ref), custom_call_target="tpu_custom_call" | custom-call | bytes 1000000 | tf_op jit(solution)/shard_map/pallas_call | solution.py:619
  19.6 1.2 %shard_map.117 = (bf16[1024,256]{1,0:T(8,128)(2,1)S(1)}, bf16[1024,256]{1,0:T(8,128)(2,1)S(1)}) custom-call(s32[4,8]{1,0:T(4,128)S(1)} %get-tuple-element.43.far_ref, f32[48,256]{1,0:T(8,128)S(1)} %get-tuple-element.38.own, f32[48,768]{1,0:T(8,128)S(1)} %collective-permute-done.r1, f32[48,256]{1,0:T(8,128)S(1)} %collective-permute-done.1.r2, ...), custom_call_target="tpu_custom_call" | custom-call | bytes 1000000 | tf_op jit(solution)/shard_map/pallas_call | solution.py:619
  20.8 0.7 %shard_map.119.part_ref = f32[32,1024]{1,0:T(8,128)S(1)} custom-call(f32[32,1024]{1,0:T(8,128)S(1)} %shard_map.115.inner_ref, f32[48,256]{1,0:T(8,128)S(1)} %get-tuple-element.38.own, f32[48,768]{1,0:T(8,128)S(1)} %collective-permute-done.r1, f32[48,256]{1,0:T(8,128)S(1)} %collective-permute-done.1.r2, f32[48,256]{1,0:T(8,128)S(1)} %collective-permute-done.2.r3, ...), custom_call_target="tpu_custom_call" | custom-call | bytes 1000000 | tf_op jit(solution)/shard_map/pallas_call | solution.py:619
  21.5 1.9 %collective-permute-done.6 = f32[1,24,128]{2,1,0:T(8,128)S(1)} collective-permute-done((f32[1,24,128]{2,1,0:T(8,128)S(1)}, f32[1,24,128]{2,1,0:T(8,128)S(1)}, u32[]{:S(2)}, u32[]{:S(2)}) %collective-permute-start.6) | collective-permute-done | bytes 12320 | tf_op jit(solution)/shard_map/ppermute | solution.py:633
  23.5 0.7 %collective-permute-start.7 = (f32[4,24,128]{2,1,0:T(8,128)S(1)}, f32[4,24,128]{2,1,0:T(8,128)S(1)}, u32[]{:S(2)}, u32[]{:S(2)}) collective-permute-start(f32[4,24,128]{2,1,0:T(8,128)S(1)} %pad_maximum_fusion), channel_id=1, source_target_pairs={{0,4},{4,0},{8,12},{12,8},{16,20},{20,16},{24,28},{28,24},{1,5},{5... | collective-permute-start | bytes 147464 | tf_op jit(solution)/shard_map/ppermute | solution.py:633
  24.2 3.4 %collective-permute-done.7 = f32[4,24,128]{2,1,0:T(8,128)S(1)} collective-permute-done((f32[4,24,128]{2,1,0:T(8,128)S(1)}, f32[4,24,128]{2,1,0:T(8,128)S(1)}, u32[]{:S(2)}, u32[]{:S(2)}) %collective-permute-start.7) | collective-permute-done | bytes 49184 | tf_op jit(solution)/shard_map/ppermute | solution.py:633
  27.6 0.6 %shard_map.121 = (f32[32,1024]{1,0:T(8,128)S(1)}, bf16[64,512]{1,0:T(8,128)(2,1)S(1)}, bf16[64,512]{1,0:T(8,128)(2,1)S(1)}, f32[32,512]{1,0:T(8,128)S(1)}) custom-call(f32[32,1024]{1,0:T(8,128)S(1)} %shard_map.119.part_ref, f32[8,24,128]{2,1,0:T(8,128)S(1)} %constant_dynamic-update-slice_fusion.group_ref, ...), custom_call_target="tpu_custom_call" | custom-call | bytes 1000000 | tf_op jit(solution)/shard_map/pallas_call | solution.py:619
  28.2 0.3 shard_map.123
  28.6 0.0 collective-permute-start.8
  28.6 0.7 %collective-permute-start.11 = (f32[32,512]{1,0:T(8,128)S(1)}, f32[32,512]{1,0:T(8,128)S(1)}, u32[]{:S(2)}, u32[]{:S(2)}) collective-permute-start(f32[32,512]{1,0:T(8,128)S(1)} %get-tuple-element.57), channel_id=1, source_target_pairs={{1,2},{3,4},{5,6},{7,8},{9,10},{11,12},{13,14},{15,16},{17,18},{19... | collective-permute-start | bytes 196616 | tf_op jit(solution)/shard_map/ppermute | solution.py:640
  29.3 3.4 %collective-permute-start.9 = (f32[40,256]{1,0:T(8,128)S(1)}, f32[40,256]{1,0:T(8,128)S(1)}, u32[]{:S(2)}, u32[]{:S(2)}) collective-permute-start(f32[40,256]{1,0:T(8,128)S(1)} %get-tuple-element.55.own), channel_id=1, source_target_pairs={{0,2},{1,3},{2,0},{3,1},{4,6},{5,7},{6,4},{7,5},{8,10},{9,11},{10,... | collective-permute-start | bytes 122888 | tf_op jit(solution)/shard_map/ppermute | solution.py:633
  32.7 0.9 %shard_map.122 = (f32[32,1024]{1,0:T(8,128)S(1)}, f32[32,128]{1,0:T(8,128)S(1)}) custom-call(f32[32,1024]{1,0:T(8,128)S(1)} %get-tuple-element.33.vec_ref.rhs_ref, f32[32,1024]{1,0:T(8,128)S(1)} %get-tuple-element.52.vec_ref.first_ref, bf16[2304,256]{1,0:T(8,128)(2,1)S(1)} %get-tuple-element.36.th_ref, bf16[2304,256]{1,0:T(8,128)(2,1)S(1)} %get-tuple-element.37.tl_ref), custom_call_target="tpu_custom_call" | custom-call | bytes 1000000 | tf_op jit(solution)/shard_map/pallas_call | solution.py:619
  33.6 1.7 %collective-permute-done.9.r2 = f32[40,256]{1,0:T(8,128)S(1)} collective-permute-done((f32[40,256]{1,0:T(8,128)S(1)}, f32[40,256]{1,0:T(8,128)S(1)}, u32[]{:S(2)}, u32[]{:S(2)}) %collective-permute-start.9) | collective-permute-done | bytes 40992 | tf_op jit(solution)/shard_map/ppermute | solution.py:633
  35.3 1.3 %collective-permute-done.10.r3 = f32[40,256]{1,0:T(8,128)S(1)} collective-permute-done((f32[40,256]{1,0:T(8,128)S(1)}, f32[40,256]{1,0:T(8,128)S(1)}, u32[]{:S(2)}, u32[]{:S(2)}) %collective-permute-start.10) | collective-permute-done | bytes 40992 | tf_op jit(solution)/shard_map/ppermute | solution.py:633
  36.6 1.6 %shard_map.124 = (f32[32,1024]{1,0:T(8,128)S(1)}, f32[32,1,640]{2,1,0:T(1,128)}) custom-call(f32[32,128]{1,0:T(8,128)S(1)} %get-tuple-element.53.columns_ref, f32[32,1024]{1,0:T(8,128)S(1)} %get-tuple-element.52.vec_ref.first_ref, f32[32,1024]{1,0:T(8,128)S(1)} %get-tuple-element.54.inner_ref, f32[40,256]{1,0:T(8,128)S(1)} %get-tuple-element.55.own, ...), custom_call_target="tpu_custom_call" | custom-call | bytes 1000000 | tf_op jit(solution)/shard_map/pallas_call | solution.py:619
  38.1 2.6 %all-to-all-start = ((f32[32,1,640]{2,1,0:T(1,128)}), f32[32,1,640]{2,1,0:T(1,128)S(1)}, u32[]{:S(2)}, u32[]{:S(2)}) async-start(f32[32,1,640]{2,1,0:T(1,128)} %get-tuple-element.59), calls=%async_computation | async-start | bytes 163840 | tf_op jit(solution)/shard_map/all_to_all | solution.py:755
  40.8 0.8 %shard_map.125 = (bf16[512,512]{1,0:T(8,128)(2,1)S(1)}, bf16[512,512]{1,0:T(8,128)(2,1)S(1)}) custom-call(f32[8,24,128]{2,1,0:T(8,128)S(1)} %constant_dynamic-update-slice_fusion.group_ref), custom_call_target="tpu_custom_call" | custom-call | bytes 1000000 | tf_op jit(solution)/shard_map/pallas_call | solution.py:619
  41.5 6.8 %all-to-all-done.group_ref = f32[32,1,640]{2,1,0:T(1,128)S(1)} async-done(((f32[32,1,640]{2,1,0:T(1,128)}), f32[32,1,640]{2,1,0:T(1,128)S(1)}, u32[]{:S(2)}, u32[]{:S(2)}) %all-to-all-start) | async-done | bytes 81952 | tf_op jit(solution)/shard_map/all_to_all | solution.py:755
  48.3 1.6 %shard_map.126 = (f32[32,1024]{1,0:T(8,128)}, f32[32,1024]{1,0:T(8,128)}) custom-call(f32[32,1024]{1,0:T(8,128)S(1)} %get-tuple-element.58.part_ref, f32[32,1,640]{2,1,0:T(1,128)S(1)} %all-to-all-done.group_ref, bf16[64,512]{1,0:T(8,128)(2,1)S(1)} %get-tuple-element.60.kgh_ref, bf16[64,512]{1,0:T(8,128)(2,1)S(1)} %get-tuple-element.61.kgl_ref, ...), custom_call_target="tpu_custom_call" | custom-call | bytes 1000000 | tf_op jit(solution)/shard_map/pallas_call | solution.py:619
  (14 shorter events, 0.0 us)
Async XLA Ops:
  2.4 7.6 %collective-permute-start = (f32[48,768]{1,0:T(8,128)S(1)}, f32[48,768]{1,0:T(8,128)S(1)}, u32[]{:S(2)}, u32[]{:S(2)}) collective-permute-start(f32[48,768]{1,0:T(8,128)S(1)} %get-tuple-element.39), channel_id=1, source_target_pairs={{0,1},{1,0},{2,3},{3,2},{4,5},{5,4},{6,7},{7,6},{8,9},{9,8},{10,11... | collective-permute-start | bytes 442376 | tf_op jit(solution)/shard_map/ppermute | solution.py:633
  2.9 7.0 %collective-permute-start.1 = (f32[48,256]{1,0:T(8,128)S(1)}, f32[48,256]{1,0:T(8,128)S(1)}, u32[]{:S(2)}, u32[]{:S(2)}) collective-permute-start(f32[48,256]{1,0:T(8,128)S(1)} %get-tuple-element.38.own), channel_id=1, source_target_pairs={{0,2},{1,3},{2,0},{3,1},{4,6},{5,7},{6,4},{7,5},{8,10},{9,11},{10,... | collective-permute-start | bytes 147464 | tf_op jit(solution)/shard_map/ppermute | solution.py:633
  5.5 4.4 %collective-permute-start.2 = (f32[48,256]{1,0:T(8,128)S(1)}, f32[48,256]{1,0:T(8,128)S(1)}, u32[]{:S(2)}, u32[]{:S(2)}) collective-permute-start(f32[48,256]{1,0:T(8,128)S(1)} %get-tuple-element.38.own), channel_id=1, source_target_pairs={{0,3},{1,2},{2,1},{3,0},{4,7},{5,6},{6,5},{7,4},{8,11},{9,10},{10,... | collective-permute-start | bytes 147464 | tf_op jit(solution)/shard_map/ppermute | solution.py:633
  5.5 12.5 %collective-permute-start.3 = (f32[40,512]{1,0:T(8,128)S(1)}, f32[40,512]{1,0:T(8,128)S(1)}, u32[]{:S(2)}, u32[]{:S(2)}) collective-permute-start(f32[40,512]{1,0:T(8,128)S(1)} %get-tuple-element.40), channel_id=1, source_target_pairs={{1,2},{3,4},{5,6},{7,8},{9,10},{11,12},{13,14},{15,16},{17,18},{19... | collective-permute-start | bytes 245768 | tf_op jit(solution)/shard_map/ppermute | solution.py:640
  10.0 11.5 %collective-permute-start.4 = (f32[1,24,128]{2,1,0:T(8,128)S(1)}, f32[1,24,128]{2,1,0:T(8,128)S(1)}, u32[]{:S(2)}, u32[]{:S(2)}) collective-permute-start(f32[1,24,128]{2,1,0:T(8,128)S(1)} %bitcast.4), channel_id=1, source_target_pairs={{0,8},{4,12},{8,0},{12,4},{16,24},{20,28},{24,16},{28,20},{1,9},{5... | collective-permute-start | bytes 36872 | tf_op jit(solution)/shard_map/ppermute | solution.py:633
  15.4 6.1 %collective-permute-start.5 = (f32[1,24,128]{2,1,0:T(8,128)S(1)}, f32[1,24,128]{2,1,0:T(8,128)S(1)}, u32[]{:S(2)}, u32[]{:S(2)}) collective-permute-start(f32[1,24,128]{2,1,0:T(8,128)S(1)} %bitcast.5), channel_id=1, source_target_pairs={{0,16},{4,20},{8,24},{12,28},{16,0},{20,4},{24,8},{28,12},{1,17},{... | collective-permute-start | bytes 36872 | tf_op jit(solution)/shard_map/ppermute | solution.py:633
  18.0 5.5 %collective-permute-start.6 = (f32[1,24,128]{2,1,0:T(8,128)S(1)}, f32[1,24,128]{2,1,0:T(8,128)S(1)}, u32[]{:S(2)}, u32[]{:S(2)}) collective-permute-start(f32[1,24,128]{2,1,0:T(8,128)S(1)} %bitcast.6), channel_id=1, source_target_pairs={{0,24},{4,28},{8,16},{12,20},{16,8},{20,12},{24,0},{28,4},{1,25},{... | collective-permute-start | bytes 36872 | tf_op jit(solution)/shard_map/ppermute | solution.py:633
  23.5 4.1 %collective-permute-start.7 = (f32[4,24,128]{2,1,0:T(8,128)S(1)}, f32[4,24,128]{2,1,0:T(8,128)S(1)}, u32[]{:S(2)}, u32[]{:S(2)}) collective-permute-start(f32[4,24,128]{2,1,0:T(8,128)S(1)} %pad_maximum_fusion), channel_id=1, source_target_pairs={{0,4},{4,0},{8,12},{12,8},{16,20},{20,16},{24,28},{28,24},{1,5},{5... | collective-permute-start | bytes 147464 | tf_op jit(solution)/shard_map/ppermute | solution.py:633
  28.6 8.0 %collective-permute-start.8 = (f32[40,768]{1,0:T(8,128)S(1)}, f32[40,768]{1,0:T(8,128)S(1)}, u32[]{:S(2)}, u32[]{:S(2)}) collective-permute-start(f32[40,768]{1,0:T(8,128)S(1)} %get-tuple-element.56), channel_id=1, source_target_pairs={{0,1},{1,0},{2,3},{3,2},{4,5},{5,4},{6,7},{7,6},{8,9},{9,8},{10,11... | collective-permute-start | bytes 368648 | tf_op jit(solution)/shard_map/ppermute | solution.py:633
  28.6 7.9 %collective-permute-start.11 = (f32[32,512]{1,0:T(8,128)S(1)}, f32[32,512]{1,0:T(8,128)S(1)}, u32[]{:S(2)}, u32[]{:S(2)}) collective-permute-start(f32[32,512]{1,0:T(8,128)S(1)} %get-tuple-element.57), channel_id=1, source_target_pairs={{1,2},{3,4},{5,6},{7,8},{9,10},{11,12},{13,14},{15,16},{17,18},{19... | collective-permute-start | bytes 196616 | tf_op jit(solution)/shard_map/ppermute | solution.py:640
  29.3 6.0 %collective-permute-start.9 = (f32[40,256]{1,0:T(8,128)S(1)}, f32[40,256]{1,0:T(8,128)S(1)}, u32[]{:S(2)}, u32[]{:S(2)}) collective-permute-start(f32[40,256]{1,0:T(8,128)S(1)} %get-tuple-element.55.own), channel_id=1, source_target_pairs={{0,2},{1,3},{2,0},{3,1},{4,6},{5,7},{6,4},{7,5},{8,10},{9,11},{10,... | collective-permute-start | bytes 122888 | tf_op jit(solution)/shard_map/ppermute | solution.py:633
  32.7 3.8 %collective-permute-start.10 = (f32[40,256]{1,0:T(8,128)S(1)}, f32[40,256]{1,0:T(8,128)S(1)}, u32[]{:S(2)}, u32[]{:S(2)}) collective-permute-start(f32[40,256]{1,0:T(8,128)S(1)} %get-tuple-element.55.own), channel_id=1, source_target_pairs={{0,3},{1,2},{2,1},{3,0},{4,7},{5,6},{6,5},{7,4},{8,11},{9,10},{10,... | collective-permute-start | bytes 122888 | tf_op jit(solution)/shard_map/ppermute | solution.py:633
  38.1 10.2 %all-to-all-start = ((f32[32,1,640]{2,1,0:T(1,128)}), f32[32,1,640]{2,1,0:T(1,128)S(1)}, u32[]{:S(2)}, u32[]{:S(2)}) async-start(f32[32,1,640]{2,1,0:T(1,128)} %get-tuple-element.59), calls=%async_computation | async-start | bytes 163840 | tf_op jit(solution)/shard_map/all_to_all | solution.py:755
